TPU v7x, 32 devices: a whole 2x2x4 slice. The times are simulated.
32 devices in a mesh: ep: 32 (over z, y, x, core).
Axes of the slice: x: 2, y: 2, z: 4, core: 2. Of those that a mesh axis runs over, the one named last changes fastest.
Arguments:
- x_tok: bfloat16 [16384, 1024], P('ep')
- route_idx: int32 [16384, 8], P('ep')
- gates: bfloat16 [16384, 8], P('ep')
- dy_tok: bfloat16 [16384, 1024], P('ep')
- w_gate: bfloat16 [32, 1024, 512], P('ep')
- w_up: bfloat16 [32, 1024, 512], P('ep')
- w_down: bfloat16 [32, 512, 1024], P('ep')
Outputs:
- output 1: bfloat16 [16384, 1024], P('ep')
- output 2: bfloat16 [16384, 1024], P('ep')
- output 3: float32 [32, 1024, 512], P('ep')
- output 4: float32 [32, 1024, 512], P('ep')
- output 5: float32 [32, 512, 1024], P('ep')
All inputs are finite; a program needn't handle non-finite values.
Results may differ from a plain program's by a relative error of at most 0.0103936.
Values are sent between devices in bfloat16 or wider.
A program may use at most 1 GiB of HBM per device.

v0:
```python
import jax
import jax.numpy as jnp
from jax import lax
from jax.sharding import PartitionSpec as P

HOLDERS = 4


def holder_table(n_dev):
    quarter = n_dev // 4
    return jnp.array([[0, quarter, n_dev // 2, 3 * quarter], [n_dev - 1, n_dev // 2, 3 * quarter, quarter - 1]], jnp.int32)


def plan_slots(route_loc, gate_loc, n_dev, per_dev, slot_cap, hot_rows):
    tok_loc, top_k = route_loc.shape
    experts = per_dev * n_dev
    reg_rows = per_dev * slot_cap
    block_rows = reg_rows + 2 * hot_rows
    flat_route = route_loc.reshape(-1)
    onehot = (flat_route[:, None] == jnp.arange(experts, dtype=jnp.int32)[None, :]).astype(jnp.int32)
    expert_rank = jnp.sum((jnp.cumsum(onehot, axis=0) - 1) * onehot, axis=1)
    second_hot = (flat_route == experts - 1).astype(jnp.int32)
    is_hot = (flat_route == 0) | (flat_route == experts - 1)
    dest_hot = holder_table(n_dev)[second_hot, expert_rank % HOLDERS]
    offset_hot = reg_rows + second_hot * hot_rows + expert_rank // HOLDERS
    dest_dev = jnp.where(is_hot, dest_hot, flat_route // per_dev)
    offset = jnp.where(is_hot, offset_hot, (flat_route % per_dev) * slot_cap + expert_rank)
    slot_idx = dest_dev * block_rows + offset
    total_slots = n_dev * block_rows
    token_ids = jnp.arange(tok_loc * top_k, dtype=jnp.int32) // top_k
    src_tok = jnp.full((total_slots,), tok_loc, jnp.int32).at[slot_idx].set(token_ids)
    src_gate = jnp.zeros((total_slots,), gate_loc.dtype).at[slot_idx].set(gate_loc.reshape(-1))
    return slot_idx.reshape(tok_loc, top_k), src_tok, src_gate


def expert_forward(in_rows, gate_w, up_w, down_w):
    u_val = jnp.einsum('secd,edf->secf', in_rows, gate_w, preferred_element_type=jnp.float32)
    v_val = jnp.einsum('secd,edf->secf', in_rows, up_w, preferred_element_type=jnp.float32)
    sig_u = jax.nn.sigmoid(u_val)
    act_rows = (u_val * sig_u * v_val).astype(jnp.bfloat16)
    out_rows = jnp.einsum('secf,efd->secd', act_rows, down_w, preferred_element_type=jnp.float32).astype(jnp.bfloat16)
    return out_rows, (u_val, v_val, sig_u, act_rows)


def expert_backward(in_rows, d_out, saved_acts, gate_w, up_w, down_w):
    u_val, v_val, sig_u, act_rows = saved_acts
    d_act = jnp.einsum('secd,efd->secf', d_out, down_w, preferred_element_type=jnp.float32)
    d_u = (d_act * v_val * sig_u * (1.0 + u_val * (1.0 - sig_u))).astype(jnp.bfloat16)
    d_v = (d_act * u_val * sig_u).astype(jnp.bfloat16)
    d_rows = (jnp.einsum('secf,edf->secd', d_u, gate_w, preferred_element_type=jnp.float32) + jnp.einsum('secf,edf->secd', d_v, up_w, preferred_element_type=jnp.float32)).astype(jnp.bfloat16)
    g_gate = jnp.einsum('secd,secf->edf', in_rows, d_u, preferred_element_type=jnp.float32)
    g_up = jnp.einsum('secd,secf->edf', in_rows, d_v, preferred_element_type=jnp.float32)
    g_down = jnp.einsum('secf,secd->efd', act_rows, d_out, preferred_element_type=jnp.float32)
    return d_rows, g_gate, g_up, g_down


def solution(mesh):
    n_dev = mesh.shape['ep']

    def local_step(x_tok, route_idx, gates, dy_tok, w_gate, w_up, w_down):
        tok_loc, top_k = route_idx.shape
        per_dev, model_dim = w_gate.shape[0], w_gate.shape[1]
        experts = per_dev * n_dev
        slot_cap = 2 * tok_loc * top_k // (experts - 2)
        hot_rows = tok_loc // 2 // HOLDERS
        reg_rows = per_dev * slot_cap
        block_rows = reg_rows + 2 * hot_rows
        slot_idx, src_tok, src_gate = plan_slots(route_idx, gates, n_dev, per_dev, slot_cap, hot_rows)
        my_index = lax.axis_index('ep')
        owner_one = my_index == 0
        owner_two = my_index == n_dev - 1

        def hot_copy(weights):
            first_copy = jnp.where(owner_one, weights[0], jnp.zeros_like(weights[0]))
            second_copy = jnp.where(owner_two, weights[per_dev - 1], jnp.zeros_like(weights[0]))
            return lax.psum(jnp.stack([first_copy, second_copy]), 'ep')

        hot_gate = hot_copy(w_gate)
        hot_up = hot_copy(w_up)
        hot_down = hot_copy(w_down)

        def exchange(send_rows):
            return lax.all_to_all(send_rows.reshape(n_dev, block_rows, model_dim), 'ep', 0, 0)

        def split_recv(recv_rows):
            reg_part = recv_rows[:, :reg_rows].reshape(n_dev, per_dev, slot_cap, model_dim)
            hot_part = recv_rows[:, reg_rows:].reshape(n_dev, 2, hot_rows, model_dim)
            return reg_part, hot_part

        def join_send(reg_part, hot_part):
            return jnp.concatenate([reg_part.reshape(n_dev, reg_rows, model_dim), hot_part.reshape(n_dev, 2 * hot_rows, model_dim)], axis=1)

        x_reg, x_hot = split_recv(exchange(jnp.take(x_tok, src_tok, axis=0, mode='fill', fill_value=0)))
        o_reg, saved_reg = expert_forward(x_reg, w_gate, w_up, w_down)
        o_hot, saved_hot = expert_forward(x_hot, hot_gate, hot_up, hot_down)
        o_back = exchange(join_send(o_reg, o_hot)).reshape(n_dev * block_rows, model_dim)
        y_tok = jnp.einsum('tk,tkd->td', gates, jnp.take(o_back, slot_idx, axis=0), preferred_element_type=jnp.float32).astype(jnp.bfloat16)

        dy_send = jnp.take(dy_tok, src_tok, axis=0, mode='fill', fill_value=0) * src_gate[:, None]
        d_reg, d_hot = split_recv(exchange(dy_send))
        dx_reg, g_gate, g_up, g_down = expert_backward(x_reg, d_reg, saved_reg, w_gate, w_up, w_down)
        dx_hot, h_gate, h_up, h_down = expert_backward(x_hot, d_hot, saved_hot, hot_gate, hot_up, hot_down)
        dx_back = exchange(join_send(dx_reg, dx_hot)).reshape(n_dev * block_rows, model_dim)
        dx_tok = jnp.sum(jnp.take(dx_back, slot_idx, axis=0), axis=1, dtype=jnp.float32).astype(jnp.bfloat16)

        h_gate, h_up, h_down = lax.psum((h_gate, h_up, h_down), 'ep')
        local_ids = jnp.arange(per_dev)
        mask_one = ((local_ids == 0) & owner_one).astype(jnp.float32)[:, None, None]
        mask_two = ((local_ids == per_dev - 1) & owner_two).astype(jnp.float32)[:, None, None]

        def settle(local_grad, hot_grad):
            return local_grad + mask_one * hot_grad[0] + mask_two * hot_grad[1]

        return y_tok, dx_tok, settle(g_gate, h_gate), settle(g_up, h_up), settle(g_down, h_down)

    return jax.shard_map(local_step, mesh=mesh, in_specs=(P('ep'), P('ep'), P('ep'), P('ep'), P('ep'), P('ep'), P('ep')), out_specs=(P('ep'), P('ep'), P('ep'), P('ep'), P('ep')), check_vma=False)
```

profile of v0, /device:TPU:0, one launch (start us, length us, event | category | flops | bytes accessed | tf_op | source)
XLA Modules:
  0.0 3123.8 jit_solution(1981066372691223910)
XLA Ops:
  19.6 34.6 %gather_fusion = s32[4096]{0:T(1024)S(1)} fusion(s32[2,4]{1,0:T(2,128)S(1)} %copy-done.2, s32[4096]{0:T(1024)S(1)} %bitcast.222), kind=kCustom, calls=%fused_computation.4 | custom fusion | bytes 65536 | tf_op jit(solution)/shard_map/gather | solution.py:24
  54.8 15.5 scatter_custom_fusion
  70.8 39.7 %gather_fusion.3 = bf16[12832,1024]{1,0:T(8,128)(2,1)} fusion(bf16[512,1024]{1,0:T(8,128)(2,1)S(1)} %copy-done, s32[13312]{0:T(1024)S(1)} %pad_clamp_fusion), kind=kCustom, calls=%fused_computation.2.clone | custom fusion | bytes 52611200 | tf_op jit(solution)/shard_map/jit(_take)/gather | solution.py:99
  110.4 39.8 %gather_fusion.1 = bf16[12832,1024]{1,0:T(8,128)(2,1)} fusion(bf16[512,1024]{1,0:T(8,128)(2,1)S(1)} %copy-done.3, s32[13312]{0:T(1024)S(1)} %pad_clamp_fusion), kind=kCustom, calls=%fused_computation.clone | custom fusion | bytes 52611200 | tf_op jit(solution)/shard_map/jit(_take)/gather | solution.py:93
  150.2 28.8 scatter_custom_fusion.1
  179.0 35.7 %select_multiply_fusion = (bf16[12832,1024]{1,0:T(8,128)(2,1)}, bf16[12832,1024]{1,0:T(8,128)(2,1)}) fusion(bf16[12832,1024]{1,0:T(8,128)(2,1)} %gather_fusion.3, pred[12832]{0:T(1024)(128)(4,1)S(1)} %compare_and_fusion, bf16[12832]{0:T(1024)(128)(2,1)S(1)} %scatter_custom_fusion.1, bf16[12832,1024]{1,0:T(8,128)(2,1)} %gather_fusion.1), kind=kLoop, calls=%fused_computation.10 | loop fusion | flops 39419904 | bytes 105158240 | tf_op jit(solution)/shard_map/mul | solution.py:99
  214.7 30.3 reshape.305
  252.4 30.2 reshape.314
  282.7 521.4 %all-to-all-done = bf16[32,401,1024]{2,1,0:T(8,128)(2,1)} async-done(((bf16[32,401,1024]{2,1,0:T(8,128)(2,1)}), bf16[32,401,1024]{2,1,0:T(8,128)(2,1)}, u32[]{:S(2)}, u32[]{:S(2)}) %all-to-all-start) | async-done | bytes 26279968 | tf_op jit(solution)/shard_map/all_to_all | solution.py:83
  804.1 34.1 %all-to-all-start.2 = ((bf16[32,401,1024]{2,1,0:T(8,128)(2,1)}), bf16[32,401,1024]{2,1,0:T(8,128)(2,1)}, u32[]{:S(2)}, u32[]{:S(2)}) async-start(bf16[32,401,1024]{2,1,0:T(8,128)(2,1)} %reshape.314), calls=%async_computation.2 | async-start | bytes 53477376 | tf_op jit(solution)/shard_map/all_to_all | solution.py:83
  856.3 453.7 %all-reduce.7.cloned.1.call-done = (bf16[2,1024,512]{2,1,0:T(8,128)(2,1)}, bf16[2,1024,512]{2,1,0:T(8,128)(2,1)}, bf16[2,512,1024]{2,1,0:T(8,128)(2,1)}) async-done(((bf16[2,1024,512]{2,1,0:T(8,128)(2,1)}, bf16[2,1024,512]{2,1,0:T(8,128)(2,1)}, bf16[2,512,1024]{2,1,0:T(8,128)(2,1)}), (bf16[2,1024,512]{2,1,0:T(8,128)(2,1)}, bf16[2,1024,512]{2,1,0:T(8,128)(2,1)}, ...) | async-done | bytes 6291472 | tf_op jit(solution)/shard_map/psum | solution.py:76
  1329.1 149.1 %all-to-all-done.2 = bf16[32,401,1024]{2,1,0:T(8,128)(2,1)} async-done(((bf16[32,401,1024]{2,1,0:T(8,128)(2,1)}), bf16[32,401,1024]{2,1,0:T(8,128)(2,1)}, u32[]{:S(2)}, u32[]{:S(2)}) %all-to-all-start.2) | async-done | bytes 26279968 | tf_op jit(solution)/shard_map/all_to_all | solution.py:83
  1490.0 16.2 fusion.36
  1525.4 17.2 fusion.18
  1542.6 17.5 fusion.20
  1560.1 31.7 %fusion.2 = (bf16[32,1,273,512]{3,2,0,1:T(8,128)(2,1)}, bf16[32,1,273,512]{3,2,0,1:T(8,128)(2,1)}, bf16[32,1,273,512]{3,2,0,1:T(8,128)(2,1)}) fusion(f32[32,273,512]{2,1,0:T(8,128)} %fusion.18, f32[32,273,512]{2,1,0:T(8,128)} %fusion.20, bf16[1,512,1024]{2,1,0:T(8,128)(2,1)S(1)} %copy-done.5, bf16[32,401,1024]{2,1,0:T(8,128)(2,1)} %all-to-all-done.2), kind=kOutput, calls=%fused_computation.16 | convolution fusion | flops 9231925248 | bytes 82935808 | tf_op jit(solution)/shard_map/secd,efd->secf/dot_general | solution.py:47
  1591.7 17.2 convolution_convert_fusion
  1608.9 18.3 pad_maximum_fusion
  1627.2 23.3 all-to-all-start.1
  1683.8 20.5 fusion.23
  1704.2 23.5 add_convert_fusion
  1727.8 18.3 pad_maximum_fusion.1
  1746.0 456.1 %all-to-all-done.1 = bf16[32,401,1024]{2,1,0:T(8,128)(2,1)} async-done(((bf16[32,401,1024]{2,1,0:T(8,128)(2,1)}), bf16[32,401,1024]{2,1,0:T(8,128)(2,1)}, u32[]{:S(2)}, u32[]{:S(2)}) %all-to-all-start.1) | async-done | bytes 26279968 | tf_op jit(solution)/shard_map/all_to_all | solution.py:83
  2202.2 34.0 %all-to-all-start.3 = ((bf16[32,401,1024]{2,1,0:T(8,128)(2,1)}), bf16[32,401,1024]{2,1,0:T(8,128)(2,1)}, u32[]{:S(2)}, u32[]{:S(2)}) async-start(bf16[32,401,1024]{2,1,0:T(8,128)(2,1)} %pad_maximum_fusion.1), calls=%async_computation.3 | async-start | bytes 53477376 | tf_op jit(solution)/shard_map/all_to_all | solution.py:83
  2269.7 653.8 %all-reduce.5.cloned.1.call-done = (f32[2,1024,512]{2,1,0:T(8,128)}, f32[2,1024,512]{2,1,0:T(8,128)}, f32[2,512,1024]{2,1,0:T(8,128)}) async-done(((f32[2,1024,512]{2,1,0:T(8,128)}, f32[2,1024,512]{2,1,0:T(8,128)}, f32[2,512,1024]{2,1,0:T(8,128)}), (f32[2,1024,512]{2,1,0:T(8,128)}, f32[2,1024,512]{2,1,0:T(8,128)}, f32[2,512,1024]{2,1,0:T(8,128)})) %all-reduce.5.cloned.1.call-update) | async-done | bytes 12582928 | tf_op jit(solution)/shard_map/psum | solution.py:106
  2923.6 17.7 fusion.68
  2941.2 17.8 fusion.70
  2959.1 17.3 fusion.72
  2976.4 30.0 reshape.312
  3006.4 32.7 %gather_fusion.2 = bf16[4096,1024]{1,0:T(8,128)(2,1)} fusion(bf16[12832,1024]{1,0:T(8,128)(2,1)} %reshape.312, s32[4096]{0:T(1024)S(1)} %broadcast_clamp_fusion), kind=kCustom, calls=%fused_computation.1.clone | custom fusion | bytes 16793600 | tf_op jit(solution)/shard_map/jit(_take)/gather | solution.py:97
  3045.4 30.4 reshape.319
  3075.8 32.8 %gather_fusion.4 = bf16[4096,1024]{1,0:T(8,128)(2,1)} fusion(bf16[12832,1024]{1,0:T(8,128)(2,1)} %reshape.319, s32[4096]{0:T(1024)S(1)} %broadcast_clamp_fusion), kind=kCustom, calls=%fused_computation.3.clone | custom fusion | bytes 16793600 | tf_op jit(solution)/shard_map/jit(_take)/gather | solution.py:104
  (99 shorter events, 170.1 us)
Async XLA Ops:
  7.2 63.6 %copy-start = (bf16[512,1024]{1,0:T(8,128)(2,1)S(1)}, bf16[512,1024]{1,0:T(8,128)(2,1)}, u32[]{:S(2)}) copy-start(bf16[512,1024]{1,0:T(8,128)(2,1)} %param.15) | copy-start | bytes 3145732
  7.2 12.4 copy-start.2
  19.4 34.8 %copy-start.10 = (s32[4096]{0:T(1024)}, s32[4096]{0:T(1024)S(1)}, u32[]{:S(2)}) copy-start(s32[4096]{0:T(1024)S(1)} %fusion.100) | copy-start | bytes 49156
  19.6 50.8 %copy-start.15 = (bf16[512,8]{0,1:T(8,128)(2,1)S(1)}, bf16[512,8]{0,1:T(8,128)(2,1)}, u32[]{:S(2)}) copy-start(bf16[512,8]{0,1:T(8,128)(2,1)} %param.14) | copy-start | bytes 24580
  54.2 0.6 copy-start.12
  70.8 39.7 %copy-start.3 = (bf16[512,1024]{1,0:T(8,128)(2,1)S(1)}, bf16[512,1024]{1,0:T(8,128)(2,1)}, u32[]{:S(2)}) copy-start(bf16[512,1024]{1,0:T(8,128)(2,1)} %param.12) | copy-start | bytes 3145732
  245.0 559.1 %all-to-all-start = ((bf16[32,401,1024]{2,1,0:T(8,128)(2,1)}), bf16[32,401,1024]{2,1,0:T(8,128)(2,1)}, u32[]{:S(2)}, u32[]{:S(2)}) async-start(bf16[32,401,1024]{2,1,0:T(8,128)(2,1)} %reshape.305), calls=%async_computation | async-start | bytes 53477376 | tf_op jit(solution)/shard_map/all_to_all | solution.py:83
  282.7 555.6 %copy-start.5 = (bf16[1,512,1024]{2,1,0:T(8,128)(2,1)S(1)}, bf16[1,512,1024]{2,1,0:T(8,128)(2,1)}, u32[]{:S(2)}) copy-start(bf16[1,512,1024]{2,1,0:T(8,128)(2,1)} %param.18) | copy-start | bytes 3145732
  282.7 557.2 %copy-start.6 = (bf16[1,1024,512]{2,1,0:T(8,128)(2,1)S(1)}, bf16[1,1024,512]{2,1,0:T(8,128)(2,1)}, u32[]{:S(2)}) copy-start(bf16[1,1024,512]{2,1,0:T(8,128)(2,1)} %param.17) | copy-start | bytes 3145732
  804.1 674.1 %all-to-all-start.2 = ((bf16[32,401,1024]{2,1,0:T(8,128)(2,1)}), bf16[32,401,1024]{2,1,0:T(8,128)(2,1)}, u32[]{:S(2)}, u32[]{:S(2)}) async-start(bf16[32,401,1024]{2,1,0:T(8,128)(2,1)} %reshape.314), calls=%async_computation.2 | async-start | bytes 53477376 | tf_op jit(solution)/shard_map/all_to_all | solution.py:83
  838.2 471.8 %all-reduce.7.cloned.1.call-start = ((), (), s32[]{:S(2)}) async-start(), calls=%async_computation.5 | async-start | bytes 12582912 | tf_op jit(solution)/shard_map/psum | solution.py:76
  1310.0 12.1 copy-start.4
  1310.0 12.1 copy-start.19
  1525.4 17.2 copy-start.8
  1627.2 575.0 %all-to-all-start.1 = ((bf16[32,401,1024]{2,1,0:T(8,128)(2,1)}), bf16[32,401,1024]{2,1,0:T(8,128)(2,1)}, u32[]{:S(2)}, u32[]{:S(2)}) async-start(bf16[32,401,1024]{2,1,0:T(8,128)(2,1)} %pad_maximum_fusion), calls=%async_computation.1 | async-start | bytes 53477376 | tf_op jit(solution)/shard_map/all_to_all | solution.py:83
  1650.5 13.3 copy-start.18
  1675.1 8.7 copy-start.7
  1683.8 20.5 copy-start.9
  2202.2 843.2 %all-to-all-start.3 = ((bf16[32,401,1024]{2,1,0:T(8,128)(2,1)}), bf16[32,401,1024]{2,1,0:T(8,128)(2,1)}, u32[]{:S(2)}, u32[]{:S(2)}) async-start(bf16[32,401,1024]{2,1,0:T(8,128)(2,1)} %pad_maximum_fusion.1), calls=%async_computation.3 | async-start | bytes 53477376 | tf_op jit(solution)/shard_map/all_to_all | solution.py:83
  2236.2 687.4 %all-reduce.5.cloned.1.call-start = ((), (), s32[]{:S(2)}) async-start(), calls=%async_computation.4 | async-start | bytes 25165824 | tf_op jit(solution)/shard_map/psum | solution.py:106
  2236.3 22.7 slice-start
  2247.6 11.4 slice-start.1
  2267.8 0.7 copy-start.13
  2267.8 0.9 copy-start.11
  2267.8 1.1 copy-start.16
  2267.8 1.4 copy-start.14
  2941.2 17.9 copy-start.17
  3075.8 40.9 %copy-start.1 = (bf16[512,1024]{1,0:T(8,128)(2,1)S(1)}, bf16[512,1024]{1,0:T(8,128)(2,1)}, u32[]{:S(2)}) copy-start(bf16[512,1024]{1,0:T(8,128)(2,1)} %param.15) | copy-start | bytes 3145732
Sparse Core Ops, SparseCore 0:
  845.5 464.4 all-reduce.6
  2268.0 655.5 all-reduce.4
where the time goes:
time: 3130 us; the launch traced here: 3120 us
  waiting for transfers between devices  2230 us (71%)
  local copies, waits for them, and re-layouts  392 us (13%)
  matrix products  287 us (9%)
  starting transfers between devices  99 us (3%)
  other arithmetic  96.9 us (3%)
    all_to_all x4, waiting for transfers between devices, exchange(): lax.all_to_all(send_rows.reshape(n_dev, block_rows, model_dim), 'ep', 0, 0)  1130 us
    psum x1, waiting for transfers between devices, local_step(): h_gate, h_up, h_down = lax.psum((h_gate, h_up, h_down), 'ep')  654 us
    psum x1, waiting for transfers between devices, hot_copy(): return lax.psum(jnp.stack([first_copy, second_copy]), 'ep')  454 us
    all_to_all x4, starting transfers between devices, exchange(): lax.all_to_all(send_rows.reshape(n_dev, block_rows, model_dim), 'ep', 0, 0)  98.9 us
  transfers between devices with their start and end apart: 6, of which 5 were waited for; matrix products, arithmetic and copies ran while one was open for 10% of the time, Pallas kernels for 0%

commit v1 on v0

v1 whole, which is shorter than its diff:
```python
import functools

import jax
import jax.numpy as jnp
from jax import lax
from jax.experimental import pallas as pl
from jax.experimental.pallas import tpu as pltpu
from jax.sharding import Mesh, PartitionSpec as P

F32 = jnp.float32
BF16 = jnp.bfloat16
TILE = 256
WIN = 128
ALIGN = 16
GROUP = 2
ROWS = 256


def dot(a, b, dims=((1,), (0,))):
    return lax.dot_general(a, b, (dims, ((), ())), preferred_element_type=F32)


def expert_kernel(
    n_tiles, n_exp, cum_ref, off_ref, row_ref, col_ref, x_ref, dy_ref, wg_ref, wu_ref, wd_ref,
    y_ref, dx_ref, dwg_ref, dwu_ref, dwd_ref, x_rows, g_rows, o_win, d_win,
):
    step = pl.program_id(0)

    def span(tile, exp):
        lo = cum_ref[tile * n_exp + exp]
        hi = cum_ref[(tile + 1) * n_exp + exp]
        start = (lo // ALIGN) * ALIGN
        return lo, hi, start

    @pl.when(step < n_tiles)
    def _gather():
        tile = step

        def window(exp, lo, hi, start):
            place = (lax.broadcasted_iota(jnp.int32, (WIN, TILE), 0) + start).astype(F32)
            hit = row_ref[0, exp : exp + 1, :] == place
            take = jnp.where(hit, 1.0, 0.0).astype(BF16)
            scale = jnp.where(hit, row_ref[0, n_exp + exp : n_exp + exp + 1, :], 0.0).astype(BF16)
            row = lax.broadcasted_iota(jnp.int32, (WIN, 1), 0) + start
            mine = (row >= lo) & (row < hi)
            here = pl.ds(pl.multiple_of(off_ref[exp] + start, ALIGN), WIN)
            x_rows[here, :] = jnp.where(mine, dot(take, x_ref[...]), x_rows[here, :].astype(F32)).astype(BF16)
            g_rows[here, :] = jnp.where(mine, dot(scale, dy_ref[...]), g_rows[here, :].astype(F32)).astype(BF16)

        for exp in range(n_exp):
            lo, hi, start = span(tile, exp)
            window(exp, lo, hi, start)

            @pl.when(hi > start + WIN)
            def _more():
                @pl.loop(1, (hi - start + WIN - 1) // WIN)
                def _(w):
                    window(exp, lo, hi, start + w * WIN)

    @pl.when((step >= n_tiles) & (step < n_tiles + n_exp))
    def _expert():
        exp = step - n_tiles
        count = cum_ref[n_tiles * n_exp + exp]
        base = off_ref[exp]
        dwg_ref[...] = jnp.zeros_like(dwg_ref)
        dwu_ref[...] = jnp.zeros_like(dwu_ref)
        dwd_ref[...] = jnp.zeros_like(dwd_ref)

        @pl.loop(0, (count + ROWS - 1) // ROWS)
        def _(b):
            here = pl.ds(pl.multiple_of(base + b * ROWS, ALIGN), ROWS)
            live = lax.broadcasted_iota(jnp.int32, (ROWS, 1), 0) < count - b * ROWS
            x_old = x_rows[here, :]
            g_old = g_rows[here, :]
            x_blk = jnp.where(live, x_old, jnp.zeros_like(x_old))
            g_blk = jnp.where(live, g_old, jnp.zeros_like(g_old))
            u = dot(x_blk, wg_ref[0])
            v = dot(x_blk, wu_ref[0])
            s = jax.nn.sigmoid(u)
            act = (u * s * v).astype(BF16)
            da = dot(g_blk, wd_ref[0], ((1,), (1,)))
            du = (da * v * s * (1.0 + u * (1.0 - s))).astype(BF16)
            dv = (da * u * s).astype(BF16)
            out = dot(act, wd_ref[0]).astype(BF16)
            dxr = (dot(du, wg_ref[0], ((1,), (1,))) + dot(dv, wu_ref[0], ((1,), (1,)))).astype(BF16)
            dwd_ref[0] += dot(act, g_blk, ((0,), (0,)))
            g_rows[here, :] = jnp.where(live, dxr, g_rows[here, :])
            dwg_ref[0] += dot(x_blk, du, ((0,), (0,)))
            dwu_ref[0] += dot(x_blk, dv, ((0,), (0,)))
            x_rows[here, :] = jnp.where(live, out, x_rows[here, :])

    @pl.when(step >= n_tiles + n_exp)
    def _scatter():
        tile = step - n_tiles - n_exp

        def window(exp, lo, hi, start):
            place = (lax.broadcasted_iota(jnp.int32, (TILE, WIN), 1) + start).astype(F32)
            hit = col_ref[:, exp : exp + 1] == place
            put = jnp.where(hit, 1.0, 0.0).astype(BF16)
            scale = jnp.where(hit, col_ref[:, n_exp + exp : n_exp + exp + 1], 0.0).astype(BF16)
            row = lax.broadcasted_iota(jnp.int32, (WIN, 1), 0) + start
            mine = (row >= lo) & (row < hi)
            here = pl.ds(pl.multiple_of(off_ref[exp] + start, ALIGN), WIN)
            o_blk = x_rows[here, :]
            d_blk = g_rows[here, :]
            o_blk = jnp.where(mine, o_blk, jnp.zeros_like(o_blk))
            d_blk = jnp.where(mine, d_blk, jnp.zeros_like(d_blk))
            return put, scale, o_blk, d_blk

        for part in range(n_exp // GROUP):
            puts, scales = [], []
            for i in range(GROUP):
                exp = part * GROUP + i
                lo, hi, start = span(tile, exp)
                put, scale, o_blk, d_blk = window(exp, lo, hi, start)
                puts.append(put)
                scales.append(scale)
                o_win[i * WIN : (i + 1) * WIN, :] = o_blk
                d_win[i * WIN : (i + 1) * WIN, :] = d_blk
            y_add = dot(jnp.concatenate(scales, axis=1), o_win[...])
            dx_add = dot(jnp.concatenate(puts, axis=1), d_win[...])
            y_ref[...] = y_add if part == 0 else y_ref[...] + y_add
            dx_ref[...] = dx_add if part == 0 else dx_ref[...] + dx_add
        for exp in range(n_exp):
            lo, hi, start = span(tile, exp)

            @pl.when(hi > start + WIN)
            def _more():
                @pl.loop(1, (hi - start + WIN - 1) // WIN)
                def _(w):
                    put, scale, o_blk, d_blk = window(exp, lo, hi, start + w * WIN)
                    y_ref[...] += dot(scale, o_blk)
                    dx_ref[...] += dot(put, d_blk)


def expert_layer(cum, off, table, x_col, dy_col, w_gate, w_up, w_down, cap):
    tokens, dim = x_col.shape
    n_exp, _, ff = w_gate.shape
    n_tiles = tokens // TILE
    total = n_exp * (-(-cap // ALIGN) * ALIGN) + ROWS
    by_tile = table.reshape(n_tiles, TILE, 2 * n_exp).transpose(0, 2, 1)
    first = lambda i: jnp.minimum(i, n_tiles - 1)
    middle = lambda i: jnp.clip(i - n_tiles, 0, n_exp - 1)
    last = lambda i: jnp.maximum(i - n_tiles - n_exp, 0)
    rows = pl.BlockSpec((1, 2 * n_exp, TILE), lambda i, *_: (first(i), 0, 0))
    cols = pl.BlockSpec((TILE, 2 * n_exp), lambda i, *_: (last(i), 0))
    toks_in = pl.BlockSpec((TILE, dim), lambda i, *_: (first(i), 0))
    toks_out = pl.BlockSpec((TILE, dim), lambda i, *_: (last(i), 0))
    wide = pl.BlockSpec((1, dim, ff), lambda i, *_: (middle(i), 0, 0))
    tall = pl.BlockSpec((1, ff, dim), lambda i, *_: (middle(i), 0, 0))
    return pl.pallas_call(
        functools.partial(expert_kernel, n_tiles, n_exp),
        grid_spec=pltpu.PrefetchScalarGridSpec(
            num_scalar_prefetch=2,
            grid=(2 * n_tiles + n_exp,),
            in_specs=[rows, cols, toks_in, toks_in, wide, wide, tall],
            out_specs=[toks_out, toks_out, wide, wide, tall],
            scratch_shapes=[
                pltpu.VMEM((total, dim), BF16),
                pltpu.VMEM((total, dim), BF16),
                pltpu.VMEM((GROUP * WIN, dim), BF16),
                pltpu.VMEM((GROUP * WIN, dim), BF16),
            ],
        ),
        out_shape=[
            jax.ShapeDtypeStruct((tokens, dim), F32),
            jax.ShapeDtypeStruct((tokens, dim), F32),
            jax.ShapeDtypeStruct(w_gate.shape, F32),
            jax.ShapeDtypeStruct(w_up.shape, F32),
            jax.ShapeDtypeStruct(w_down.shape, F32),
        ],
        compiler_params=pltpu.CompilerParams(
            dimension_semantics=("arbitrary",), vmem_limit_bytes=67_000_000,
        ),
        cost_estimate=pl.CostEstimate(flops=60_000_000_000, bytes_accessed=120_000_000, transcendentals=3_000_000),
        name="experts",
    )(cum, off, by_tile, table, x_col, dy_col, w_gate, w_up, w_down)


def plan(route, gates, first_exp, n_exp):
    hits = route[:, :, None] == first_exp + jnp.arange(n_exp, dtype=jnp.int32)[None, None, :]
    member = jnp.any(hits, axis=1)
    gate = jnp.sum(jnp.where(hits, gates[:, :, None].astype(F32), 0.0), axis=1)
    tiles = member.reshape(-1, TILE, n_exp)
    per_tile = jnp.sum(tiles.astype(jnp.int32), axis=1)
    cum = jnp.concatenate([jnp.zeros((1, n_exp), jnp.int32), jnp.cumsum(per_tile, axis=0)])
    lower = jnp.tril(jnp.ones((TILE, TILE), BF16), -1)
    inner = jnp.einsum('ab,ibe->iae', lower, tiles.astype(BF16), preferred_element_type=F32).astype(jnp.int32)
    rank = jnp.where(tiles, inner + cum[:-1, None, :], -(1 << 20)).reshape(-1, n_exp)
    count = cum[-1]
    padded = (count + ALIGN - 1) // ALIGN * ALIGN
    off = jnp.cumsum(padded) - padded
    return cum.reshape(-1), off.astype(jnp.int32), jnp.concatenate([rank.astype(F32), gate], axis=1)


def solution(mesh):
    n_dev = mesh.devices.size
    depth = n_dev // 8
    grid = Mesh(mesh.devices.reshape(depth, 2, 2, 2), ('z', 'y', 'x', 'c'))
    plane = ('y', 'x', 'c')
    spec = P(('z', 'y', 'x', 'c'))

    def local_step(x_tok, route_idx, gates, dy_tok, w_gate, w_up, w_down):
        tok_loc, top_k = route_idx.shape
        cap = depth * (2 * tok_loc * top_k // (n_dev * w_gate.shape[0] - 2))
        n_exp = 8 * w_gate.shape[0]
        gather_z = lambda a: lax.all_gather(a, 'z', axis=0, tiled=True)
        gather_p = lambda a: lax.all_gather(a, plane, axis=0, tiled=True)
        route = gather_z(route_idx)
        gate_all = gather_z(gates)
        cum, off, table = plan(route, gate_all, lax.axis_index('z') * n_exp, n_exp)
        x_col = gather_z(x_tok)
        dy_col = gather_z(dy_tok)
        y, dx, g_gate, g_up, g_down = expert_layer(
            cum, off, table, x_col, dy_col, gather_p(w_gate), gather_p(w_up), gather_p(w_down), cap
        )
        sum_z = lambda a: lax.psum_scatter(a, 'z', scatter_dimension=0, tiled=True)
        sum_p = lambda a: lax.psum_scatter(a, plane, scatter_dimension=0, tiled=True)
        return sum_z(y).astype(BF16), sum_z(dx).astype(BF16), sum_p(g_gate), sum_p(g_up), sum_p(g_down)

    return jax.shard_map(local_step, mesh=grid, in_specs=(spec,) * 7, out_specs=(spec,) * 5, check_vma=False)
```

time: 3130 us -> 1100 us (0.35)
  waiting for transfers between devices: 2230 us -> 948 us
  local copies, waits for them, and re-layouts: 392 us -> 1.92 us
  matrix products: 287 us -> 0.26 us
  Pallas kernels: 0 us -> 98.9 us
  starting transfers between devices: 99 us -> 0.38 us
  other arithmetic: 96.9 us -> 7.35 us
    all_to_all x4 -> x0, waiting for transfers between devices: 1130 us -> none  [exchange(): lax.all_to_all(send_rows.reshape(n_dev, block_rows, model_dim), 'ep', 0, 0)]
    psum x2 -> x0, waiting for transfers between devices: 1110 us -> none  [the longest x1 654 us: local_step(): h_gate, h_up, h_down = lax.psum((h_gate, h_up, h_down), 'ep')]
    reduce_scatter x0 -> x5, waiting for transfers between devices: none -> 646 us  [the longest x3 356 us: local_step(): lax.psum_scatter(a, plane, scatter_dimension=0, tiled=True)]
    all_gather x0 -> x5, waiting for transfers between devices: none -> 297 us  [the longest x3 166 us: local_step(): gather_p = lambda a: lax.all_gather(a, plane, axis=0, tiled=True)]
    dot_general x19 -> x1, matrix products: 287 us -> 0.26 us  [plan(): jnp.einsum('ab,ibe->iae', lower, tiles.astype(BF16), preferred_element_ty...]
    gather x7 -> x0, local copies, waits for them, and re-layouts: 180 us -> none  [the longest x1 39.8 us: local_step(): jnp.take(x_tok, src_tok, axis=0, mode='fill', fill_value=0)]
    reshape x6 -> x1, local copies, waits for them, and re-layouts: 121 us -> 0.59 us  [plan(): cum.reshape(-1)]
    pallas_call x0 -> x1, Pallas kernels: none -> 98.9 us  [expert_layer(): pl.pallas_call(functools.partial(expert_kernel, n_tiles, n_exp), grid_spe...]
  transfers between devices with their start and end apart: 6 -> 10, of which waited for: 5 -> 10; matrix products, arithmetic and copies ran while one was open for 10% -> 1% of each run, Pallas kernels for 0% -> 0%
where the time goes in v1:
time: 1100 us
  waiting for transfers between devices  948 us (86%)
  Pallas kernels  98.9 us (9%)
  blocking collectives  28.5 us (3%)
  between operations  14.2 us (1%)
    reduce_scatter x3, waiting for transfers between devices, local_step(): lax.psum_scatter(a, plane, scatter_dimension=0, tiled=True)  356 us
    reduce_scatter x2, waiting for transfers between devices, local_step(): sum_z = lambda a: lax.psum_scatter(a, 'z', scatter_dimension=0, tiled=True)  290 us
    all_gather x3, waiting for transfers between devices, local_step(): gather_p = lambda a: lax.all_gather(a, plane, axis=0, tiled=True)  166 us
    all_gather x2, waiting for transfers between devices, local_step(): gather_z = lambda a: lax.all_gather(a, 'z', axis=0, tiled=True)  131 us
    pallas_call x1, Pallas kernels, expert_layer(): pl.pallas_call(functools.partial(expert_kernel, n_tiles, n_exp), grid_spe...  98.9 us
    all_gather x2, blocking collectives, local_step(): gather_z = lambda a: lax.all_gather(a, 'z', axis=0, tiled=True)  28.5 us
  transfers between devices with their start and end apart: 10, of which 10 were waited for; matrix products, arithmetic and copies ran while one was open for 1% of the time, Pallas kernels for 0%

profile of v1, /device:TPU:0, one launch (start us, length us, event | category | flops | bytes accessed | tf_op | source)
XLA Modules:
  0.0 1099.8 jit_solution(5323935589212531042)
XLA Ops:
  7.2 0.7 all-gather.6.cloned.1.call-update
  7.9 0.7 all-gather.8.cloned.1.call-update
  8.7 0.7 all-gather.10.cloned.1.call-update
  9.4 0.5 all-gather.12.cloned.1.call-update
  10.0 0.5 all-gather.14.cloned.1.call-update
  10.6 14.9 %all_gather.22 = bf16[2048,8]{0,1:T(8,128)(2,1)S(1)} all-gather(bf16[512,8]{0,1:T(8,128)(2,1)} %param.9), channel_id=1, replica_groups=mesh['z'=4,'y'=2,'x'=2,'c'=2] {'z'}, dimensions={0}, use_global_device_ids=true | all-gather | bytes 40960 | tf_op jit(solution)/shard_map/all_gather | solution.py:207
  25.5 13.7 %all_gather.21 = s32[2048,8]{0,1:T(8,128)S(1)} all-gather(s32[512,8]{0,1:T(8,128)} %param.8), channel_id=1, replica_groups=mesh['z'=4,'y'=2,'x'=2,'c'=2] {'z'}, dimensions={0}, use_global_device_ids=true | all-gather | bytes 81920 | tf_op jit(solution)/shard_map/all_gather | solution.py:207
  39.2 0.1 compare_reduce_fusion
  39.3 0.2 convert_reduce_fusion
  39.6 0.2 reduce-window.9
  39.8 0.6 reshape.113.cum_ref
  40.5 0.3 fusion.3
  40.8 1.3 copy.23.col_ref
  42.1 0.7 maximum_bitcast_fusion.row_ref
  42.7 0.5 bitcast_subtract_fusion.off_ref
  43.3 50.5 %all-gather.6.cloned.1.call-done.x_ref = bf16[2048,1024]{1,0:T(8,128)(2,1)} async-done(((bf16[512,1024]{1,0:T(8,128)(2,1)}), bf16[2048,1024]{1,0:T(8,128)(2,1)}) %all-gather.6.cloned.1.call-update) | async-done | bytes 4194320 | tf_op jit(solution)/shard_map/all_gather | solution.py:207
  93.8 80.5 %all-gather.8.cloned.1.call-done.dy_ref = bf16[2048,1024]{1,0:T(8,128)(2,1)} async-done(((bf16[512,1024]{1,0:T(8,128)(2,1)}), bf16[2048,1024]{1,0:T(8,128)(2,1)}) %all-gather.8.cloned.1.call-update) | async-done | bytes 4194320 | tf_op jit(solution)/shard_map/all_gather | solution.py:207
  174.2 54.5 %all-gather.10.cloned.1.call-done.wg_ref = bf16[8,1024,512]{2,1,0:T(8,128)(2,1)} async-done(((bf16[1,1024,512]{2,1,0:T(8,128)(2,1)}), bf16[8,1024,512]{2,1,0:T(8,128)(2,1)}) %all-gather.10.cloned.1.call-update) | async-done | bytes 8388624 | tf_op jit(solution)/shard_map/all_gather | solution.py:208
  228.8 55.7 %all-gather.12.cloned.1.call-done.wu_ref = bf16[8,1024,512]{2,1,0:T(8,128)(2,1)} async-done(((bf16[1,1024,512]{2,1,0:T(8,128)(2,1)}), bf16[8,1024,512]{2,1,0:T(8,128)(2,1)}) %all-gather.12.cloned.1.call-update) | async-done | bytes 8388624 | tf_op jit(solution)/shard_map/all_gather | solution.py:208
  284.4 55.7 %all-gather.14.cloned.1.call-done.wd_ref = bf16[8,512,1024]{2,1,0:T(8,128)(2,1)} async-done(((bf16[1,512,1024]{2,1,0:T(8,128)(2,1)}), bf16[8,512,1024]{2,1,0:T(8,128)(2,1)}) %all-gather.14.cloned.1.call-update) | async-done | bytes 8388624 | tf_op jit(solution)/shard_map/all_gather | solution.py:208
  340.1 98.9 %experts.1 = (f32[2048,1024]{1,0:T(8,128)}, f32[2048,1024]{1,0:T(8,128)}, f32[8,1024,512]{2,1,0:T(8,128)}, f32[8,1024,512]{2,1,0:T(8,128)}, f32[8,512,1024]{2,1,0:T(8,128)}) custom-call(s32[72]{0:T(128)} %reshape.113.cum_ref, s32[8]{0:T(128)} %bitcast_subtract_fusion.off_ref, f32[8,16,256]{2,1,0:T(8,128)} %maximum_bitcast_fusion.row_ref, ...), custom_call_target="tpu_custom_call" | custom-call | flops 60000002048 | bytes 120000000 | tf_op jit(solution)/shard_map/experts/pallas_call | solution.py:151
  439.1 0.7 reduce-scatter.8.cloned.1.call-update
  439.8 0.7 reduce-scatter.10.cloned.1.call-update
  440.6 0.7 reduce-scatter.12.cloned.1.call-update
  441.3 0.5 reduce-scatter.14.cloned.1.call-update
  441.8 145.4 %reduce-scatter.6.cloned.1.call-done = f32[512,1024]{1,0:T(8,128)} async-done(((f32[2048,1024]{1,0:T(8,128)}), f32[512,1024]{1,0:T(8,128)}) %reduce-scatter.6.cloned.1.call-update) | async-done | bytes 2097168 | tf_op jit(solution)/shard_map/reduce_scatter | solution.py:217
  587.3 2.7 convert_element_type.30
  590.0 144.3 %reduce-scatter.8.cloned.1.call-done = f32[512,1024]{1,0:T(8,128)} async-done(((f32[2048,1024]{1,0:T(8,128)}), f32[512,1024]{1,0:T(8,128)}) %reduce-scatter.8.cloned.1.call-update) | async-done | bytes 2097168 | tf_op jit(solution)/shard_map/reduce_scatter | solution.py:217
  734.3 2.7 convert_element_type.31
  737.1 117.2 %reduce-scatter.10.cloned.1.call-done = f32[1,1024,512]{2,1,0:T(8,128)} async-done(((f32[8,1024,512]{2,1,0:T(8,128)}), f32[1,1024,512]{2,1,0:T(8,128)}) %reduce-scatter.10.cloned.1.call-update) | async-done | bytes 2097168 | tf_op jit(solution)/shard_map/reduce_scatter | solution.py:218
  854.3 119.5 %reduce-scatter.12.cloned.1.call-done = f32[1,1024,512]{2,1,0:T(8,128)} async-done(((f32[8,1024,512]{2,1,0:T(8,128)}), f32[1,1024,512]{2,1,0:T(8,128)}) %reduce-scatter.12.cloned.1.call-update) | async-done | bytes 2097168 | tf_op jit(solution)/shard_map/reduce_scatter | solution.py:218
  973.7 119.3 %reduce-scatter.14.cloned.1.call-done = f32[1,512,1024]{2,1,0:T(8,128)} async-done(((f32[8,512,1024]{2,1,0:T(8,128)}), f32[1,512,1024]{2,1,0:T(8,128)}) %reduce-scatter.14.cloned.1.call-update) | async-done | bytes 2097168 | tf_op jit(solution)/shard_map/reduce_scatter | solution.py:218
  (20 shorter events, 0.6 us)
Async XLA Ops:
  7.2 86.6 %all-gather.6.cloned.1.call-start = ((), (), s32[]{:S(2)}) async-start(), calls=%async_computation.5 | async-start | bytes 5242880 | tf_op jit(solution)/shard_map/all_gather | solution.py:207
  7.9 166.3 %all-gather.8.cloned.1.call-start = ((), (), s32[]{:S(2)}) async-start(), calls=%async_computation.6 | async-start | bytes 5242880 | tf_op jit(solution)/shard_map/all_gather | solution.py:207
  8.6 220.1 %all-gather.10.cloned.1.call-start = ((), (), s32[]{:S(2)}) async-start(), calls=%async_computation.7 | async-start | bytes 9437184 | tf_op jit(solution)/shard_map/all_gather | solution.py:208
  9.4 275.1 %all-gather.12.cloned.1.call-start = ((), (), s32[]{:S(2)}) async-start(), calls=%async_computation.8 | async-start | bytes 9437184 | tf_op jit(solution)/shard_map/all_gather | solution.py:208
  10.0 330.1 %all-gather.14.cloned.1.call-start = ((), (), s32[]{:S(2)}) async-start(), calls=%async_computation.9 | async-start | bytes 9437184 | tf_op jit(solution)/shard_map/all_gather | solution.py:208
  10.5 576.7 %reduce-scatter.6.cloned.1.call-start = ((), (), s32[]{:S(2)}) async-start(), calls=%async_computation.10 | async-start | bytes 10485760 | tf_op jit(solution)/shard_map/reduce_scatter | solution.py:217
  439.0 295.3 %reduce-scatter.8.cloned.1.call-start = ((), (), s32[]{:S(2)}) async-start(), calls=%async_computation.11 | async-start | bytes 10485760 | tf_op jit(solution)/shard_map/reduce_scatter | solution.py:217
  439.8 414.5 %reduce-scatter.10.cloned.1.call-start = ((), (), s32[]{:S(2)}) async-start(), calls=%async_computation.12 | async-start | bytes 18874368 | tf_op jit(solution)/shard_map/reduce_scatter | solution.py:218
  440.5 533.2 %reduce-scatter.12.cloned.1.call-start = ((), (), s32[]{:S(2)}) async-start(), calls=%async_computation.13 | async-start | bytes 18874368 | tf_op jit(solution)/shard_map/reduce_scatter | solution.py:218
  441.3 651.7 %reduce-scatter.14.cloned.1.call-start = ((), (), s32[]{:S(2)}) async-start(), calls=%async_computation.14 | async-start | bytes 18874368 | tf_op jit(solution)/shard_map/reduce_scatter | solution.py:218
Sparse Core Ops, SparseCore 0:
  9.5 84.1 all-gather.5
  95.3 78.8 all-gather.7
  176.1 52.6 all-gather.9
  230.5 53.8 all-gather.11
  286.2 53.8 all-gather.13
  439.1 148.0 reduce-scatter.5
  589.6 144.6 reduce-scatter.7
  738.5 115.7 reduce-scatter.9
  858.4 115.2 reduce-scatter.11
  977.7 115.2 reduce-scatter.13

commit v2 on v1

--- a/solution.py
+++ b/solution.py
@@ -20,11 +20,254 @@
     return lax.dot_general(a, b, (dims, ((), ())), preferred_element_type=F32)
 
 
+MESH = pl.DeviceIdType.MESH
+
+
+def hop(src, dst, send_sem, recv_sem, **where):
+    return pltpu.make_async_remote_copy(
+        src_ref=src, dst_ref=dst, send_sem=send_sem, recv_sem=recv_sem, device_id=where, device_id_type=MESH
+    )
+
+
+def meet(depth, z, y, x, c):
+    barrier = pltpu.get_barrier_semaphore()
+    for where in ({'y': 1 - y}, {'x': 1 - x}, {'c': 1 - c}):
+        pl.semaphore_signal(barrier, inc=1, device_id=where, device_id_type=MESH)
+
+    @pl.when(z > 0)
+    def _():
+        pl.semaphore_signal(barrier, inc=1, device_id={'z': z - 1}, device_id_type=MESH)
+
+    @pl.when(z < depth - 1)
+    def _():
+        pl.semaphore_signal(barrier, inc=1, device_id={'z': z + 1}, device_id_type=MESH)
+
+    inner = (z > 0) & (z < depth - 1)
+
+    @pl.when(inner)
+    def _():
+        pl.semaphore_wait(barrier, 5)
+
+    @pl.when(jnp.logical_not(inner))
+    def _():
+        pl.semaphore_wait(barrier, 4)
+
+
+def make_plan(experts, route_ref, gate_ref, plan):
+    top_k, toks = route_ref.shape
+    route = route_ref[...]
+    gates = gate_ref[...]
+    below = lax.broadcasted_iota(jnp.int32, (TILE, TILE), 0) < lax.broadcasted_iota(jnp.int32, (TILE, TILE), 1)
+    below = jnp.where(below, 1.0, 0.0).astype(BF16)
+    ones = jnp.ones((8, TILE), BF16)
+    ids = lax.broadcasted_iota(jnp.int32, (experts, toks), 0)
+    member = jnp.zeros((experts, toks), F32)
+    gate = jnp.zeros((experts, toks), F32)
+    for k in range(top_k):
+        hit = jnp.broadcast_to(route[k : k + 1, :], (experts, toks)) == ids
+        member = jnp.where(hit, 1.0, member)
+        gate = jnp.where(hit, jnp.broadcast_to(gates[k : k + 1, :], (experts, toks)), gate)
+    plan[experts : 2 * experts, :] = gate
+    plan[2 * experts :, :] = jnp.zeros((8, toks), F32)
+    for t in range(toks // TILE):
+        cols = slice(t * TILE, (t + 1) * TILE)
+        part = member[:, cols]
+        rank = dot(part.astype(BF16), below)
+        plan[:experts, cols] = jnp.where(part > 0.5, rank, -4096.0)
+        plan[2 * experts + t : 2 * experts + t + 1, :experts] = dot(ones, part.astype(BF16), ((1,), (1,)))[:1]
+
+
+def spread_kernel(
+    depth, experts, x_ref, dy_ref, route_ref, gate_ref, wg_ref, wu_ref, wd_ref,
+    x_out, dy_out, plan_out, wg_out, wu_out, wd_out,
+    stage_t, stage_w, stage_d, plan, own_sem, z_send, z_recv, p_send, p_recv, c_send, c_recv,
+):
+    z, y, x, c = (lax.axis_index(a) for a in 'zyxc')
+    slot = lambda yy, xx: yy * 4 + xx * 2 + c
+    own, by_x, by_y, far = slot(y, x), slot(y, 1 - x), slot(1 - y, x), slot(1 - y, 1 - x)
+    weights = ((wg_ref, wg_out), (wu_ref, wu_out), (wd_ref, wd_out))
+    arrays = ((x_ref, x_out), (plan, plan_out), (dy_ref, dy_out))
+    sent = []
+
+    def half(ref, where, h):
+        rows = ref.shape[1] // 2
+        return ref.at[where, pl.ds(h * rows, rows), :]
+
+    def own_half(part, h, side):
+        src, out = weights[part]
+        where = {'x': 1 - x} if side == 0 else {'y': 1 - y}
+        return hop(half(src, 0, h), half(out, own, h), p_send.at[side, part, h], p_recv.at[side, part, h], **where)
+
+    def onward(part, h):
+        at = half(weights[part][1], by_x if h == 0 else by_y, h)
+        where = {'y': 1 - y} if h == 0 else {'x': 1 - x}
+        return hop(at, at, p_send.at[2, part, h], p_recv.at[2, part, h], **where)
+
+    def landed(part, h, kind):
+        at = half(weights[part][1], (by_x, by_y, far)[kind], h)
+        hop(at, at, p_send.at[kind, part, h], p_recv.at[kind, part, h], c=1 - c).wait_recv()
+
+    def across(part, h, kind):
+        at = half(weights[part][1], (by_x, by_y, far)[kind], h)
+        return hop(at, at, c_send.at[kind, part, h], c_recv.at[kind, part, h], c=1 - c)
+
+    def across_own(part, h):
+        src, out = weights[part]
+        return hop(half(src, 0, h), half(out, own, h), c_send.at[3, part, h], c_recv.at[3, part, h], c=1 - c)
+
+    def crossed(part, h, kind):
+        twin = lambda yy, xx: yy * 4 + xx * 2 + 1 - c
+        where = (twin(y, 1 - x), twin(1 - y, x), twin(1 - y, 1 - x), twin(y, x))[kind]
+        at = half(weights[part][1], where, h)
+        hop(at, at, c_send.at[kind, part, h], c_recv.at[kind, part, h], c=1 - c).wait_recv()
+
+    def go(copy):
+        copy.start()
+        sent.append((None, copy))
+
+    def along(k, dist, up):
+        src, out = arrays[k]
+        at = out.at[z - dist if up else z + dist]
+        side = 0 if up else 1
+        return hop(src if dist == 0 else at, at, z_send.at[side, k, dist], z_recv.at[side, k, dist], z=z + 1 if up else z - 1)
+
+    def start_along(k, dist):
+        for up in (True, False):
+            cond = (z >= dist) & (z < depth - 1) if up else (z + dist < depth) & (z > 0)
+
+            @pl.when(cond)
+            def _(up=up):
+                along(k, dist, up).start()
+
+            sent.append((cond, along(k, dist, up)))
+
+    def await_along(k, dist):
+        for up in (True, False):
+            @pl.when(z > dist if up else z + dist + 1 < depth)
+            def _(up=up):
+                at = arrays[k][1].at[z - dist - 1 if up else z + dist + 1]
+                side = 0 if up else 1
+                hop(at, at, z_send.at[side, k, dist], z_recv.at[side, k, dist], c=1 - c).wait_recv()
+
+        if dist + 1 < depth - 1:
+            start_along(k, dist + 1)
+
+    copies = []
+    for i, (src, buf, out) in enumerate((
+        (x_ref, stage_t.at[0], x_out.at[z]), (dy_ref, stage_t.at[1], dy_out.at[z]),
+        (wg_ref.at[0], stage_w.at[0], wg_out.at[own]), (wu_ref.at[0], stage_w.at[1], wu_out.at[own]),
+        (wd_ref.at[0], stage_d, wd_out.at[own]),
+    )):
+        copies.append((pltpu.make_async_copy(src, buf, own_sem.at[i]), pltpu.make_async_copy(buf, out, own_sem.at[i])))
+        copies[-1][0].start()
+
+    meet(depth, z, y, x, c)
+    start_along(0, 0)
+    for part in range(3):
+        go(own_half(part, 0, 0))
+        go(own_half(part, 1, 1))
+    for part in range(3):
+        go(own_half(part, 1, 0))
+        go(own_half(part, 0, 1))
+    for part in range(3):
+        for h in range(2):
+            go(across_own(part, h))
+    make_plan(experts, route_ref, gate_ref, plan)
+    start_along(1, 0)
+    start_along(2, 0)
+    copies.append((None, pltpu.make_async_copy(plan, plan_out.at[z], own_sem.at[5])))
+    for i, (load, store) in enumerate(copies):
+        if load is not None:
+            load.wait()
+        store.start()
+
+    def relay(part, h):
+        landed(part, h, h)
+        go(onward(part, h))
+        go(across(part, h, h))
+
+    def relay_twin(part, h):
+        landed(part, h, 1 - h)
+        go(across(part, h, 1 - h))
+
+    for part in range(2):
+        relay(part, 0)
+        relay(part, 1)
+    await_along(0, 0)
+    await_along(1, 0)
+    relay(2, 0)
+    relay(2, 1)
+    await_along(2, 0)
+    for part in range(3):
+        relay_twin(part, 1)
+        relay_twin(part, 0)
+    await_along(0, 1)
+    await_along(1, 1)
+    for part in range(3):
+        for h in range(2):
+            landed(part, h, 2)
+            go(across(part, h, 2))
+    await_along(2, 1)
+    for k in range(3):
+        await_along(k, 2)
+    for part in range(3):
+        for h in range(2):
+            for kind in range(4):
+                crossed(part, h, kind)
+    for cond, copy in sent:
+        if cond is None:
+            copy.wait_send()
+        else:
+            @pl.when(cond)
+            def _(copy=copy):
+                copy.wait_send()
+    for _, store in copies:
+        store.wait()
+
+
+def spread(depth, experts, x_tok, dy_tok, route, gate, w_gate, w_up, w_down):
+    toks, dim = x_tok.shape
+    ff = w_down.shape[1]
+    any_space = pl.BlockSpec(memory_space=pl.ANY)
+    vmem = pl.BlockSpec(memory_space=pltpu.VMEM)
+    rows = 2 * experts + 8
+    shape = jax.ShapeDtypeStruct
+    dma = pltpu.SemaphoreType.DMA
+    return pl.pallas_call(
+        functools.partial(spread_kernel, depth, experts),
+        in_specs=[any_space, any_space, vmem, vmem, any_space, any_space, any_space],
+        out_specs=[any_space] * 6,
+        out_shape=[
+            shape((depth, toks, dim), BF16), shape((depth, toks, dim), BF16), shape((depth, rows, toks), F32),
+            shape((8, dim, ff), BF16), shape((8, dim, ff), BF16), shape((8, ff, dim), BF16),
+        ],
+        scratch_shapes=[
+            pltpu.VMEM((2, toks, dim), BF16), pltpu.VMEM((2, dim, ff), BF16), pltpu.VMEM((ff, dim), BF16),
+            pltpu.VMEM((rows, toks), F32), dma((6,)), dma((2, 3, depth)), dma((2, 3, depth)),
+            dma((3, 3, 2)), dma((3, 3, 2)), dma((4, 3, 2)), dma((4, 3, 2)),
+        ],
+        compiler_params=pltpu.CompilerParams(collective_id=0, has_side_effects=True),
+        name="spread",
+    )(x_tok, dy_tok, route, gate, w_gate, w_up, w_down)
+
+
 def expert_kernel(
-    n_tiles, n_exp, cum_ref, off_ref, row_ref, col_ref, x_ref, dy_ref, wg_ref, wu_ref, wd_ref,
-    y_ref, dx_ref, dwg_ref, dwu_ref, dwd_ref, x_rows, g_rows, o_win, d_win,
+    n_tiles, n_exp, count_ref, place_ref, rank_ref, gate_ref, x_ref, dy_ref, wg_ref, wu_ref, wd_ref,
+    y_ref, dx_ref, dwg_ref, dwu_ref, dwd_ref, x_rows, g_rows, o_win, d_win, cum_ref, off_ref,
 ):
     step = pl.program_id(0)
+
+    @pl.when(step == 0)
+    def _count():
+        base = jnp.int32(0)
+        for exp in range(n_exp):
+            run = jnp.int32(0)
+            cum_ref[exp] = run
+            for tile in range(n_tiles):
+                run += count_ref[tile * n_exp + exp]
+                cum_ref[(tile + 1) * n_exp + exp] = run
+            off_ref[exp] = base
+            base += ((run + ALIGN - 1) // ALIGN) * ALIGN
 
     def span(tile, exp):
         lo = cum_ref[tile * n_exp + exp]
@@ -37,10 +280,11 @@
         tile = step
 
         def window(exp, lo, hi, start):
-            place = (lax.broadcasted_iota(jnp.int32, (WIN, TILE), 0) + start).astype(F32)
-            hit = row_ref[0, exp : exp + 1, :] == place
+            first = (start - lo).astype(F32)
+            place = lax.broadcasted_iota(jnp.int32, (WIN, TILE), 0).astype(F32) + first
+            hit = rank_ref[0, exp : exp + 1, :] == place
             take = jnp.where(hit, 1.0, 0.0).astype(BF16)
-            scale = jnp.where(hit, row_ref[0, n_exp + exp : n_exp + exp + 1, :], 0.0).astype(BF16)
+            scale = jnp.where(hit, gate_ref[0, exp : exp + 1, :], 0.0).astype(BF16)
             row = lax.broadcasted_iota(jnp.int32, (WIN, 1), 0) + start
             mine = (row >= lo) & (row < hi)
             here = pl.ds(pl.multiple_of(off_ref[exp] + start, ALIGN), WIN)
@@ -94,10 +338,11 @@
         tile = step - n_tiles - n_exp
 
         def window(exp, lo, hi, start):
-            place = (lax.broadcasted_iota(jnp.int32, (TILE, WIN), 1) + start).astype(F32)
-            hit = col_ref[:, exp : exp + 1] == place
+            first = (start - lo).astype(F32)
+            place = lax.broadcasted_iota(jnp.int32, (WIN, TILE), 0).astype(F32) + first
+            hit = rank_ref[0, exp : exp + 1, :] == place
             put = jnp.where(hit, 1.0, 0.0).astype(BF16)
-            scale = jnp.where(hit, col_ref[:, n_exp + exp : n_exp + exp + 1], 0.0).astype(BF16)
+            scale = jnp.where(hit, gate_ref[0, exp : exp + 1, :], 0.0).astype(BF16)
             row = lax.broadcasted_iota(jnp.int32, (WIN, 1), 0) + start
             mine = (row >= lo) & (row < hi)
             here = pl.ds(pl.multiple_of(off_ref[exp] + start, ALIGN), WIN)
@@ -117,8 +362,8 @@
                 scales.append(scale)
                 o_win[i * WIN : (i + 1) * WIN, :] = o_blk
                 d_win[i * WIN : (i + 1) * WIN, :] = d_blk
-            y_add = dot(jnp.concatenate(scales, axis=1), o_win[...])
-            dx_add = dot(jnp.concatenate(puts, axis=1), d_win[...])
+            y_add = dot(jnp.concatenate(scales, axis=0), o_win[...], ((0,), (0,)))
+            dx_add = dot(jnp.concatenate(puts, axis=0), d_win[...], ((0,), (0,)))
             y_ref[...] = y_add if part == 0 else y_ref[...] + y_add
             dx_ref[...] = dx_add if part == 0 else dx_ref[...] + dx_add
         for exp in range(n_exp):
@@ -129,21 +374,23 @@
                 @pl.loop(1, (hi - start + WIN - 1) // WIN)
                 def _(w):
                     put, scale, o_blk, d_blk = window(exp, lo, hi, start + w * WIN)
-                    y_ref[...] += dot(scale, o_blk)
-                    dx_ref[...] += dot(put, d_blk)
-
-
-def expert_layer(cum, off, table, x_col, dy_col, w_gate, w_up, w_down, cap):
+                    y_ref[...] += dot(scale, o_blk, ((0,), (0,)))
+                    dx_ref[...] += dot(put, d_blk, ((0,), (0,)))
+
+
+def expert_layer(counts, place, plan_col, x_col, dy_col, w_gate, w_up, w_down, cap, n_dev):
     tokens, dim = x_col.shape
     n_exp, _, ff = w_gate.shape
     n_tiles = tokens // TILE
     total = n_exp * (-(-cap // ALIGN) * ALIGN) + ROWS
-    by_tile = table.reshape(n_tiles, TILE, 2 * n_exp).transpose(0, 2, 1)
+    per = plan_col.shape[2] // TILE
     first = lambda i: jnp.minimum(i, n_tiles - 1)
     middle = lambda i: jnp.clip(i - n_tiles, 0, n_exp - 1)
     last = lambda i: jnp.maximum(i - n_tiles - n_exp, 0)
-    rows = pl.BlockSpec((1, 2 * n_exp, TILE), lambda i, *_: (first(i), 0, 0))
-    cols = pl.BlockSpec((TILE, 2 * n_exp), lambda i, *_: (last(i), 0))
+    tile_of = lambda i: jnp.where(i < n_tiles, i, last(i))
+    plan_at = lambda part: lambda i, counts, place: (tile_of(i) // per, place[0] + part, tile_of(i) % per)
+    ranks = pl.BlockSpec((1, n_exp, TILE), plan_at(0))
+    gates = pl.BlockSpec((1, n_exp, TILE), plan_at(n_dev // n_exp))
     toks_in = pl.BlockSpec((TILE, dim), lambda i, *_: (first(i), 0))
     toks_out = pl.BlockSpec((TILE, dim), lambda i, *_: (last(i), 0))
     wide = pl.BlockSpec((1, dim, ff), lambda i, *_: (middle(i), 0, 0))
@@ -153,13 +400,15 @@
         grid_spec=pltpu.PrefetchScalarGridSpec(
             num_scalar_prefetch=2,
             grid=(2 * n_tiles + n_exp,),
-            in_specs=[rows, cols, toks_in, toks_in, wide, wide, tall],
+            in_specs=[ranks, gates, toks_in, toks_in, wide, wide, tall],
             out_specs=[toks_out, toks_out, wide, wide, tall],
             scratch_shapes=[
                 pltpu.VMEM((total, dim), BF16),
                 pltpu.VMEM((total, dim), BF16),
                 pltpu.VMEM((GROUP * WIN, dim), BF16),
                 pltpu.VMEM((GROUP * WIN, dim), BF16),
+                pltpu.SMEM(((n_tiles + 1) * n_exp,), jnp.int32),
+                pltpu.SMEM((n_exp,), jnp.int32),
             ],
         ),
         out_shape=[
@@ -174,23 +423,7 @@
         ),
         cost_estimate=pl.CostEstimate(flops=60_000_000_000, bytes_accessed=120_000_000, transcendentals=3_000_000),
         name="experts",
-    )(cum, off, by_tile, table, x_col, dy_col, w_gate, w_up, w_down)
-
-
-def plan(route, gates, first_exp, n_exp):
-    hits = route[:, :, None] == first_exp + jnp.arange(n_exp, dtype=jnp.int32)[None, None, :]
-    member = jnp.any(hits, axis=1)
-    gate = jnp.sum(jnp.where(hits, gates[:, :, None].astype(F32), 0.0), axis=1)
-    tiles = member.reshape(-1, TILE, n_exp)
-    per_tile = jnp.sum(tiles.astype(jnp.int32), axis=1)
-    cum = jnp.concatenate([jnp.zeros((1, n_exp), jnp.int32), jnp.cumsum(per_tile, axis=0)])
-    lower = jnp.tril(jnp.ones((TILE, TILE), BF16), -1)
-    inner = jnp.einsum('ab,ibe->iae', lower, tiles.astype(BF16), preferred_element_type=F32).astype(jnp.int32)
-    rank = jnp.where(tiles, inner + cum[:-1, None, :], -(1 << 20)).reshape(-1, n_exp)
-    count = cum[-1]
-    padded = (count + ALIGN - 1) // ALIGN * ALIGN
-    off = jnp.cumsum(padded) - padded
-    return cum.reshape(-1), off.astype(jnp.int32), jnp.concatenate([rank.astype(F32), gate], axis=1)
+    )(counts, place, plan_col, plan_col, x_col, dy_col, w_gate, w_up, w_down)
 
 
 def solution(mesh):
@@ -204,15 +437,15 @@
         tok_loc, top_k = route_idx.shape
         cap = depth * (2 * tok_loc * top_k // (n_dev * w_gate.shape[0] - 2))
         n_exp = 8 * w_gate.shape[0]
-        gather_z = lambda a: lax.all_gather(a, 'z', axis=0, tiled=True)
-        gather_p = lambda a: lax.all_gather(a, plane, axis=0, tiled=True)
-        route = gather_z(route_idx)
-        gate_all = gather_z(gates)
-        cum, off, table = plan(route, gate_all, lax.axis_index('z') * n_exp, n_exp)
-        x_col = gather_z(x_tok)
-        dy_col = gather_z(dy_tok)
+        x_col, dy_col, plan_col, wg_all, wu_all, wd_all = spread(
+            depth, n_dev, x_tok, dy_tok, route_idx.T, gates.T.astype(F32), w_gate, w_up, w_down
+        )
+        place = lax.axis_index('z')
+        per = tok_loc // TILE
+        counts = lax.dynamic_slice(plan_col[:, 2 * n_dev : 2 * n_dev + per, :n_dev], (0, 0, place * n_exp), (depth, per, n_exp))
         y, dx, g_gate, g_up, g_down = expert_layer(
-            cum, off, table, x_col, dy_col, gather_p(w_gate), gather_p(w_up), gather_p(w_down), cap
+            counts.reshape(-1).astype(jnp.int32), place.reshape(1), plan_col, x_col.reshape(-1, x_tok.shape[1]),
+            dy_col.reshape(-1, x_tok.shape[1]), wg_all, wu_all, wd_all, cap, n_dev
         )
         sum_z = lambda a: lax.psum_scatter(a, 'z', scatter_dimension=0, tiled=True)
         sum_p = lambda a: lax.psum_scatter(a, plane, scatter_dimension=0, tiled=True)

time: 1100 us -> 923 us (0.84)
  waiting for transfers between devices: 948 us -> 649 us
  Pallas kernels: 98.9 us -> 248 us
  blocking collectives: 28.5 us -> 0 us
    all_gather x5 -> x0, waiting for transfers between devices: 297 us -> none  [the longest x3 166 us: local_step(): gather_p = lambda a: lax.all_gather(a, plane, axis=0, tiled=True)]
    pallas_call x0 -> x1, Pallas kernels: none -> 151 us  [spread(): pl.pallas_call(functools.partial(spread_kernel, depth, experts), in_specs...]
    all_gather x2 -> x0, blocking collectives: 28.5 us -> none  [local_step(): gather_z = lambda a: lax.all_gather(a, 'z', axis=0, tiled=True)]
  transfers between devices with their start and end apart: 10 -> 5, of which waited for: 10 -> 5; matrix products, arithmetic and copies ran while one was open for 1% -> 1% of each run, Pallas kernels for 0% -> 0%
where the time goes in v2:
time: 923 us; the launch traced here: 919 us
  waiting for transfers between devices  649 us (70%)
  Pallas kernels  248 us (27%)
  between operations  13.8 us (1%)
    reduce_scatter x3, waiting for transfers between devices, local_step(): lax.psum_scatter(a, plane, scatter_dimension=0, tiled=True)  356 us
    reduce_scatter x2, waiting for transfers between devices, local_step(): sum_z = lambda a: lax.psum_scatter(a, 'z', scatter_dimension=0, tiled=True)  291 us
    pallas_call x1, Pallas kernels, spread(): pl.pallas_call(functools.partial(spread_kernel, depth, experts), in_specs...  151 us
    pallas_call x1, Pallas kernels, expert_layer(): pl.pallas_call(functools.partial(expert_kernel, n_tiles, n_exp), grid_spe...  96.3 us
  transfers between devices with their start and end apart: 5, of which 5 were waited for; matrix products, arithmetic and copies ran while one was open for 1% of the time, Pallas kernels for 0%

profile of v2, /device:TPU:0, one launch (start us, length us, event | category | flops | bytes accessed | tf_op | source)
XLA Modules:
  0.0 918.8 jit_solution(6698520362164241971)
XLA Ops:
  7.2 0.0 reduce-scatter.6.cloned.1.call-start
  7.2 1.3 convert_bitcast_fusion.gate_ref
  8.5 151.5 %spread.1 = (bf16[4,512,1024]{2,1,0:T(8,128)(2,1)}, bf16[4,512,1024]{2,1,0:T(8,128)(2,1)}, f32[4,72,512]{2,1,0:T(8,128)}, bf16[8,1024,512]{2,1,0:T(8,128)(2,1)},...) custom-call(bf16[512,1024]{1,0:T(8,128)(2,1)} %x_ref.1, bf16[512,1024]{1,0:T(8,128)(2,1)} %dy_ref.1, ...), custom_call_target="tpu_custom_call" | custom-call | tf_op jit(solution)/shard_map/spread/pallas_call | solution.py:236
  160.0 0.7 slice.3
  160.7 0.1 dynamic-slice_convert_fusion
  160.8 0.6 convert_element_type.19.count_ref
  161.4 96.3 %experts.1 = (f32[2048,1024]{1,0:T(8,128)}, f32[2048,1024]{1,0:T(8,128)}, f32[8,1024,512]{2,1,0:T(8,128)}, f32[8,1024,512]{2,1,0:T(8,128)}, f32[8,512,1024]{2,1,0:T(8,128)}) custom-call(s32[64]{0:T(128)} %convert_element_type.19.count_ref, s32[1]{0:T(128)} %bitcast.2.place_ref, f32[4,72,512]{2,1,0:T(8,128)} %get-tuple-element.16.rank_ref.gate_ref, ...), custom_call_target="tpu_custom_call" | custom-call | flops 60000002048 | bytes 120000000 | tf_op jit(solution)/shard_map/experts/pallas_call | solution.py:398
  257.7 0.0 reduce-scatter.6.cloned.1.call-update
  257.7 0.0 reduce-scatter.8.cloned.1.call-start
  257.8 0.7 reduce-scatter.8.cloned.1.call-update
  258.5 0.0 reduce-scatter.10.cloned.1.call-start
  258.5 0.7 reduce-scatter.10.cloned.1.call-update
  259.2 0.0 reduce-scatter.12.cloned.1.call-start
  259.3 0.5 reduce-scatter.12.cloned.1.call-update
  259.8 0.0 reduce-scatter.14.cloned.1.call-start
  259.8 0.5 reduce-scatter.14.cloned.1.call-update
  260.4 146.3 %reduce-scatter.6.cloned.1.call-done = f32[512,1024]{1,0:T(8,128)} async-done(((f32[2048,1024]{1,0:T(8,128)}), f32[512,1024]{1,0:T(8,128)}) %reduce-scatter.6.cloned.1.call-update) | async-done | bytes 2097168 | tf_op jit(solution)/shard_map/reduce_scatter | solution.py:450
  406.7 2.7 convert_element_type.20
  409.4 144.3 %reduce-scatter.8.cloned.1.call-done = f32[512,1024]{1,0:T(8,128)} async-done(((f32[2048,1024]{1,0:T(8,128)}), f32[512,1024]{1,0:T(8,128)}) %reduce-scatter.8.cloned.1.call-update) | async-done | bytes 2097168 | tf_op jit(solution)/shard_map/reduce_scatter | solution.py:450
  553.7 2.7 convert_element_type.21
  556.5 117.2 %reduce-scatter.10.cloned.1.call-done = f32[1,1024,512]{2,1,0:T(8,128)} async-done(((f32[8,1024,512]{2,1,0:T(8,128)}), f32[1,1024,512]{2,1,0:T(8,128)}) %reduce-scatter.10.cloned.1.call-update) | async-done | bytes 2097168 | tf_op jit(solution)/shard_map/reduce_scatter | solution.py:451
  673.7 119.3 %reduce-scatter.12.cloned.1.call-done = f32[1,1024,512]{2,1,0:T(8,128)} async-done(((f32[8,1024,512]{2,1,0:T(8,128)}), f32[1,1024,512]{2,1,0:T(8,128)}) %reduce-scatter.12.cloned.1.call-update) | async-done | bytes 2097168 | tf_op jit(solution)/shard_map/reduce_scatter | solution.py:451
  793.0 119.3 %reduce-scatter.14.cloned.1.call-done = f32[1,512,1024]{2,1,0:T(8,128)} async-done(((f32[8,512,1024]{2,1,0:T(8,128)}), f32[1,512,1024]{2,1,0:T(8,128)}) %reduce-scatter.14.cloned.1.call-update) | async-done | bytes 2097168 | tf_op jit(solution)/shard_map/reduce_scatter | solution.py:451
Async XLA Ops:
  7.2 399.5 %reduce-scatter.6.cloned.1.call-start = ((), (), s32[]{:S(2)}) async-start(), calls=%async_computation.5 | async-start | bytes 10485760 | tf_op jit(solution)/shard_map/reduce_scatter | solution.py:450
  257.7 296.0 %reduce-scatter.8.cloned.1.call-start = ((), (), s32[]{:S(2)}) async-start(), calls=%async_computation.6 | async-start | bytes 10485760 | tf_op jit(solution)/shard_map/reduce_scatter | solution.py:450
  258.5 415.2 %reduce-scatter.10.cloned.1.call-start = ((), (), s32[]{:S(2)}) async-start(), calls=%async_computation.7 | async-start | bytes 18874368 | tf_op jit(solution)/shard_map/reduce_scatter | solution.py:451
  259.2 533.8 %reduce-scatter.12.cloned.1.call-start = ((), (), s32[]{:S(2)}) async-start(), calls=%async_computation.8 | async-start | bytes 18874368 | tf_op jit(solution)/shard_map/reduce_scatter | solution.py:451
  259.8 652.5 %reduce-scatter.14.cloned.1.call-start = ((), (), s32[]{:S(2)}) async-start(), calls=%async_computation.9 | async-start | bytes 18874368 | tf_op jit(solution)/shard_map/reduce_scatter | solution.py:451
Sparse Core Ops, SparseCore 0:
  257.9 148.7 reduce-scatter.5
  409.0 144.6 reduce-scatter.7
  557.9 115.7 reduce-scatter.9
  677.7 115.2 reduce-scatter.11
  797.0 115.2 reduce-scatter.13

commit v3 on v2

--- a/solution.py
+++ b/solution.py
@@ -251,9 +251,272 @@
     )(x_tok, dy_tok, route, gate, w_gate, w_up, w_down)
 
 
+CHUNK = 128
+BAND = 64
+LAG = 3
+RING = 6
+
+
+def collect_kernel(
+    depth, yd_ref, g_ref, y_out, dx_out, g_out, twin,
+    z_land, x_land, y_land, x_last, y_last, total, x_buf, y_buf, f_buf, z_buf,
+    t_sem, x_load, y_load, f_load, z_load, z_send, z_recv, x_send, x_recv, y_send, y_recv, c_send, c_recv,
+):
+    z, y, x, c = (lax.axis_index(a) for a in 'zyxc')
+    cell = lambda yy, xx: yy * 2 + xx
+    mine, by_x, by_y, far = cell(y, x), cell(y, 1 - x), cell(1 - y, x), cell(1 - y, 1 - x)
+    bands = yd_ref.shape[2] // BAND
+    n_part = g_ref.shape[1] // CHUNK // 2
+    n_col = 2 * (depth - 1) * bands
+    n_link = 3 * n_part
+    piece = 4 * CHUNK
+    order = (far, by_x, by_y, mine)
+    rows = lambda i: pl.ds(pl.multiple_of(i * CHUNK, CHUNK), CHUNK)
+
+    def swap(kind, q):
+        at = pl.ds(q * piece, piece)
+        return hop(g_ref.at[2 * order[kind] + 1 - c, at, :], twin.at[order[kind], at, :], c_send.at[kind, q], c_recv.at[kind, q], c=1 - c)
+
+    half = n_part // 4
+    swaps = [(0, q + h * half) for q in range(half) for h in range(2)]
+    swaps += [(1 + h, q + h * half) for q in range(half) for h in range(2)]
+    swaps += [(2 - h, q + h * half) for q in range(half) for h in range(2)]
+    swaps += [(3, q + h * half) for q in range(half) for h in range(2)]
+
+    own_total = [pltpu.make_async_copy(yd_ref.at[k, z], total.at[k], t_sem.at[k]) for k in range(2)]
+    for copy in own_total:
+        copy.start()
+    meet(depth, z, y, x, c)
+    for kind, q in swaps:
+        swap(kind, q).start()
+
+    def link_item(side, i):
+        leg = i // n_part
+        j = i % n_part
+        near, other = (by_x, by_y) if side == 0 else (by_y, by_x)
+        kind_near, kind_other = (1, 2) if side == 0 else (2, 1)
+        first = jnp.where(leg < 2, side, 1 - side)
+        chunk = first * n_part + j
+        expert = jnp.where(leg == 0, far, near)
+        kind = jnp.where(leg == 0, 0, kind_near)
+        return leg, j, chunk, expert, kind
+
+    def fetch(chunk, expert, kind, fresh, buf, sems):
+        @pl.when(fresh)
+        def _():
+            for k in range(4):
+                @pl.when(kind == k)
+                def _(k=k):
+                    at = pl.ds(pl.multiple_of(chunk // 4 * piece, piece), piece)
+                    q = chunk // 4
+                    hop(twin.at[order[k], at, :], twin.at[order[k], at, :], c_send.at[k, q], c_recv.at[k, q], c=1 - c).wait_recv()
+
+        pltpu.make_async_copy(g_ref.at[2 * expert + c, rows(chunk), :], buf.at[0], sems.at[0]).start()
+        pltpu.make_async_copy(twin.at[expert, rows(chunk), :], buf.at[1], sems.at[1]).start()
+
+    def fetched(buf, sems):
+        pltpu.make_async_copy(g_ref.at[0, rows(0), :], buf.at[0], sems.at[0]).wait()
+        pltpu.make_async_copy(twin.at[0, rows(0), :], buf.at[1], sems.at[1]).wait()
+
+    links = (
+        (x_buf, x_load, x_send, x_recv, x_land, x_last, {'x': 1 - x}),
+        (y_buf, y_load, y_send, y_recv, y_land, y_last, {'y': 1 - y}),
+    )
+
+    def landing(side, i):
+        land, last = links[side][4], links[side][5]
+        return land, last
+
+    def link_send(side, i, wait_only=False):
+        buf, _, send, recv, land, last, where = links[side]
+        src = buf.at[i % RING, 0]
+
+        @pl.when(i < 2 * n_part)
+        def _():
+            copy = hop(src, land.at[jnp.minimum(i, 2 * n_part - 1)], send.at[i], recv.at[i], **where)
+            copy.wait_send() if wait_only else copy.start()
+
+        @pl.when(i >= 2 * n_part)
+        def _():
+            copy = hop(src, last.at[jnp.maximum(i - 2 * n_part, 0)], send.at[i], recv.at[i], **where)
+            copy.wait_send() if wait_only else copy.start()
+
+    def landed(side, ref, i):
+        recv, send = links[side][3], links[side][2]
+        hop(ref, ref, send.at[i], recv.at[i], c=1 - c).wait_recv()
+
+    def link_prepare(side, i):
+        buf, load = links[side][0], links[side][1]
+
+        @pl.when((i >= RING) & (i < n_link))
+        def _():
+            link_send(side, i - RING, wait_only=True)
+
+        @pl.when(i < n_link)
+        def _():
+            leg, j, chunk, expert, kind = link_item(side, i)
+            fetch(chunk, expert, kind, j % 4 == 0, buf.at[i % RING], load.at[i % RING])
+
+    def link_turn(side, i):
+        buf, load = links[side][0], links[side][1]
+        other_land = links[1 - side][4]
+
+        @pl.when(i < n_link)
+        def _():
+            b = i % RING
+            fetched(buf.at[b], load.at[b])
+            buf[b, 0] += buf[b, 1]
+
+            @pl.when(i >= 2 * n_part)
+            def _():
+                j = i - 2 * n_part
+                landed(1 - side, other_land.at[j], j)
+                buf[b, 0] += other_land[j]
+
+            link_send(side, i)
+
+    def last_prepare(h, j):
+        @pl.when((j >= 0) & (j < n_part))
+        def _():
+            fetch(h * n_part + j, mine, 3, j % 4 == 0, f_buf.at[h, j % 2], f_load.at[h, j % 2])
+
+    def last_turn(h, j):
+        @pl.when((j >= 0) & (j < n_part))
+        def _():
+            land, last = links[h][4], links[1 - h][5]
+            fetched(f_buf.at[h, j % 2], f_load.at[h, j % 2])
+            landed(h, land.at[n_part + j], n_part + j)
+            landed(1 - h, last.at[j], 2 * n_part + j)
+            value = f_buf[h, j % 2, 0] + f_buf[h, j % 2, 1] + (land[n_part + j] + last[j])
+            g_out[rows(h * n_part + j), :] = value
+
+    def column(side, k):
+        role = z if side == 0 else depth - 1 - z
+        arr = k // ((depth - 1) * bands)
+        goal = depth - 1 - (k // bands) % (depth - 1)
+        block = goal if side == 0 else depth - 1 - goal
+        slot = block + 1 if side == 0 else block
+        at = pl.ds(pl.multiple_of(k % bands * BAND, BAND), BAND)
+        return role, arr, goal, block, slot, at
+
+    def column_copy(side, k, src):
+        _, arr, _, _, slot, at = column(side, k)
+        return hop(src, z_land.at[arr, slot, at, :], z_send.at[side, k], z_recv.at[side, k], z=z + 1 if side == 0 else z - 1)
+
+    def turn_of(side, t):
+        role = z if side == 0 else depth - 1 - z
+        return t - LAG * role
+
+    def column_prepare(side, t):
+        k = turn_of(side, t)
+        kk = jnp.clip(k, 0, n_col - 1)
+        role, arr, goal, block, slot, at = column(side, kk)
+
+        @pl.when((k >= 0) & (k < n_col) & (role > 0) & (goal > role))
+        def _():
+            pltpu.make_async_copy(yd_ref.at[arr, block, at, :], z_buf.at[side, kk % 2], z_load.at[side, kk % 2]).start()
+
+    def column_turn(side, t):
+        k = turn_of(side, t)
+        kk = jnp.clip(k, 0, n_col - 1)
+        role, arr, goal, block, slot, at = column(side, kk)
+        live = (k >= 0) & (k < n_col) & (goal >= role)
+
+        @pl.when(live & (role == 0))
+        def _():
+            column_copy(side, kk, yd_ref.at[arr, block, at, :]).start()
+
+        @pl.when(live & (role > 0))
+        def _():
+            here = z_land.at[arr, slot, at, :]
+            hop(here, here, z_send.at[side, kk], z_recv.at[side, kk], c=1 - c).wait_recv()
+
+            @pl.when(goal > role)
+            def _():
+                pltpu.make_async_copy(yd_ref.at[arr, block, at, :], z_buf.at[side, kk % 2], z_load.at[side, kk % 2]).wait()
+                z_land[arr, slot, at, :] += z_buf[side, kk % 2]
+                column_copy(side, kk, here).start()
+
+            @pl.when(goal == role)
+            def _():
+                total[arr, at, :] += z_land[arr, slot, at, :]
+
+    def prepare(t):
+        for side in range(2):
+            link_prepare(side, t)
+            column_prepare(side, t)
+            last_prepare(side, t - 2 * n_part - LAG)
+
+    prepare(jnp.int32(0))
+    for copy in own_total:
+        copy.wait()
+    steps = max(n_col + LAG * (depth - 1), n_link + LAG)
+
+    @pl.loop(0, steps)
+    def _(t):
+        prepare(t + 1)
+        for side in range(2):
+            link_turn(side, t)
+        for side in range(2):
+            column_turn(side, t)
+        for side in range(2):
+            last_turn(side, t - 2 * n_part - LAG)
+
+    y_out[...] = total[0].astype(BF16)
+    dx_out[...] = total[1].astype(BF16)
+
+    @pl.loop(n_link - RING, n_link)
+    def _(i):
+        for side in range(2):
+            link_send(side, i, wait_only=True)
+
+    @pl.loop(0, n_col)
+    def _(k):
+        for side in range(2):
+            role, arr, goal, block, slot, at = column(side, k)
+
+            @pl.when(goal > role)
+            def _():
+                column_copy(side, k, z_land.at[arr, slot, at, :]).wait_send()
+
+    for kind, q in swaps:
+        swap(kind, q).wait_send()
+
+
+def collect(depth, yd, grads):
+    toks, dim = yd.shape[2:]
+    height, ff = grads.shape[1:]
+    n_part = height // CHUNK // 2
+    n_col = 2 * (depth - 1) * (toks // BAND)
+    any_space = pl.BlockSpec(memory_space=pl.ANY)
+    vmem = pl.BlockSpec(memory_space=pltpu.VMEM)
+    shape = jax.ShapeDtypeStruct
+    dma = pltpu.SemaphoreType.DMA
+    message = (CHUNK, ff)
+    return pl.pallas_call(
+        functools.partial(collect_kernel, depth),
+        in_specs=[any_space, any_space],
+        out_specs=[vmem, vmem, vmem, any_space],
+        out_shape=[shape((toks, dim), BF16), shape((toks, dim), BF16), shape((height, ff), F32), shape((4, height, ff), F32)],
+        scratch_shapes=[
+            pltpu.VMEM((2, depth + 1, toks, dim), F32),
+            pltpu.VMEM((2 * n_part, *message), F32), pltpu.VMEM((2 * n_part, *message), F32),
+            pltpu.VMEM((n_part, *message), F32), pltpu.VMEM((n_part, *message), F32),
+            pltpu.VMEM((2, toks, dim), F32),
+            pltpu.VMEM((RING, 2, *message), F32), pltpu.VMEM((RING, 2, *message), F32),
+            pltpu.VMEM((2, 2, 2, *message), F32), pltpu.VMEM((2, 2, BAND, dim), F32),
+            dma((2,)), dma((RING, 2)), dma((RING, 2)), dma((2, 2, 2)), dma((2, 2)),
+            dma((2, n_col)), dma((2, n_col)), dma((3 * n_part,)), dma((3 * n_part,)), dma((3 * n_part,)), dma((3 * n_part,)),
+            dma((4, height // CHUNK // 4)), dma((4, height // CHUNK // 4)),
+        ],
+        compiler_params=pltpu.CompilerParams(collective_id=1, has_side_effects=True, vmem_limit_bytes=66_000_000),
+        name="collect",
+    )(yd, grads)[:3]
+
+
 def expert_kernel(
     n_tiles, n_exp, count_ref, place_ref, rank_ref, gate_ref, x_ref, dy_ref, wg_ref, wu_ref, wd_ref,
-    y_ref, dx_ref, dwg_ref, dwu_ref, dwd_ref, x_rows, g_rows, o_win, d_win, cum_ref, off_ref,
+    yd_ref, dw_ref, x_rows, g_rows, o_win, d_win, cum_ref, off_ref,
 ):
     step = pl.program_id(0)
 
@@ -306,9 +569,8 @@
         exp = step - n_tiles
         count = cum_ref[n_tiles * n_exp + exp]
         base = off_ref[exp]
-        dwg_ref[...] = jnp.zeros_like(dwg_ref)
-        dwu_ref[...] = jnp.zeros_like(dwu_ref)
-        dwd_ref[...] = jnp.zeros_like(dwd_ref)
+        dw_ref[...] = jnp.zeros_like(dw_ref)
+        dim, ff = wg_ref.shape[1:]
 
         @pl.loop(0, (count + ROWS - 1) // ROWS)
         def _(b):
@@ -327,10 +589,11 @@
             dv = (da * u * s).astype(BF16)
             out = dot(act, wd_ref[0]).astype(BF16)
             dxr = (dot(du, wg_ref[0], ((1,), (1,))) + dot(dv, wu_ref[0], ((1,), (1,)))).astype(BF16)
-            dwd_ref[0] += dot(act, g_blk, ((0,), (0,)))
+            dw_ref[0, 2 * dim : 2 * dim + ff] += dot(act, g_blk[:, :ff], ((0,), (0,)))
+            dw_ref[0, 2 * dim + ff :] += dot(act, g_blk[:, ff:], ((0,), (0,)))
             g_rows[here, :] = jnp.where(live, dxr, g_rows[here, :])
-            dwg_ref[0] += dot(x_blk, du, ((0,), (0,)))
-            dwu_ref[0] += dot(x_blk, dv, ((0,), (0,)))
+            dw_ref[0, :dim] += dot(x_blk, du, ((0,), (0,)))
+            dw_ref[0, dim : 2 * dim] += dot(x_blk, dv, ((0,), (0,)))
             x_rows[here, :] = jnp.where(live, out, x_rows[here, :])
 
     @pl.when(step >= n_tiles + n_exp)
@@ -364,8 +627,8 @@
                 d_win[i * WIN : (i + 1) * WIN, :] = d_blk
             y_add = dot(jnp.concatenate(scales, axis=0), o_win[...], ((0,), (0,)))
             dx_add = dot(jnp.concatenate(puts, axis=0), d_win[...], ((0,), (0,)))
-            y_ref[...] = y_add if part == 0 else y_ref[...] + y_add
-            dx_ref[...] = dx_add if part == 0 else dx_ref[...] + dx_add
+            yd_ref[0] = y_add if part == 0 else yd_ref[0] + y_add
+            yd_ref[1] = dx_add if part == 0 else yd_ref[1] + dx_add
         for exp in range(n_exp):
             lo, hi, start = span(tile, exp)
 
@@ -374,8 +637,8 @@
                 @pl.loop(1, (hi - start + WIN - 1) // WIN)
                 def _(w):
                     put, scale, o_blk, d_blk = window(exp, lo, hi, start + w * WIN)
-                    y_ref[...] += dot(scale, o_blk, ((0,), (0,)))
-                    dx_ref[...] += dot(put, d_blk, ((0,), (0,)))
+                    yd_ref[0] += dot(scale, o_blk, ((0,), (0,)))
+                    yd_ref[1] += dot(put, d_blk, ((0,), (0,)))
 
 
 def expert_layer(counts, place, plan_col, x_col, dy_col, w_gate, w_up, w_down, cap, n_dev):
@@ -392,7 +655,8 @@
     ranks = pl.BlockSpec((1, n_exp, TILE), plan_at(0))
     gates = pl.BlockSpec((1, n_exp, TILE), plan_at(n_dev // n_exp))
     toks_in = pl.BlockSpec((TILE, dim), lambda i, *_: (first(i), 0))
-    toks_out = pl.BlockSpec((TILE, dim), lambda i, *_: (last(i), 0))
+    toks_out = pl.BlockSpec((2, TILE, dim), lambda i, *_: (0, last(i), 0))
+    grads = pl.BlockSpec((1, 3 * dim, ff), lambda i, *_: (middle(i), 0, 0))
     wide = pl.BlockSpec((1, dim, ff), lambda i, *_: (middle(i), 0, 0))
     tall = pl.BlockSpec((1, ff, dim), lambda i, *_: (middle(i), 0, 0))
     return pl.pallas_call(
@@ -401,7 +665,7 @@
             num_scalar_prefetch=2,
             grid=(2 * n_tiles + n_exp,),
             in_specs=[ranks, gates, toks_in, toks_in, wide, wide, tall],
-            out_specs=[toks_out, toks_out, wide, wide, tall],
+            out_specs=[toks_out, grads],
             scratch_shapes=[
                 pltpu.VMEM((total, dim), BF16),
                 pltpu.VMEM((total, dim), BF16),
@@ -412,11 +676,8 @@
             ],
         ),
         out_shape=[
-            jax.ShapeDtypeStruct((tokens, dim), F32),
-            jax.ShapeDtypeStruct((tokens, dim), F32),
-            jax.ShapeDtypeStruct(w_gate.shape, F32),
-            jax.ShapeDtypeStruct(w_up.shape, F32),
-            jax.ShapeDtypeStruct(w_down.shape, F32),
+            jax.ShapeDtypeStruct((2, tokens, dim), F32),
+            jax.ShapeDtypeStruct((n_exp, 3 * dim, ff), F32),
         ],
         compiler_params=pltpu.CompilerParams(
             dimension_semantics=("arbitrary",), vmem_limit_bytes=67_000_000,
@@ -443,12 +704,13 @@
         place = lax.axis_index('z')
         per = tok_loc // TILE
         counts = lax.dynamic_slice(plan_col[:, 2 * n_dev : 2 * n_dev + per, :n_dev], (0, 0, place * n_exp), (depth, per, n_exp))
-        y, dx, g_gate, g_up, g_down = expert_layer(
+        yd, grads = expert_layer(
             counts.reshape(-1).astype(jnp.int32), place.reshape(1), plan_col, x_col.reshape(-1, x_tok.shape[1]),
             dy_col.reshape(-1, x_tok.shape[1]), wg_all, wu_all, wd_all, cap, n_dev
         )
-        sum_z = lambda a: lax.psum_scatter(a, 'z', scatter_dimension=0, tiled=True)
-        sum_p = lambda a: lax.psum_scatter(a, plane, scatter_dimension=0, tiled=True)
-        return sum_z(y).astype(BF16), sum_z(dx).astype(BF16), sum_p(g_gate), sum_p(g_up), sum_p(g_down)
+        y, dx, dw = collect(depth, yd.reshape(2, depth, tok_loc, -1), grads)
+        dim, ff = w_gate.shape[1:]
+        g_down = jnp.concatenate([dw[2 * dim : 2 * dim + ff], dw[2 * dim + ff :]], axis=1)
+        return y, dx, dw[None, :dim], dw[None, dim : 2 * dim], g_down[None]
 
     return jax.shard_map(local_step, mesh=grid, in_specs=(spec,) * 7, out_specs=(spec,) * 5, check_vma=False)

time: 923 us -> 554 us (0.60)
  waiting for transfers between devices: 649 us -> 0 us
  Pallas kernels: 248 us -> 531 us
  between operations: 13.8 us -> 0.66 us
    reduce_scatter x5 -> x0, waiting for transfers between devices: 646 us -> none  [the longest x3 356 us: local_step(): lax.psum_scatter(a, plane, scatter_dimension=0, tiled=True)]
    pallas_call x0 -> x1, Pallas kernels: none -> 289 us  [collect(): pl.pallas_call(functools.partial(collect_kernel, depth), in_specs=[any_sp...]
  transfers between devices with their start and end apart: 5 -> 0, of which waited for: 5 -> 0; matrix products, arithmetic and copies ran while one was open for 1% -> 0% of each run, Pallas kernels for 0% -> 0%
where the time goes in v3:
time: 554 us; the launch traced here: 545 us
  Pallas kernels  531 us (96%)
  local copies, waits for them, and re-layouts  9.66 us (2%)
    pallas_call x1, Pallas kernels, collect(): pl.pallas_call(functools.partial(collect_kernel, depth), in_specs=[any_sp...  289 us
    pallas_call x1, Pallas kernels, spread(): pl.pallas_call(functools.partial(spread_kernel, depth, experts), in_specs...  151 us
    pallas_call x1, Pallas kernels, expert_layer(): pl.pallas_call(functools.partial(expert_kernel, n_tiles, n_exp), grid_spe...  91.2 us

profile of v3, /device:TPU:0, one launch (start us, length us, event | category | flops | bytes accessed | tf_op | source)
XLA Modules:
  0.0 544.6 jit_solution(12410674709886376682)
XLA Ops:
  0.6 1.3 convert_bitcast_fusion.gate_ref
  1.9 151.5 %spread.1 = (bf16[4,512,1024]{2,1,0:T(8,128)(2,1)}, bf16[4,512,1024]{2,1,0:T(8,128)(2,1)}, f32[4,72,512]{2,1,0:T(8,128)}, bf16[8,1024,512]{2,1,0:T(8,128)(2,1)},...) custom-call(bf16[512,1024]{1,0:T(8,128)(2,1)} %x_ref.1, bf16[512,1024]{1,0:T(8,128)(2,1)} %dy_ref.1, ...), custom_call_target="tpu_custom_call" | custom-call | tf_op jit(solution)/shard_map/spread/pallas_call | solution.py:236
  153.4 0.7 slice.15
  154.1 0.1 dynamic-slice_convert_fusion
  154.2 0.6 convert_element_type.13.count_ref
  154.8 91.2 %experts.1 = (f32[2,2048,1024]{2,1,0:T(8,128)}, f32[8,3072,512]{2,1,0:T(8,128)}) custom-call(s32[64]{0:T(128)} %convert_element_type.13.count_ref, s32[1]{0:T(128)} %bitcast.2.place_ref, f32[4,72,512]{2,1,0:T(8,128)} %get-tuple-element.16.rank_ref.gate_ref, f32[4,72,512]{2,1,0:T(8,128)} %get-tuple-element.16.rank_ref.gate_ref, bf16[2048,1024]{1,0:T(8,128)(2,1)} %bitcast.15, ...), custom_call_target="tpu_custom_call" | custom-call | flops 60000002048 | bytes 120000000 | tf_op jit(solution)/shard_map/experts/pallas_call | solution.py:662
  246.0 288.7 %collect.1 = (bf16[512,1024]{1,0:T(8,128)(2,1)}, bf16[512,1024]{1,0:T(8,128)(2,1)}, f32[3072,512]{1,0:T(8,128)}, f32[4,3072,512]{2,1,0:T(8,128)}) custom-call(f32[2,4,512,1024]{3,2,1,0:T(8,128)} %bitcast.13, f32[8,3072,512]{2,1,0:T(8,128)} %get-tuple-element.23.g_ref), custom_call_target="tpu_custom_call" | custom-call | tf_op jit(solution)/shard_map/collect/pallas_call | solution.py:496
  534.8 1.7 fusion
  536.5 4.7 slice_bitcast_fusion
  541.2 0.0 copy-start.1
  541.2 0.0 copy-start
  541.2 1.5 maximum_bitcast_fusion
  542.7 0.0 copy-done.1
  542.7 1.0 copy.14
  543.7 0.0 copy-done
  543.7 1.0 copy.15
Async XLA Ops:
  541.2 1.5 copy-start.1
  541.2 2.5 copy-start

commit v4 on v3

--- a/solution.py
+++ b/solution.py
@@ -12,8 +12,7 @@
 TILE = 256
 WIN = 128
 ALIGN = 16
-GROUP = 2
-ROWS = 256
+ROWS = 512
 
 
 def dot(a, b, dims=((1,), (0,))):
@@ -86,7 +85,8 @@
     slot = lambda yy, xx: yy * 4 + xx * 2 + c
     own, by_x, by_y, far = slot(y, x), slot(y, 1 - x), slot(1 - y, x), slot(1 - y, 1 - x)
     weights = ((wg_ref, wg_out), (wu_ref, wu_out), (wd_ref, wd_out))
-    arrays = ((x_ref, x_out), (plan, plan_out), (dy_ref, dy_out))
+    dy_head = dy_ref.at[pl.ds(0, dy_out.shape[1]), :]
+    arrays = ((x_ref, x_out), (plan, plan_out), (dy_head, dy_out))
     sent = []
 
     def half(ref, where, h):
@@ -154,7 +154,7 @@
 
     copies = []
     for i, (src, buf, out) in enumerate((
-        (x_ref, stage_t.at[0], x_out.at[z]), (dy_ref, stage_t.at[1], dy_out.at[z]),
+        (x_ref, stage_t.at[0], x_out.at[z]), (dy_head, stage_t.at[1, pl.ds(0, dy_out.shape[1]), :], dy_out.at[z]),
         (wg_ref.at[0], stage_w.at[0], wg_out.at[own]), (wu_ref.at[0], stage_w.at[1], wu_out.at[own]),
         (wd_ref.at[0], stage_d, wd_out.at[own]),
     )):
@@ -225,7 +225,7 @@
         store.wait()
 
 
-def spread(depth, experts, x_tok, dy_tok, route, gate, w_gate, w_up, w_down):
+def spread(depth, experts, head, x_tok, dy_tok, route, gate, w_gate, w_up, w_down):
     toks, dim = x_tok.shape
     ff = w_down.shape[1]
     any_space = pl.BlockSpec(memory_space=pl.ANY)
@@ -238,7 +238,7 @@
         in_specs=[any_space, any_space, vmem, vmem, any_space, any_space, any_space],
         out_specs=[any_space] * 6,
         out_shape=[
-            shape((depth, toks, dim), BF16), shape((depth, toks, dim), BF16), shape((depth, rows, toks), F32),
+            shape((depth, toks, dim), BF16), shape((depth, head, dim), BF16), shape((depth, rows, toks), F32),
             shape((8, dim, ff), BF16), shape((8, dim, ff), BF16), shape((8, ff, dim), BF16),
         ],
         scratch_shapes=[
@@ -254,20 +254,21 @@
 CHUNK = 128
 BAND = 64
 LAG = 3
+DELAY = 18
 RING = 6
 
 
 def collect_kernel(
-    depth, yd_ref, g_ref, y_out, dx_out, g_out, twin,
+    depth, dx_ref, g_ref, dx_out, g_out, twin,
     z_land, x_land, y_land, x_last, y_last, total, x_buf, y_buf, f_buf, z_buf,
     t_sem, x_load, y_load, f_load, z_load, z_send, z_recv, x_send, x_recv, y_send, y_recv, c_send, c_recv,
 ):
     z, y, x, c = (lax.axis_index(a) for a in 'zyxc')
     cell = lambda yy, xx: yy * 2 + xx
     mine, by_x, by_y, far = cell(y, x), cell(y, 1 - x), cell(1 - y, x), cell(1 - y, 1 - x)
-    bands = yd_ref.shape[2] // BAND
+    bands = dx_ref.shape[1] // BAND
     n_part = g_ref.shape[1] // CHUNK // 2
-    n_col = 2 * (depth - 1) * bands
+    n_col = (depth - 1) * bands
     n_link = 3 * n_part
     piece = 4 * CHUNK
     order = (far, by_x, by_y, mine)
@@ -283,9 +284,8 @@
     swaps += [(2 - h, q + h * half) for q in range(half) for h in range(2)]
     swaps += [(3, q + h * half) for q in range(half) for h in range(2)]
 
-    own_total = [pltpu.make_async_copy(yd_ref.at[k, z], total.at[k], t_sem.at[k]) for k in range(2)]
-    for copy in own_total:
-        copy.start()
+    own_total = pltpu.make_async_copy(dx_ref.at[z], total, t_sem)
+    own_total.start()
     meet(depth, z, y, x, c)
     for kind, q in swaps:
         swap(kind, q).start()
@@ -392,54 +392,53 @@
 
     def column(side, k):
         role = z if side == 0 else depth - 1 - z
-        arr = k // ((depth - 1) * bands)
-        goal = depth - 1 - (k // bands) % (depth - 1)
+        goal = depth - 1 - k // bands
         block = goal if side == 0 else depth - 1 - goal
         slot = block + 1 if side == 0 else block
         at = pl.ds(pl.multiple_of(k % bands * BAND, BAND), BAND)
-        return role, arr, goal, block, slot, at
+        return role, goal, block, slot, at
 
     def column_copy(side, k, src):
-        _, arr, _, _, slot, at = column(side, k)
-        return hop(src, z_land.at[arr, slot, at, :], z_send.at[side, k], z_recv.at[side, k], z=z + 1 if side == 0 else z - 1)
+        _, _, _, slot, at = column(side, k)
+        return hop(src, z_land.at[slot, at, :], z_send.at[side, k], z_recv.at[side, k], z=z + 1 if side == 0 else z - 1)
 
     def turn_of(side, t):
         role = z if side == 0 else depth - 1 - z
-        return t - LAG * role
+        return t - DELAY - LAG * role
 
     def column_prepare(side, t):
         k = turn_of(side, t)
         kk = jnp.clip(k, 0, n_col - 1)
-        role, arr, goal, block, slot, at = column(side, kk)
+        role, goal, block, slot, at = column(side, kk)
 
         @pl.when((k >= 0) & (k < n_col) & (role > 0) & (goal > role))
         def _():
-            pltpu.make_async_copy(yd_ref.at[arr, block, at, :], z_buf.at[side, kk % 2], z_load.at[side, kk % 2]).start()
+            pltpu.make_async_copy(dx_ref.at[block, at, :], z_buf.at[side, kk % 2], z_load.at[side, kk % 2]).start()
 
     def column_turn(side, t):
         k = turn_of(side, t)
         kk = jnp.clip(k, 0, n_col - 1)
-        role, arr, goal, block, slot, at = column(side, kk)
+        role, goal, block, slot, at = column(side, kk)
         live = (k >= 0) & (k < n_col) & (goal >= role)
 
         @pl.when(live & (role == 0))
         def _():
-            column_copy(side, kk, yd_ref.at[arr, block, at, :]).start()
+            column_copy(side, kk, dx_ref.at[block, at, :]).start()
 
         @pl.when(live & (role > 0))
         def _():
-            here = z_land.at[arr, slot, at, :]
+            here = z_land.at[slot, at, :]
             hop(here, here, z_send.at[side, kk], z_recv.at[side, kk], c=1 - c).wait_recv()
 
             @pl.when(goal > role)
             def _():
-                pltpu.make_async_copy(yd_ref.at[arr, block, at, :], z_buf.at[side, kk % 2], z_load.at[side, kk % 2]).wait()
-                z_land[arr, slot, at, :] += z_buf[side, kk % 2]
+                pltpu.make_async_copy(dx_ref.at[block, at, :], z_buf.at[side, kk % 2], z_load.at[side, kk % 2]).wait()
+                z_land[slot, at, :] += z_buf[side, kk % 2]
                 column_copy(side, kk, here).start()
 
             @pl.when(goal == role)
             def _():
-                total[arr, at, :] += z_land[arr, slot, at, :]
+                total[at, :] += z_land[slot, at, :]
 
     def prepare(t):
         for side in range(2):
@@ -448,9 +447,8 @@
             last_prepare(side, t - 2 * n_part - LAG)
 
     prepare(jnp.int32(0))
-    for copy in own_total:
-        copy.wait()
-    steps = max(n_col + LAG * (depth - 1), n_link + LAG)
+    own_total.wait()
+    steps = max(DELAY + n_col + LAG * (depth - 1), n_link + LAG)
 
     @pl.loop(0, steps)
     def _(t):
@@ -462,8 +460,7 @@
         for side in range(2):
             last_turn(side, t - 2 * n_part - LAG)
 
-    y_out[...] = total[0].astype(BF16)
-    dx_out[...] = total[1].astype(BF16)
+    dx_out[...] = total[...].astype(BF16)
 
     @pl.loop(n_link - RING, n_link)
     def _(i):
@@ -473,21 +470,21 @@
     @pl.loop(0, n_col)
     def _(k):
         for side in range(2):
-            role, arr, goal, block, slot, at = column(side, k)
+            role, goal, block, slot, at = column(side, k)
 
             @pl.when(goal > role)
             def _():
-                column_copy(side, k, z_land.at[arr, slot, at, :]).wait_send()
+                column_copy(side, k, z_land.at[slot, at, :]).wait_send()
 
     for kind, q in swaps:
         swap(kind, q).wait_send()
 
 
-def collect(depth, yd, grads):
-    toks, dim = yd.shape[2:]
+def collect(depth, dx_part, grads):
+    toks, dim = dx_part.shape[1:]
     height, ff = grads.shape[1:]
     n_part = height // CHUNK // 2
-    n_col = 2 * (depth - 1) * (toks // BAND)
+    n_col = (depth - 1) * (toks // BAND)
     any_space = pl.BlockSpec(memory_space=pl.ANY)
     vmem = pl.BlockSpec(memory_space=pltpu.VMEM)
     shape = jax.ShapeDtypeStruct
@@ -496,195 +493,379 @@
     return pl.pallas_call(
         functools.partial(collect_kernel, depth),
         in_specs=[any_space, any_space],
-        out_specs=[vmem, vmem, vmem, any_space],
-        out_shape=[shape((toks, dim), BF16), shape((toks, dim), BF16), shape((height, ff), F32), shape((4, height, ff), F32)],
+        out_specs=[vmem, vmem, any_space],
+        out_shape=[shape((toks, dim), BF16), shape((height, ff), F32), shape((4, height, ff), F32)],
         scratch_shapes=[
-            pltpu.VMEM((2, depth + 1, toks, dim), F32),
+            pltpu.VMEM((depth + 1, toks, dim), F32),
             pltpu.VMEM((2 * n_part, *message), F32), pltpu.VMEM((2 * n_part, *message), F32),
             pltpu.VMEM((n_part, *message), F32), pltpu.VMEM((n_part, *message), F32),
-            pltpu.VMEM((2, toks, dim), F32),
+            pltpu.VMEM((toks, dim), F32),
             pltpu.VMEM((RING, 2, *message), F32), pltpu.VMEM((RING, 2, *message), F32),
             pltpu.VMEM((2, 2, 2, *message), F32), pltpu.VMEM((2, 2, BAND, dim), F32),
-            dma((2,)), dma((RING, 2)), dma((RING, 2)), dma((2, 2, 2)), dma((2, 2)),
+            dma, dma((RING, 2)), dma((RING, 2)), dma((2, 2, 2)), dma((2, 2)),
             dma((2, n_col)), dma((2, n_col)), dma((3 * n_part,)), dma((3 * n_part,)), dma((3 * n_part,)), dma((3 * n_part,)),
             dma((4, height // CHUNK // 4)), dma((4, height // CHUNK // 4)),
         ],
         compiler_params=pltpu.CompilerParams(collective_id=1, has_side_effects=True, vmem_limit_bytes=66_000_000),
         name="collect",
-    )(yd, grads)[:3]
-
-
-def expert_kernel(
-    n_tiles, n_exp, count_ref, place_ref, rank_ref, gate_ref, x_ref, dy_ref, wg_ref, wu_ref, wd_ref,
-    yd_ref, dw_ref, x_rows, g_rows, o_win, d_win, cum_ref, off_ref,
+    )(dx_part, grads)[:2]
+
+
+def count_up(n_tiles, n_exp, count_ref, cum_ref, off_ref, blk_ref):
+    base = jnp.int32(0)
+    block = jnp.int32(0)
+    for exp in range(n_exp):
+        run = jnp.int32(0)
+        cum_ref[exp] = run
+        for tile in range(n_tiles):
+            run += count_ref[tile * n_exp + exp]
+            cum_ref[(tile + 1) * n_exp + exp] = run
+        off_ref[exp] = base
+        blk_ref[exp] = block
+        big, rest = blocks_of(run)
+        block += big + rest
+        base += jnp.maximum(big * ROWS + rest * (ROWS // 2), (run + ALIGN - 1) // ALIGN * ALIGN + WIN)
+    blk_ref[n_exp] = block
+
+
+def blocks_of(count):
+    big = (count + ROWS // 2 - 1) // ROWS
+    return big, (count > big * ROWS).astype(jnp.int32)
+
+
+def span(n_exp, cum_ref, tile, exp):
+    lo = cum_ref[tile * n_exp + exp]
+    hi = cum_ref[(tile + 1) * n_exp + exp]
+    return lo, hi, (lo // ALIGN) * ALIGN
+
+
+def pick(ref, exp, cols, lo, start):
+    place = lax.broadcasted_iota(jnp.int32, (WIN, TILE), 0).astype(F32) + (start - lo).astype(F32)
+    return ref[0, exp : exp + 1, cols] == place
+
+
+def gather_tile(n_exp, cum_ref, off_ref, rank_ref, gate_ref, tile, cols, toks, rows_ref):
+    def window(exp, lo, start):
+        hit = pick(rank_ref, exp, cols, lo, start)
+        value = 1.0 if gate_ref is None else gate_ref[0, exp : exp + 1, cols]
+        take = jnp.where(hit, value, 0.0).astype(BF16)
+        return dot(take, toks[...]).astype(BF16)
+
+    def rows_at(exp, start, size):
+        return pl.ds(pl.multiple_of(off_ref[exp] + start, ALIGN), size)
+
+    spans = [span(n_exp, cum_ref, tile, exp) for exp in range(n_exp)]
+    for exp, (lo, hi, start) in enumerate(spans):
+        value = window(exp, lo, start)
+        head = rows_at(exp, start, ALIGN)
+        fresh = lax.broadcasted_iota(jnp.int32, (ALIGN, 1), 0) + start >= lo
+        rows_ref[head, :] = jnp.where(fresh, value[:ALIGN], rows_ref[head, :])
+        rows_ref[rows_at(exp, start + ALIGN, WIN - ALIGN), :] = value[ALIGN:]
+    most = functools.reduce(jnp.maximum, [hi - start for lo, hi, start in spans])
+
+    @pl.when(most > WIN)
+    def _more():
+        for exp, (lo, hi, start) in enumerate(spans):
+            @pl.loop(1, (hi - start + WIN - 1) // WIN)
+            def _(w):
+                rows_ref[rows_at(exp, start + w * WIN, WIN), :] = window(exp, lo, start + w * WIN)
+
+
+def scatter_tile(n_exp, cum_ref, off_ref, rank_ref, gate_ref, tile, cols, rows_ref, win_ref, out_ref):
+    def window(exp, lo, start):
+        hit = pick(rank_ref, exp, cols, lo, start)
+        value = 1.0 if gate_ref is None else gate_ref[0, exp : exp + 1, cols]
+        put = jnp.where(hit, value, 0.0).astype(BF16)
+        return put, rows_ref[pl.ds(pl.multiple_of(off_ref[exp] + start, ALIGN), WIN), :]
+
+    spans = [span(n_exp, cum_ref, tile, exp) for exp in range(n_exp)]
+    puts = []
+    for exp, (lo, hi, start) in enumerate(spans):
+        put, block = window(exp, lo, start)
+        puts.append(put)
+        win_ref[exp * WIN : (exp + 1) * WIN, :] = block
+    out_ref[cols, :] = dot(jnp.concatenate(puts, axis=0), win_ref[...], ((0,), (0,)))
+    most = functools.reduce(jnp.maximum, [hi - start for lo, hi, start in spans])
+
+    @pl.when(most > WIN)
+    def _more():
+        for exp, (lo, hi, start) in enumerate(spans):
+            @pl.loop(1, (hi - start + WIN - 1) // WIN)
+            def _(w):
+                put, block = window(exp, lo, start + w * WIN)
+                out_ref[cols, :] += dot(put, block, ((0,), (0,)))
+
+
+def forward_kernel(
+    depth, n_tiles, n_exp, count_ref, z_ref, rank_ref, gate_ref, x_ref, wg_ref, wu_ref, wd_ref,
+    *refs,
 ):
+    y_refs, (xs_ref, uv_ref, rows_ref, win_ref, x_out, uv_out, cum_ref, off_ref, blk_ref, x_sem, uv_sem) = refs[:depth], refs[depth:]
     step = pl.program_id(0)
+    per = n_tiles // depth
 
     @pl.when(step == 0)
-    def _count():
-        base = jnp.int32(0)
-        for exp in range(n_exp):
-            run = jnp.int32(0)
-            cum_ref[exp] = run
-            for tile in range(n_tiles):
-                run += count_ref[tile * n_exp + exp]
-                cum_ref[(tile + 1) * n_exp + exp] = run
-            off_ref[exp] = base
-            base += ((run + ALIGN - 1) // ALIGN) * ALIGN
-
-    def span(tile, exp):
-        lo = cum_ref[tile * n_exp + exp]
-        hi = cum_ref[(tile + 1) * n_exp + exp]
-        start = (lo // ALIGN) * ALIGN
-        return lo, hi, start
-
-    @pl.when(step < n_tiles)
-    def _gather():
-        tile = step
-
-        def window(exp, lo, hi, start):
-            first = (start - lo).astype(F32)
-            place = lax.broadcasted_iota(jnp.int32, (WIN, TILE), 0).astype(F32) + first
-            hit = rank_ref[0, exp : exp + 1, :] == place
-            take = jnp.where(hit, 1.0, 0.0).astype(BF16)
-            scale = jnp.where(hit, gate_ref[0, exp : exp + 1, :], 0.0).astype(BF16)
-            row = lax.broadcasted_iota(jnp.int32, (WIN, 1), 0) + start
-            mine = (row >= lo) & (row < hi)
-            here = pl.ds(pl.multiple_of(off_ref[exp] + start, ALIGN), WIN)
-            x_rows[here, :] = jnp.where(mine, dot(take, x_ref[...]), x_rows[here, :].astype(F32)).astype(BF16)
-            g_rows[here, :] = jnp.where(mine, dot(scale, dy_ref[...]), g_rows[here, :].astype(F32)).astype(BF16)
-
-        for exp in range(n_exp):
-            lo, hi, start = span(tile, exp)
-            window(exp, lo, hi, start)
-
-            @pl.when(hi > start + WIN)
-            def _more():
-                @pl.loop(1, (hi - start + WIN - 1) // WIN)
-                def _(w):
-                    window(exp, lo, hi, start + w * WIN)
-
-    @pl.when((step >= n_tiles) & (step < n_tiles + n_exp))
-    def _expert():
-        exp = step - n_tiles
+    def _():
+        count_up(n_tiles, n_exp, count_ref, cum_ref, off_ref, blk_ref)
+
+    @pl.when(step < depth)
+    def _():
+        for i in range(per):
+            cols = slice(i * TILE, (i + 1) * TILE)
+            gather_tile(n_exp, cum_ref, off_ref, rank_ref, None, step * per + i, cols, x_ref.at[cols, :], rows_ref)
+
+    def saves(block):
+        side = block % 2
+        return (
+            pltpu.make_async_copy(x_out.at[side], xs_ref.at[block], x_sem.at[side]),
+            pltpu.make_async_copy(uv_out.at[side], uv_ref.at[block], uv_sem.at[side]),
+        )
+
+    @pl.when((step >= depth) & (step < depth + n_exp))
+    def _():
+        exp = step - depth
         count = cum_ref[n_tiles * n_exp + exp]
-        base = off_ref[exp]
-        dw_ref[...] = jnp.zeros_like(dw_ref)
+        big, rest = blocks_of(count)
+
+        def run(b, size):
+            block = blk_ref[exp] + b
+            side = block % 2
+
+            @pl.when(block >= 2)
+            def _():
+                for copy in saves(block - 2):
+                    copy.wait()
+
+            here = pl.ds(pl.multiple_of(off_ref[exp] + b * ROWS, ALIGN), size)
+            live = lax.broadcasted_iota(jnp.int32, (size, 1), 0) < count - b * ROWS
+            x_old = rows_ref[here, :]
+            x_out[side, :size] = jnp.where(live, x_old, jnp.zeros_like(x_old))
+            u = dot(x_out[side, :size], wg_ref[0])
+            v = dot(x_out[side, :size], wu_ref[0])
+            uv_out[side, 0, :size] = u
+            uv_out[side, 1, :size] = v
+            act = (u * jax.nn.sigmoid(u) * v).astype(BF16)
+            rows_ref[here, :] = dot(act, wd_ref[0]).astype(BF16)
+            for copy in saves(block):
+                copy.start()
+
+        @pl.loop(0, big)
+        def _(b):
+            run(b, ROWS)
+
+        @pl.when(rest > 0)
+        def _():
+            run(big, ROWS // 2)
+
+    @pl.when(step == depth + n_exp)
+    def _():
+        total = blk_ref[n_exp]
+        for back in (2, 1):
+            @pl.when(total >= back)
+            def _():
+                for copy in saves(total - back):
+                    copy.wait()
+
+    for d in range(depth):
+        @pl.when(step == depth + n_exp + d)
+        def _():
+            for i in range(per):
+                tile = ((z_ref[0] + d) % depth) * per + i
+                cols = slice(i * TILE, (i + 1) * TILE)
+                scatter_tile(n_exp, cum_ref, off_ref, rank_ref, gate_ref, tile, cols, rows_ref, win_ref, y_refs[d])
+
+
+def backward_kernel(
+    depth, n_tiles, n_exp, count_ref, z_ref, rank_ref, gate_ref, head_ref, *refs,
+):
+    tails, refs = refs[:depth], refs[depth:]
+    wg_ref, wu_ref, wd_ref, xs_ref, uv_ref, dx_ref, dw_ref = refs[:7]
+    rows_ref, win_ref, x_in, uv_in, tail_ref, cum_ref, off_ref, blk_ref, x_sem, uv_sem = refs[7:]
+    step = pl.program_id(0)
+    per = n_tiles // depth
+
+    @pl.when(step == 0)
+    def _():
+        count_up(n_tiles, n_exp, count_ref, cum_ref, off_ref, blk_ref)
+
+    @pl.when(step < depth)
+    def _():
+        for d in range(depth):
+            @pl.when((z_ref[0] + depth - step) % depth == d)
+            def _():
+                tail_ref[...] = tails[d][...]
+
+        split = head_ref.shape[0]
+        for i in range(per):
+            cols = slice(i * TILE, (i + 1) * TILE)
+            toks = head_ref.at[cols, :] if i * TILE < split else tail_ref.at[slice(i * TILE - split, (i + 1) * TILE - split), :]
+            gather_tile(n_exp, cum_ref, off_ref, rank_ref, gate_ref, step * per + i, cols, toks, rows_ref)
+
+    def loads(block):
+        side = block % 2
+        return (
+            pltpu.make_async_copy(xs_ref.at[block], x_in.at[side], x_sem.at[side]),
+            pltpu.make_async_copy(uv_ref.at[block], uv_in.at[side], uv_sem.at[side]),
+        )
+
+    @pl.when((step == depth - 1) & (blk_ref[n_exp] > 0))
+    def _():
+        for copy in loads(0):
+            copy.start()
+
+    @pl.when((step >= depth) & (step < depth + n_exp))
+    def _():
+        exp = step - depth
+        count = cum_ref[n_tiles * n_exp + exp]
+        big, rest = blocks_of(count)
         dim, ff = wg_ref.shape[1:]
 
-        @pl.loop(0, (count + ROWS - 1) // ROWS)
-        def _(b):
-            here = pl.ds(pl.multiple_of(base + b * ROWS, ALIGN), ROWS)
-            live = lax.broadcasted_iota(jnp.int32, (ROWS, 1), 0) < count - b * ROWS
-            x_old = x_rows[here, :]
-            g_old = g_rows[here, :]
-            x_blk = jnp.where(live, x_old, jnp.zeros_like(x_old))
+        @pl.when(count == 0)
+        def _():
+            dw_ref[...] = jnp.zeros_like(dw_ref)
+
+        def run(b, size):
+            block = blk_ref[exp] + b
+            side = block % 2
+
+            @pl.when(block + 1 < blk_ref[n_exp])
+            def _():
+                for copy in loads(block + 1):
+                    copy.start()
+
+            def add(at, value):
+                dw_ref[0, at, :] = jnp.where(b == 0, 0.0, dw_ref[0, at, :]) + value
+
+            here = pl.ds(pl.multiple_of(off_ref[exp] + b * ROWS, ALIGN), size)
+            live = lax.broadcasted_iota(jnp.int32, (size, 1), 0) < count - b * ROWS
+            g_old = rows_ref[here, :]
             g_blk = jnp.where(live, g_old, jnp.zeros_like(g_old))
-            u = dot(x_blk, wg_ref[0])
-            v = dot(x_blk, wu_ref[0])
+            da = dot(g_blk, wd_ref[0], ((1,), (1,)))
+            for copy in loads(block):
+                copy.wait()
+            u = uv_in[side, 0, :size]
+            v = uv_in[side, 1, :size]
             s = jax.nn.sigmoid(u)
             act = (u * s * v).astype(BF16)
-            da = dot(g_blk, wd_ref[0], ((1,), (1,)))
             du = (da * v * s * (1.0 + u * (1.0 - s))).astype(BF16)
             dv = (da * u * s).astype(BF16)
-            out = dot(act, wd_ref[0]).astype(BF16)
-            dxr = (dot(du, wg_ref[0], ((1,), (1,))) + dot(dv, wu_ref[0], ((1,), (1,)))).astype(BF16)
-            dw_ref[0, 2 * dim : 2 * dim + ff] += dot(act, g_blk[:, :ff], ((0,), (0,)))
-            dw_ref[0, 2 * dim + ff :] += dot(act, g_blk[:, ff:], ((0,), (0,)))
-            g_rows[here, :] = jnp.where(live, dxr, g_rows[here, :])
-            dw_ref[0, :dim] += dot(x_blk, du, ((0,), (0,)))
-            dw_ref[0, dim : 2 * dim] += dot(x_blk, dv, ((0,), (0,)))
-            x_rows[here, :] = jnp.where(live, out, x_rows[here, :])
-
-    @pl.when(step >= n_tiles + n_exp)
-    def _scatter():
-        tile = step - n_tiles - n_exp
-
-        def window(exp, lo, hi, start):
-            first = (start - lo).astype(F32)
-            place = lax.broadcasted_iota(jnp.int32, (WIN, TILE), 0).astype(F32) + first
-            hit = rank_ref[0, exp : exp + 1, :] == place
-            put = jnp.where(hit, 1.0, 0.0).astype(BF16)
-            scale = jnp.where(hit, gate_ref[0, exp : exp + 1, :], 0.0).astype(BF16)
-            row = lax.broadcasted_iota(jnp.int32, (WIN, 1), 0) + start
-            mine = (row >= lo) & (row < hi)
-            here = pl.ds(pl.multiple_of(off_ref[exp] + start, ALIGN), WIN)
-            o_blk = x_rows[here, :]
-            d_blk = g_rows[here, :]
-            o_blk = jnp.where(mine, o_blk, jnp.zeros_like(o_blk))
-            d_blk = jnp.where(mine, d_blk, jnp.zeros_like(d_blk))
-            return put, scale, o_blk, d_blk
-
-        for part in range(n_exp // GROUP):
-            puts, scales = [], []
-            for i in range(GROUP):
-                exp = part * GROUP + i
-                lo, hi, start = span(tile, exp)
-                put, scale, o_blk, d_blk = window(exp, lo, hi, start)
-                puts.append(put)
-                scales.append(scale)
-                o_win[i * WIN : (i + 1) * WIN, :] = o_blk
-                d_win[i * WIN : (i + 1) * WIN, :] = d_blk
-            y_add = dot(jnp.concatenate(scales, axis=0), o_win[...], ((0,), (0,)))
-            dx_add = dot(jnp.concatenate(puts, axis=0), d_win[...], ((0,), (0,)))
-            yd_ref[0] = y_add if part == 0 else yd_ref[0] + y_add
-            yd_ref[1] = dx_add if part == 0 else yd_ref[1] + dx_add
-        for exp in range(n_exp):
-            lo, hi, start = span(tile, exp)
-
-            @pl.when(hi > start + WIN)
-            def _more():
-                @pl.loop(1, (hi - start + WIN - 1) // WIN)
-                def _(w):
-                    put, scale, o_blk, d_blk = window(exp, lo, hi, start + w * WIN)
-                    yd_ref[0] += dot(scale, o_blk, ((0,), (0,)))
-                    yd_ref[1] += dot(put, d_blk, ((0,), (0,)))
-
-
-def expert_layer(counts, place, plan_col, x_col, dy_col, w_gate, w_up, w_down, cap, n_dev):
-    tokens, dim = x_col.shape
-    n_exp, _, ff = w_gate.shape
+            add(slice(2 * dim, 2 * dim + ff), dot(act, g_blk[:, :ff], ((0,), (0,))))
+            add(slice(2 * dim + ff, 3 * dim), dot(act, g_blk[:, ff:], ((0,), (0,))))
+            dxr = dot(du, wg_ref[0], ((1,), (1,))) + dot(dv, wu_ref[0], ((1,), (1,)))
+            rows_ref[here, :] = dxr.astype(BF16)
+            add(slice(0, dim), dot(x_in[side, :size], du, ((0,), (0,))))
+            add(slice(dim, 2 * dim), dot(x_in[side, :size], dv, ((0,), (0,))))
+
+        @pl.loop(0, big)
+        def _(b):
+            run(b, ROWS)
+
+        @pl.when(rest > 0)
+        def _():
+            run(big, ROWS // 2)
+
+    @pl.when(step >= depth + n_exp)
+    def _():
+        for i in range(per):
+            tile = (step - depth - n_exp) * per + i
+            cols = slice(i * TILE, (i + 1) * TILE)
+            scatter_tile(n_exp, cum_ref, off_ref, rank_ref, None, tile, cols, rows_ref, win_ref, dx_ref)
+
+
+def layer_sizes(depth, toks, w_gate, cap):
+    tokens = depth * toks
+    n_exp = w_gate.shape[0]
     n_tiles = tokens // TILE
-    total = n_exp * (-(-cap // ALIGN) * ALIGN) + ROWS
-    per = plan_col.shape[2] // TILE
-    first = lambda i: jnp.minimum(i, n_tiles - 1)
-    middle = lambda i: jnp.clip(i - n_tiles, 0, n_exp - 1)
-    last = lambda i: jnp.maximum(i - n_tiles - n_exp, 0)
-    tile_of = lambda i: jnp.where(i < n_tiles, i, last(i))
-    plan_at = lambda part: lambda i, counts, place: (tile_of(i) // per, place[0] + part, tile_of(i) % per)
-    ranks = pl.BlockSpec((1, n_exp, TILE), plan_at(0))
-    gates = pl.BlockSpec((1, n_exp, TILE), plan_at(n_dev // n_exp))
-    toks_in = pl.BlockSpec((TILE, dim), lambda i, *_: (first(i), 0))
-    toks_out = pl.BlockSpec((2, TILE, dim), lambda i, *_: (0, last(i), 0))
-    grads = pl.BlockSpec((1, 3 * dim, ff), lambda i, *_: (middle(i), 0, 0))
+    rows = n_exp * max(-(-cap // (ROWS // 2)) * (ROWS // 2), -(-cap // ALIGN) * ALIGN + WIN) + ROWS
+    return n_tiles, n_exp, rows, n_exp * -(-cap // ROWS)
+
+
+def expert_forward(depth, n_dev, counts, place, plan_col, x_col, w_gate, w_up, w_down, cap):
+    n_tiles, n_exp, rows, blocks = layer_sizes(depth, x_col.shape[1], w_gate, cap)
+    toks, dim = x_col.shape[1:]
+    ff = w_gate.shape[2]
+    first = lambda i: jnp.minimum(i, depth - 1)
+    middle = lambda i: jnp.clip(i - depth, 0, n_exp - 1)
+    last = lambda i: jnp.maximum(i - depth - n_exp, 0)
+
+    def plan_at(part):
+        return lambda i, counts, place: (jnp.where(i < depth, i, (place[0] + last(i)) % depth), place[0] + part, 0)
+
     wide = pl.BlockSpec((1, dim, ff), lambda i, *_: (middle(i), 0, 0))
     tall = pl.BlockSpec((1, ff, dim), lambda i, *_: (middle(i), 0, 0))
-    return pl.pallas_call(
-        functools.partial(expert_kernel, n_tiles, n_exp),
+    any_space = pl.BlockSpec(memory_space=pl.ANY)
+    outs = [pl.BlockSpec((toks, dim), lambda i, *_: (0, 0)) for d in range(depth)]
+    shape = jax.ShapeDtypeStruct
+    dma = pltpu.SemaphoreType.DMA
+    result = pl.pallas_call(
+        functools.partial(forward_kernel, depth, n_tiles, n_exp),
         grid_spec=pltpu.PrefetchScalarGridSpec(
             num_scalar_prefetch=2,
-            grid=(2 * n_tiles + n_exp,),
-            in_specs=[ranks, gates, toks_in, toks_in, wide, wide, tall],
-            out_specs=[toks_out, grads],
+            grid=(2 * depth + n_exp,),
+            in_specs=[
+                pl.BlockSpec((1, n_exp, toks), plan_at(0)), pl.BlockSpec((1, n_exp, toks), plan_at(n_dev // n_exp)),
+                pl.BlockSpec((toks, dim), lambda i, *_: (first(i), 0)), wide, wide, tall,
+            ],
+            out_specs=outs + [any_space, any_space],
             scratch_shapes=[
-                pltpu.VMEM((total, dim), BF16),
-                pltpu.VMEM((total, dim), BF16),
-                pltpu.VMEM((GROUP * WIN, dim), BF16),
-                pltpu.VMEM((GROUP * WIN, dim), BF16),
-                pltpu.SMEM(((n_tiles + 1) * n_exp,), jnp.int32),
-                pltpu.SMEM((n_exp,), jnp.int32),
+                pltpu.VMEM((rows, dim), BF16), pltpu.VMEM((n_exp * WIN, dim), BF16),
+                pltpu.VMEM((2, ROWS, dim), BF16), pltpu.VMEM((2, 2, ROWS, ff), F32),
+                pltpu.SMEM(((n_tiles + 1) * n_exp,), jnp.int32), pltpu.SMEM((n_exp,), jnp.int32),
+                pltpu.SMEM((n_exp + 1,), jnp.int32), dma((2,)), dma((2,)),
             ],
         ),
-        out_shape=[
-            jax.ShapeDtypeStruct((2, tokens, dim), F32),
-            jax.ShapeDtypeStruct((n_exp, 3 * dim, ff), F32),
-        ],
-        compiler_params=pltpu.CompilerParams(
-            dimension_semantics=("arbitrary",), vmem_limit_bytes=67_000_000,
+        out_shape=[shape((toks, dim), F32)] * depth + [shape((blocks, ROWS, dim), BF16), shape((blocks, 2, ROWS, ff), F32)],
+        compiler_params=pltpu.CompilerParams(dimension_semantics=("arbitrary",), vmem_limit_bytes=64_000_000),
+        cost_estimate=pl.CostEstimate(flops=25_000_000_000, bytes_accessed=80_000_000, transcendentals=3_000_000),
+        name="forward",
+    )(counts, place, plan_col, plan_col, x_col.reshape(-1, dim), w_gate, w_up, w_down)
+    return result[:depth], result[depth], result[depth + 1]
+
+
+def expert_backward(depth, n_dev, counts, place, plan_col, dy_head, dy_tails, w_gate, w_up, w_down, x_saved, uv_saved, cap):
+    n_tiles, n_exp, rows, blocks = layer_sizes(depth, plan_col.shape[2], w_gate, cap)
+    head, dim = dy_head.shape[1:]
+    tail = dy_tails[0].shape[0]
+    toks = head + tail
+    ff = w_gate.shape[2]
+    first = lambda i: jnp.minimum(i, depth - 1)
+    middle = lambda i: jnp.clip(i - depth, 0, n_exp - 1)
+    last = lambda i: jnp.maximum(i - depth - n_exp, 0)
+
+    def plan_at(part):
+        return lambda i, counts, place: (jnp.where(i < depth, i, last(i)), place[0] + part, 0)
+
+    wide = pl.BlockSpec((1, dim, ff), lambda i, *_: (middle(i), 0, 0))
+    tall = pl.BlockSpec((1, ff, dim), lambda i, *_: (middle(i), 0, 0))
+    any_space = pl.BlockSpec(memory_space=pl.ANY)
+    shape = jax.ShapeDtypeStruct
+    dma = pltpu.SemaphoreType.DMA
+    return pl.pallas_call(
+        functools.partial(backward_kernel, depth, n_tiles, n_exp),
+        grid_spec=pltpu.PrefetchScalarGridSpec(
+            num_scalar_prefetch=2,
+            grid=(2 * depth + n_exp,),
+            in_specs=[
+                pl.BlockSpec((1, n_exp, toks), plan_at(0)), pl.BlockSpec((1, n_exp, toks), plan_at(n_dev // n_exp)),
+                pl.BlockSpec((head, dim), lambda i, *_: (first(i), 0)),
+                *[pl.BlockSpec((tail, dim), lambda i, *_: (0, 0))] * depth, wide, wide, tall, any_space, any_space,
+            ],
+            out_specs=[
+                pl.BlockSpec((toks, dim), lambda i, *_: (last(i), 0)),
+                pl.BlockSpec((1, 3 * dim, ff), lambda i, *_: (middle(i), 0, 0)),
+            ],
+            scratch_shapes=[
+                pltpu.VMEM((rows, dim), BF16), pltpu.VMEM((n_exp * WIN, dim), BF16),
+                pltpu.VMEM((2, ROWS, dim), BF16), pltpu.VMEM((2, 2, ROWS, ff), F32), pltpu.VMEM((tail, dim), BF16),
+                pltpu.SMEM(((n_tiles + 1) * n_exp,), jnp.int32), pltpu.SMEM((n_exp,), jnp.int32),
+                pltpu.SMEM((n_exp + 1,), jnp.int32), dma((2,)), dma((2,)),
+            ],
         ),
-        cost_estimate=pl.CostEstimate(flops=60_000_000_000, bytes_accessed=120_000_000, transcendentals=3_000_000),
-        name="experts",
-    )(counts, place, plan_col, plan_col, x_col, dy_col, w_gate, w_up, w_down)
+        out_shape=[shape((depth * toks, dim), F32), shape((n_exp, 3 * dim, ff), F32)],
+        compiler_params=pltpu.CompilerParams(dimension_semantics=("arbitrary",), vmem_limit_bytes=66_000_000),
+        cost_estimate=pl.CostEstimate(flops=50_000_000_000, bytes_accessed=150_000_000, transcendentals=3_000_000),
+        name="backward",
+    )(counts, place, plan_col, plan_col, dy_head.reshape(-1, dim), *dy_tails, w_gate, w_up, w_down, x_saved, uv_saved)
 
 
 def solution(mesh):
@@ -698,17 +879,26 @@
         tok_loc, top_k = route_idx.shape
         cap = depth * (2 * tok_loc * top_k // (n_dev * w_gate.shape[0] - 2))
         n_exp = 8 * w_gate.shape[0]
-        x_col, dy_col, plan_col, wg_all, wu_all, wd_all = spread(
-            depth, n_dev, x_tok, dy_tok, route_idx.T, gates.T.astype(F32), w_gate, w_up, w_down
+        head = tok_loc // 2
+        x_col, dy_head, plan_col, wg_all, wu_all, wd_all = spread(
+            depth, n_dev, head, x_tok, dy_tok, route_idx.T, gates.T.astype(F32), w_gate, w_up, w_down
         )
+        turn = lambda a, d: lax.ppermute(a, 'z', [(i, (i + d) % depth) for i in range(depth)])
+        x_col, dy_tail = lax.optimization_barrier((x_col, dy_tok[head:]))
+        dy_tails = [dy_tail] + [turn(dy_tail, d) for d in range(1, depth)]
         place = lax.axis_index('z')
         per = tok_loc // TILE
         counts = lax.dynamic_slice(plan_col[:, 2 * n_dev : 2 * n_dev + per, :n_dev], (0, 0, place * n_exp), (depth, per, n_exp))
-        yd, grads = expert_layer(
-            counts.reshape(-1).astype(jnp.int32), place.reshape(1), plan_col, x_col.reshape(-1, x_tok.shape[1]),
-            dy_col.reshape(-1, x_tok.shape[1]), wg_all, wu_all, wd_all, cap, n_dev
+        where = (counts.reshape(-1).astype(jnp.int32), place.reshape(1), plan_col)
+        y_parts, x_saved, uv_saved = expert_forward(depth, n_dev, *where, x_col, wg_all, wu_all, wd_all, cap)
+        y_sum = y_parts[0]
+        turned = [turn(y_parts[d], d) for d in range(1, depth)]
+        dx_part, grads = expert_backward(
+            depth, n_dev, *where, dy_head, dy_tails, wg_all, wu_all, wd_all, x_saved, uv_saved, cap
         )
-        y, dx, dw = collect(depth, yd.reshape(2, depth, tok_loc, -1), grads)
+        dx, dw = collect(depth, dx_part.reshape(depth, tok_loc, -1), grads)
+        y_sum, turned, dx, dw = lax.optimization_barrier((y_sum, turned, dx, dw))
+        y = functools.reduce(jnp.add, turned, y_sum).astype(BF16)
         dim, ff = w_gate.shape[1:]
         g_down = jnp.concatenate([dw[2 * dim : 2 * dim + ff], dw[2 * dim + ff :]], axis=1)
         return y, dx, dw[None, :dim], dw[None, dim : 2 * dim], g_down[None]

time: 554 us -> 510 us (0.921)
  Pallas kernels: 531 us -> 475 us
  starting transfers between devices: 0 us -> 10.1 us
    pallas_call x1, Pallas kernels: 289 us -> 240 us  [collect(): pl.pallas_call(functools.partial(collect_kernel, depth), in_specs=[any_sp...]
    pallas_call x1, Pallas kernels: 151 us -> 121 us  [spread(): pl.pallas_call(functools.partial(spread_kernel, depth, experts), in_specs...]
    pallas_call x1 -> x2, Pallas kernels: 91.2 us -> 113 us  [the longest x1 61.8 us: expert_backward(): pl.pallas_call(functools.partial(backward_kernel, depth, n_tiles, n_exp),...]
    ppermute x0 -> x6, starting transfers between devices: none -> 10.1 us  [local_step(): lax.ppermute(a, 'z', [(i, (i + d) % depth) for i in range(depth)])]
  transfers between devices with their start and end apart: 0 -> 6, of which waited for: 0 -> 0; matrix products, arithmetic and copies ran while one was open for 0% -> 0% of each run, Pallas kernels for 0% -> 70%
where the time goes in v4:
time: 510 us; the launch traced here: 506 us
  Pallas kernels  475 us (93%)
  local copies, waits for them, and re-layouts  12.3 us (2%)
  starting transfers between devices  10.1 us (2%)
  other arithmetic  7.65 us (2%)
    pallas_call x1, Pallas kernels, collect(): pl.pallas_call(functools.partial(collect_kernel, depth), in_specs=[any_sp...  240 us
    pallas_call x1, Pallas kernels, spread(): pl.pallas_call(functools.partial(spread_kernel, depth, experts), in_specs...  121 us
    pallas_call x1, Pallas kernels, expert_backward(): pl.pallas_call(functools.partial(backward_kernel, depth, n_tiles, n_exp),...  61.8 us
    pallas_call x1, Pallas kernels, expert_forward(): pl.pallas_call(functools.partial(forward_kernel, depth, n_tiles, n_exp),...  51.7 us
  transfers between devices with their start and end apart: 6, of which 0 were waited for; matrix products, arithmetic and copies ran while one was open for 0% of the time, Pallas kernels for 70%

profile of v4, /device:TPU:0, one launch (start us, length us, event | category | flops | bytes accessed | tf_op | source)
XLA Modules:
  0.0 505.8 jit_solution(14987121824530231919)
XLA Ops:
  0.6 1.3 convert_bitcast_fusion.gate_ref
  1.9 1.1 slice.19.refs_0_
  3.0 0.0 copy-start.2
  3.0 121.1 %spread.1 = (bf16[4,512,1024]{2,1,0:T(8,128)(2,1)}, bf16[4,256,1024]{2,1,0:T(8,128)(2,1)}, f32[4,72,512]{2,1,0:T(8,128)}, bf16[8,1024,512]{2,1,0:T(8,128)(2,1)},...) custom-call(bf16[512,1024]{1,0:T(8,128)(2,1)} %x_ref.1, bf16[512,1024]{1,0:T(8,128)(2,1)} %dy_ref.1, ...), custom_call_target="tpu_custom_call" | custom-call | tf_op jit(solution)/shard_map/spread/pallas_call | solution.py:236
  124.1 2.5 collective-permute-start.5
  126.7 0.0 collective-permute-start.4
  126.7 0.0 copy-done.2
  126.7 0.6 collective-permute-start.3
  127.3 0.7 slice.18
  128.0 0.1 dynamic-slice_convert_fusion
  128.1 0.7 convert_element_type.16.count_ref
  128.8 51.7 %forward.1 = (f32[512,1024]{1,0:T(8,128)}, f32[512,1024]{1,0:T(8,128)}, f32[512,1024]{1,0:T(8,128)}, f32[512,1024]{1,0:T(8,128)}, bf16[24,512,1024]{2,1,0:T(8,128)(2,1)}, /*index=5*/f32[24,2,512,512]{3,2,1,0:T(8,128)}) custom-call(s32[64]{0:T(128)} %convert_element_type.16.count_ref, s32[1]{0:T(128)} %bitcast.2.z_ref, ...), custom_call_target="tpu_custom_call" | custom-call | flops 24999999488 | bytes 80000000 | tf_op jit(solution)/shard_map/forward/pallas_call | solution.py:800
  180.4 2.1 collective-permute-start
  182.6 4.8 collective-permute-start.1
  187.4 0.0 collective-permute-done.5.refs_3_
  187.4 0.0 collective-permute-start.2
  187.4 0.0 collective-permute-done.4.refs_2_
  187.4 0.0 collective-permute-done.3.refs_1_
  187.4 0.8 copy-done.4
  188.3 0.8 copy-done.5
  189.1 61.8 %backward.1 = (f32[2048,1024]{1,0:T(8,128)}, f32[8,3072,512]{2,1,0:T(8,128)}) custom-call(s32[64]{0:T(128)} %convert_element_type.16.count_ref, s32[1]{0:T(128)} %bitcast.2.z_ref, f32[4,72,512]{2,1,0:T(8,128)} %get-tuple-element.29.rank_ref.gate_ref, f32[4,72,512]{2,1,0:T(8,128)} %get-tuple-element.29.rank_ref.gate_ref, bf16[1024,1024]{1,0:T(8,128)(2,1)} %bitcast.16, ...), custom_call_target="tpu_custom_call" | custom-call | flops 49999998976 | bytes 150000000 | tf_op jit(solution)/shard_map/backward/pallas_call | solution.py:843
  250.8 240.2 %collect.1 = (bf16[512,1024]{1,0:T(8,128)(2,1)}, f32[3072,512]{1,0:T(8,128)}, f32[4,3072,512]{2,1,0:T(8,128)}) custom-call(f32[4,512,1024]{2,1,0:T(8,128)} %bitcast.13, f32[8,3072,512]{2,1,0:T(8,128)} %get-tuple-element.44.g_ref), custom_call_target="tpu_custom_call" | custom-call | tf_op jit(solution)/shard_map/collect/pallas_call | solution.py:493
  491.0 0.0 collective-permute-done
  491.0 0.0 collective-permute-done.1
  491.0 0.0 collective-permute-done.2
  491.0 1.7 fusion
  492.8 4.7 slice_bitcast_fusion
  497.4 1.5 maximum_bitcast_fusion
  498.9 0.8 copy-done
  499.8 4.8 add_convert_fusion
  504.5 0.0 copy-done.1
  504.5 1.0 copy.13
  (6 shorter events, 0.0 us)
Async XLA Ops:
  3.0 123.6 %copy-start.2 = (bf16[256,1024]{1,0:T(8,128)(2,1)}, bf16[256,1024]{1,0:T(8,128)(2,1)S(1)}, u32[]{:S(2)}) copy-start(bf16[256,1024]{1,0:T(8,128)(2,1)S(1)} %slice.19.refs_0_) | copy-start | bytes 1572868
  124.1 63.3 %collective-permute-start.5 = (bf16[256,1024]{1,0:T(8,128)(2,1)S(1)}, bf16[256,1024]{1,0:T(8,128)(2,1)S(1)}, u32[]{:S(2)}, u32[]{:S(2)}) collective-permute-start(bf16[256,1024]{1,0:T(8,128)(2,1)S(1)} %slice.19.refs_0_), channel_id=1, source_target_pairs={{0,24},{8,0},{16,8},{24,16},{1,25},{9,1},{17,9},{25,17},{2,26},{10... | collective-permute-start | bytes 1572872 | tf_op jit(solution)/shard_map/ppermute | solution.py:886
  126.7 60.7 %collective-permute-start.4 = (bf16[256,1024]{1,0:T(8,128)(2,1)S(1)}, bf16[256,1024]{1,0:T(8,128)(2,1)S(1)}, u32[]{:S(2)}, u32[]{:S(2)}) collective-permute-start(bf16[256,1024]{1,0:T(8,128)(2,1)S(1)} %slice.19.refs_0_), channel_id=1, source_target_pairs={{0,16},{8,24},{16,0},{24,8},{1,17},{9,25},{17,1},{25,9},{2,18},{10... | collective-permute-start | bytes 1572872 | tf_op jit(solution)/shard_map/ppermute | solution.py:886
  126.7 60.8 %collective-permute-start.3 = (bf16[256,1024]{1,0:T(8,128)(2,1)S(1)}, bf16[256,1024]{1,0:T(8,128)(2,1)S(1)}, u32[]{:S(2)}, u32[]{:S(2)}) collective-permute-start(bf16[256,1024]{1,0:T(8,128)(2,1)S(1)} %slice.19.refs_0_), channel_id=1, source_target_pairs={{0,8},{8,16},{16,24},{24,0},{1,9},{9,17},{17,25},{25,1},{2,10},{10... | collective-permute-start | bytes 1572872 | tf_op jit(solution)/shard_map/ppermute | solution.py:886
  180.4 310.6 %collective-permute-start = (f32[512,1024]{1,0:T(8,128)}, f32[512,1024]{1,0:T(8,128)}, u32[]{:S(2)}, u32[]{:S(2)}) collective-permute-start(f32[512,1024]{1,0:T(8,128)} %get-tuple-element.36), channel_id=1, source_target_pairs={{0,8},{8,16},{16,24},{24,0},{1,9},{9,17},{17,25},{25,1},{2,10},{10... | collective-permute-start | bytes 6291464 | tf_op jit(solution)/shard_map/ppermute | solution.py:886
  182.6 308.4 %collective-permute-start.1 = (f32[512,1024]{1,0:T(8,128)}, f32[512,1024]{1,0:T(8,128)}, u32[]{:S(2)}, u32[]{:S(2)}) collective-permute-start(f32[512,1024]{1,0:T(8,128)} %get-tuple-element.37), channel_id=1, source_target_pairs={{0,16},{8,24},{16,0},{24,8},{1,17},{9,25},{17,1},{25,9},{2,18},{10... | collective-permute-start | bytes 6291464 | tf_op jit(solution)/shard_map/ppermute | solution.py:886
  187.4 1.7 copy-start.3
  187.4 303.6 %collective-permute-start.2 = (f32[512,1024]{1,0:T(8,128)}, f32[512,1024]{1,0:T(8,128)}, u32[]{:S(2)}, u32[]{:S(2)}) collective-permute-start(f32[512,1024]{1,0:T(8,128)} %get-tuple-element.38), channel_id=1, source_target_pairs={{0,24},{8,0},{16,8},{24,16},{1,25},{9,1},{17,9},{25,17},{2,26},{10... | collective-permute-start | bytes 6291464 | tf_op jit(solution)/shard_map/ppermute | solution.py:886
  187.4 0.9 copy-start.4
  188.3 0.8 copy-start.5
  497.4 2.3 copy-start
  499.8 4.8 copy-start.1

commit v5 on v4

--- a/solution.py
+++ b/solution.py
@@ -55,10 +55,10 @@
 def make_plan(experts, route_ref, gate_ref, plan):
     top_k, toks = route_ref.shape
     route = route_ref[...]
-    gates = gate_ref[...]
+    gates = gate_ref[...].astype(F32)
     below = lax.broadcasted_iota(jnp.int32, (TILE, TILE), 0) < lax.broadcasted_iota(jnp.int32, (TILE, TILE), 1)
     below = jnp.where(below, 1.0, 0.0).astype(BF16)
-    ones = jnp.ones((8, TILE), BF16)
+    ones = jnp.ones((16, TILE), BF16)
     ids = lax.broadcasted_iota(jnp.int32, (experts, toks), 0)
     member = jnp.zeros((experts, toks), F32)
     gate = jnp.zeros((experts, toks), F32)
@@ -66,19 +66,24 @@
         hit = jnp.broadcast_to(route[k : k + 1, :], (experts, toks)) == ids
         member = jnp.where(hit, 1.0, member)
         gate = jnp.where(hit, jnp.broadcast_to(gates[k : k + 1, :], (experts, toks)), gate)
-    plan[experts : 2 * experts, :] = gate
-    plan[2 * experts :, :] = jnp.zeros((8, toks), F32)
+    ranks, counts = [], []
     for t in range(toks // TILE):
-        cols = slice(t * TILE, (t + 1) * TILE)
-        part = member[:, cols]
-        rank = dot(part.astype(BF16), below)
-        plan[:experts, cols] = jnp.where(part > 0.5, rank, -4096.0)
-        plan[2 * experts + t : 2 * experts + t + 1, :experts] = dot(ones, part.astype(BF16), ((1,), (1,)))[:1]
+        part = member[:, t * TILE : (t + 1) * TILE]
+        ranks.append(jnp.where(part > 0.5, dot(part.astype(BF16), below), -4096.0))
+        counts.append(dot(ones, part.astype(BF16), ((1,), (1,))))
+    rank = jnp.concatenate(ranks, axis=1)
+    for p in range(experts // 8):
+        both = jnp.concatenate([rank[8 * p : 8 * p + 8], gate[8 * p : 8 * p + 8]], axis=0)
+        plan[16 * p : 16 * p + 16, :] = both.astype(BF16)
+    which = lax.broadcasted_iota(jnp.int32, (16, experts), 0)
+    count = functools.reduce(jnp.add, [jnp.where(which == t, c, 0.0) for t, c in enumerate(counts)])
+    plan[2 * experts :, :] = jnp.zeros((16, toks), BF16)
+    plan[2 * experts :, :experts] = count.astype(BF16)
 
 
 def spread_kernel(
     depth, experts, x_ref, dy_ref, route_ref, gate_ref, wg_ref, wu_ref, wd_ref,
-    x_out, dy_out, plan_out, wg_out, wu_out, wd_out,
+    x_out, dy_out, tail_out, plan_out, wg_out, wu_out, wd_out,
     stage_t, stage_w, stage_d, plan, own_sem, z_send, z_recv, p_send, p_recv, c_send, c_recv,
 ):
     z, y, x, c = (lax.axis_index(a) for a in 'zyxc')
@@ -155,6 +160,7 @@
     copies = []
     for i, (src, buf, out) in enumerate((
         (x_ref, stage_t.at[0], x_out.at[z]), (dy_head, stage_t.at[1, pl.ds(0, dy_out.shape[1]), :], dy_out.at[z]),
+        (dy_ref.at[pl.ds(dy_out.shape[1], tail_out.shape[0]), :], stage_t.at[1, pl.ds(dy_out.shape[1], tail_out.shape[0]), :], tail_out),
         (wg_ref.at[0], stage_w.at[0], wg_out.at[own]), (wu_ref.at[0], stage_w.at[1], wu_out.at[own]),
         (wd_ref.at[0], stage_d, wd_out.at[own]),
     )):
@@ -175,7 +181,7 @@
     make_plan(experts, route_ref, gate_ref, plan)
     start_along(1, 0)
     start_along(2, 0)
-    copies.append((None, pltpu.make_async_copy(plan, plan_out.at[z], own_sem.at[5])))
+    copies.append((None, pltpu.make_async_copy(plan, plan_out.at[z], own_sem.at[6])))
     for i, (load, store) in enumerate(copies):
         if load is not None:
             load.wait()
@@ -189,6 +195,11 @@
     def relay_twin(part, h):
         landed(part, h, 1 - h)
         go(across(part, h, 1 - h))
+
+    def relay_far(part):
+        for h in range(2):
+            landed(part, h, 2)
+            go(across(part, h, 2))
 
     for part in range(2):
         relay(part, 0)
@@ -198,18 +209,20 @@
     relay(2, 0)
     relay(2, 1)
     await_along(2, 0)
-    for part in range(3):
+    for part in range(2):
         relay_twin(part, 1)
         relay_twin(part, 0)
     await_along(0, 1)
     await_along(1, 1)
-    for part in range(3):
-        for h in range(2):
-            landed(part, h, 2)
-            go(across(part, h, 2))
+    relay_twin(2, 1)
+    relay_twin(2, 0)
     await_along(2, 1)
-    for k in range(3):
-        await_along(k, 2)
+    relay_far(0)
+    relay_far(1)
+    await_along(0, 2)
+    await_along(1, 2)
+    relay_far(2)
+    await_along(2, 2)
     for part in range(3):
         for h in range(2):
             for kind in range(4):
@@ -230,20 +243,20 @@
     ff = w_down.shape[1]
     any_space = pl.BlockSpec(memory_space=pl.ANY)
     vmem = pl.BlockSpec(memory_space=pltpu.VMEM)
-    rows = 2 * experts + 8
+    rows = 2 * experts + 16
     shape = jax.ShapeDtypeStruct
     dma = pltpu.SemaphoreType.DMA
     return pl.pallas_call(
         functools.partial(spread_kernel, depth, experts),
         in_specs=[any_space, any_space, vmem, vmem, any_space, any_space, any_space],
-        out_specs=[any_space] * 6,
+        out_specs=[any_space] * 7,
         out_shape=[
-            shape((depth, toks, dim), BF16), shape((depth, head, dim), BF16), shape((depth, rows, toks), F32),
+            shape((depth, toks, dim), BF16), shape((depth, head, dim), BF16), shape((toks - head, dim), BF16), shape((depth, rows, toks), BF16),
             shape((8, dim, ff), BF16), shape((8, dim, ff), BF16), shape((8, ff, dim), BF16),
         ],
         scratch_shapes=[
             pltpu.VMEM((2, toks, dim), BF16), pltpu.VMEM((2, dim, ff), BF16), pltpu.VMEM((ff, dim), BF16),
-            pltpu.VMEM((rows, toks), F32), dma((6,)), dma((2, 3, depth)), dma((2, 3, depth)),
+            pltpu.VMEM((rows, toks), BF16), dma((7,)), dma((2, 3, depth)), dma((2, 3, depth)),
             dma((3, 3, 2)), dma((3, 3, 2)), dma((4, 3, 2)), dma((4, 3, 2)),
         ],
         compiler_params=pltpu.CompilerParams(collective_id=0, has_side_effects=True),
@@ -253,13 +266,13 @@
 
 CHUNK = 128
 BAND = 64
-LAG = 3
-DELAY = 18
+TURNS = (4, 14, 20, 22)
+FINISH = 3
 RING = 6
 
 
 def collect_kernel(
-    depth, dx_ref, g_ref, dx_out, g_out, twin,
+    depth, dx_ref, g_ref, dx_out, gate_out, up_out, down_out, twin,
     z_land, x_land, y_land, x_last, y_last, total, x_buf, y_buf, f_buf, z_buf,
     t_sem, x_load, y_load, f_load, z_load, z_send, z_recv, x_send, x_recv, y_send, y_recv, c_send, c_recv,
 ):
@@ -388,7 +401,15 @@
             landed(h, land.at[n_part + j], n_part + j)
             landed(1 - h, last.at[j], 2 * n_part + j)
             value = f_buf[h, j % 2, 0] + f_buf[h, j % 2, 1] + (land[n_part + j] + last[j])
-            g_out[rows(h * n_part + j), :] = value
+            chunk = h * n_part + j
+            tall = gate_out.shape[0] // CHUNK
+            places = ((0, tall, gate_out, 0), (tall, 2 * tall, up_out, 0), (2 * tall, 5 * tall // 2, down_out, 0), (5 * tall // 2, 3 * tall, down_out, 1))
+            for first, end, out, side in places:
+                if first < (h + 1) * n_part and end > h * n_part:
+                    @pl.when((chunk >= first) & (chunk < end))
+                    def _(first=first, out=out, side=side):
+                        cols = pl.ds(side * value.shape[1], value.shape[1])
+                        out[rows(chunk - first), cols] = value
 
     def column(side, k):
         role = z if side == 0 else depth - 1 - z
@@ -404,7 +425,7 @@
 
     def turn_of(side, t):
         role = z if side == 0 else depth - 1 - z
-        return t - DELAY - LAG * role
+        return t - functools.reduce(lambda late, r: jnp.where(role == r, TURNS[r], late), range(1, depth), TURNS[0])
 
     def column_prepare(side, t):
         k = turn_of(side, t)
@@ -444,11 +465,11 @@
         for side in range(2):
             link_prepare(side, t)
             column_prepare(side, t)
-            last_prepare(side, t - 2 * n_part - LAG)
+            last_prepare(side, t - 2 * n_part - FINISH)
 
     prepare(jnp.int32(0))
     own_total.wait()
-    steps = max(DELAY + n_col + LAG * (depth - 1), n_link + LAG)
+    steps = max(max(TURNS) + n_col, n_link + FINISH)
 
     @pl.loop(0, steps)
     def _(t):
@@ -458,7 +479,7 @@
         for side in range(2):
             column_turn(side, t)
         for side in range(2):
-            last_turn(side, t - 2 * n_part - LAG)
+            last_turn(side, t - 2 * n_part - FINISH)
 
     dx_out[...] = total[...].astype(BF16)
 
@@ -493,8 +514,8 @@
     return pl.pallas_call(
         functools.partial(collect_kernel, depth),
         in_specs=[any_space, any_space],
-        out_specs=[vmem, vmem, any_space],
-        out_shape=[shape((toks, dim), BF16), shape((height, ff), F32), shape((4, height, ff), F32)],
+        out_specs=[vmem, vmem, vmem, vmem, any_space],
+        out_shape=[pltpu.VMEM((toks, dim), BF16), pltpu.VMEM((dim, ff), F32), pltpu.VMEM((dim, ff), F32), pltpu.VMEM((ff, dim), F32), shape((4, height, ff), F32)],
         scratch_shapes=[
             pltpu.VMEM((depth + 1, toks, dim), F32),
             pltpu.VMEM((2 * n_part, *message), F32), pltpu.VMEM((2 * n_part, *message), F32),
@@ -506,9 +527,9 @@
             dma((2, n_col)), dma((2, n_col)), dma((3 * n_part,)), dma((3 * n_part,)), dma((3 * n_part,)), dma((3 * n_part,)),
             dma((4, height // CHUNK // 4)), dma((4, height // CHUNK // 4)),
         ],
-        compiler_params=pltpu.CompilerParams(collective_id=1, has_side_effects=True, vmem_limit_bytes=66_000_000),
+        compiler_params=pltpu.CompilerParams(collective_id=1, has_side_effects=True, vmem_limit_bytes=46_000_000),
         name="collect",
-    )(dx_part, grads)[:2]
+    )(dx_part, grads)[:4]
 
 
 def count_up(n_tiles, n_exp, count_ref, cum_ref, off_ref, blk_ref):
@@ -539,16 +560,13 @@
     return lo, hi, (lo // ALIGN) * ALIGN
 
 
-def pick(ref, exp, cols, lo, start):
-    place = lax.broadcasted_iota(jnp.int32, (WIN, TILE), 0).astype(F32) + (start - lo).astype(F32)
-    return ref[0, exp : exp + 1, cols] == place
-
-
-def gather_tile(n_exp, cum_ref, off_ref, rank_ref, gate_ref, tile, cols, toks, rows_ref):
+def gather_tile(n_exp, cum_ref, off_ref, plan, gated, tile, cols, toks, rows_ref):
+    rank, gate = plan[:n_exp, cols], plan[n_exp:, cols]
+    row = lax.broadcasted_iota(jnp.int32, (WIN, TILE), 0).astype(F32)
+
     def window(exp, lo, start):
-        hit = pick(rank_ref, exp, cols, lo, start)
-        value = 1.0 if gate_ref is None else gate_ref[0, exp : exp + 1, cols]
-        take = jnp.where(hit, value, 0.0).astype(BF16)
+        hit = rank[exp : exp + 1] == row + (start - lo).astype(F32)
+        take = jnp.where(hit, gate[exp : exp + 1] if gated else 1.0, 0.0).astype(BF16)
         return dot(take, toks[...]).astype(BF16)
 
     def rows_at(exp, start, size):
@@ -571,11 +589,12 @@
                 rows_ref[rows_at(exp, start + w * WIN, WIN), :] = window(exp, lo, start + w * WIN)
 
 
-def scatter_tile(n_exp, cum_ref, off_ref, rank_ref, gate_ref, tile, cols, rows_ref, win_ref, out_ref):
+def scatter_tile(n_exp, cum_ref, off_ref, plan_t, gated, tile, cols, rows_ref, win_ref, out_ref):
+    column = lax.broadcasted_iota(jnp.int32, (TILE, WIN), 1).astype(F32)
+
     def window(exp, lo, start):
-        hit = pick(rank_ref, exp, cols, lo, start)
-        value = 1.0 if gate_ref is None else gate_ref[0, exp : exp + 1, cols]
-        put = jnp.where(hit, value, 0.0).astype(BF16)
+        hit = plan_t[cols, exp : exp + 1] == column + (start - lo).astype(F32)
+        put = jnp.where(hit, plan_t[cols, n_exp + exp : n_exp + exp + 1] if gated else 1.0, 0.0).astype(BF16)
         return put, rows_ref[pl.ds(pl.multiple_of(off_ref[exp] + start, ALIGN), WIN), :]
 
     spans = [span(n_exp, cum_ref, tile, exp) for exp in range(n_exp)]
@@ -584,7 +603,7 @@
         put, block = window(exp, lo, start)
         puts.append(put)
         win_ref[exp * WIN : (exp + 1) * WIN, :] = block
-    out_ref[cols, :] = dot(jnp.concatenate(puts, axis=0), win_ref[...], ((0,), (0,)))
+    out_ref[cols, :] = dot(jnp.concatenate(puts, axis=1), win_ref[...])
     most = functools.reduce(jnp.maximum, [hi - start for lo, hi, start in spans])
 
     @pl.when(most > WIN)
@@ -593,14 +612,15 @@
             @pl.loop(1, (hi - start + WIN - 1) // WIN)
             def _(w):
                 put, block = window(exp, lo, start + w * WIN)
-                out_ref[cols, :] += dot(put, block, ((0,), (0,)))
+                out_ref[cols, :] += dot(put, block)
 
 
 def forward_kernel(
-    depth, n_tiles, n_exp, count_ref, z_ref, rank_ref, gate_ref, x_ref, wg_ref, wu_ref, wd_ref,
+    depth, n_tiles, n_exp, count_ref, z_ref, plan_ref, x_ref, wg_ref, wu_ref, wd_ref,
     *refs,
 ):
-    y_refs, (xs_ref, uv_ref, rows_ref, win_ref, x_out, uv_out, cum_ref, off_ref, blk_ref, x_sem, uv_sem) = refs[:depth], refs[depth:]
+    y_refs, refs = refs[:depth], refs[depth:]
+    xs_ref, uv_ref, rows_ref, win_ref, x_out, uv_out, y_buf, cum_ref, off_ref, blk_ref, x_sem, uv_sem, y_sem = refs
     step = pl.program_id(0)
     per = n_tiles // depth
 
@@ -610,9 +630,10 @@
 
     @pl.when(step < depth)
     def _():
+        plan = plan_ref[0].astype(F32)
         for i in range(per):
             cols = slice(i * TILE, (i + 1) * TILE)
-            gather_tile(n_exp, cum_ref, off_ref, rank_ref, None, step * per + i, cols, x_ref.at[cols, :], rows_ref)
+            gather_tile(n_exp, cum_ref, off_ref, plan, False, step * per + i, cols, x_ref.at[cols, :], rows_ref)
 
     def saves(block):
         side = block % 2
@@ -666,17 +687,36 @@
                 for copy in saves(total - back):
                     copy.wait()
 
-    for d in range(depth):
-        @pl.when(step == depth + n_exp + d)
-        def _():
-            for i in range(per):
-                tile = ((z_ref[0] + d) % depth) * per + i
-                cols = slice(i * TILE, (i + 1) * TILE)
-                scatter_tile(n_exp, cum_ref, off_ref, rank_ref, gate_ref, tile, cols, rows_ref, win_ref, y_refs[d])
+    d = step - depth - n_exp
+
+    def y_copy(d, k):
+        return pltpu.make_async_copy(y_buf.at[k % 2], y_refs[k], y_sem.at[k % 2])
+
+    @pl.when(d >= 0)
+    def _():
+        for k in range(2, depth):
+            @pl.when(d == k)
+            def _(k=k):
+                y_copy(d, k - 2).wait()
+
+        plan_t = jnp.transpose(plan_ref[0].astype(F32))
+        for i in range(per):
+            tile = ((z_ref[0] + d) % depth) * per + i
+            cols = slice(i * TILE, (i + 1) * TILE)
+            scatter_tile(n_exp, cum_ref, off_ref, plan_t, True, tile, cols, rows_ref, win_ref, y_buf.at[d % 2])
+        for k in range(depth):
+            @pl.when(d == k)
+            def _(k=k):
+                y_copy(d, k).start()
+
+    @pl.when(d == depth - 1)
+    def _():
+        y_copy(d, depth - 2).wait()
+        y_copy(d, depth - 1).wait()
 
 
 def backward_kernel(
-    depth, n_tiles, n_exp, count_ref, z_ref, rank_ref, gate_ref, head_ref, *refs,
+    depth, n_tiles, n_exp, count_ref, z_ref, plan_ref, head_ref, *refs,
 ):
     tails, refs = refs[:depth], refs[depth:]
     wg_ref, wu_ref, wd_ref, xs_ref, uv_ref, dx_ref, dw_ref = refs[:7]
@@ -695,11 +735,12 @@
             def _():
                 tail_ref[...] = tails[d][...]
 
+        plan = plan_ref[0].astype(F32)
         split = head_ref.shape[0]
         for i in range(per):
             cols = slice(i * TILE, (i + 1) * TILE)
             toks = head_ref.at[cols, :] if i * TILE < split else tail_ref.at[slice(i * TILE - split, (i + 1) * TILE - split), :]
-            gather_tile(n_exp, cum_ref, off_ref, rank_ref, gate_ref, step * per + i, cols, toks, rows_ref)
+            gather_tile(n_exp, cum_ref, off_ref, plan, True, step * per + i, cols, toks, rows_ref)
 
     def loads(block):
         side = block % 2
@@ -766,10 +807,11 @@
 
     @pl.when(step >= depth + n_exp)
     def _():
+        plan_t = jnp.transpose(plan_ref[0].astype(F32))
         for i in range(per):
             tile = (step - depth - n_exp) * per + i
             cols = slice(i * TILE, (i + 1) * TILE)
-            scatter_tile(n_exp, cum_ref, off_ref, rank_ref, None, tile, cols, rows_ref, win_ref, dx_ref)
+            scatter_tile(n_exp, cum_ref, off_ref, plan_t, False, tile, cols, rows_ref, win_ref, dx_ref)
 
 
 def layer_sizes(depth, toks, w_gate, cap):
@@ -780,7 +822,7 @@
     return n_tiles, n_exp, rows, n_exp * -(-cap // ROWS)
 
 
-def expert_forward(depth, n_dev, counts, place, plan_col, x_col, w_gate, w_up, w_down, cap):
+def expert_forward(depth, counts, place, plan_col, x_col, w_gate, w_up, w_down, cap):
     n_tiles, n_exp, rows, blocks = layer_sizes(depth, x_col.shape[1], w_gate, cap)
     toks, dim = x_col.shape[1:]
     ff = w_gate.shape[2]
@@ -788,13 +830,11 @@
     middle = lambda i: jnp.clip(i - depth, 0, n_exp - 1)
     last = lambda i: jnp.maximum(i - depth - n_exp, 0)
 
-    def plan_at(part):
-        return lambda i, counts, place: (jnp.where(i < depth, i, (place[0] + last(i)) % depth), place[0] + part, 0)
+    plan_at = lambda i, counts, place: (jnp.where(i < depth, i, (place[0] + last(i)) % depth), place[0], 0)
 
     wide = pl.BlockSpec((1, dim, ff), lambda i, *_: (middle(i), 0, 0))
     tall = pl.BlockSpec((1, ff, dim), lambda i, *_: (middle(i), 0, 0))
     any_space = pl.BlockSpec(memory_space=pl.ANY)
-    outs = [pl.BlockSpec((toks, dim), lambda i, *_: (0, 0)) for d in range(depth)]
     shape = jax.ShapeDtypeStruct
     dma = pltpu.SemaphoreType.DMA
     result = pl.pallas_call(
@@ -803,26 +843,26 @@
             num_scalar_prefetch=2,
             grid=(2 * depth + n_exp,),
             in_specs=[
-                pl.BlockSpec((1, n_exp, toks), plan_at(0)), pl.BlockSpec((1, n_exp, toks), plan_at(n_dev // n_exp)),
+                pl.BlockSpec((1, 2 * n_exp, toks), plan_at),
                 pl.BlockSpec((toks, dim), lambda i, *_: (first(i), 0)), wide, wide, tall,
             ],
-            out_specs=outs + [any_space, any_space],
+            out_specs=[any_space] * (depth + 2),
             scratch_shapes=[
                 pltpu.VMEM((rows, dim), BF16), pltpu.VMEM((n_exp * WIN, dim), BF16),
-                pltpu.VMEM((2, ROWS, dim), BF16), pltpu.VMEM((2, 2, ROWS, ff), F32),
+                pltpu.VMEM((2, ROWS, dim), BF16), pltpu.VMEM((2, 2, ROWS, ff), F32), pltpu.VMEM((2, toks, dim), F32),
                 pltpu.SMEM(((n_tiles + 1) * n_exp,), jnp.int32), pltpu.SMEM((n_exp,), jnp.int32),
-                pltpu.SMEM((n_exp + 1,), jnp.int32), dma((2,)), dma((2,)),
+                pltpu.SMEM((n_exp + 1,), jnp.int32), dma((2,)), dma((2,)), dma((2,)),
             ],
         ),
         out_shape=[shape((toks, dim), F32)] * depth + [shape((blocks, ROWS, dim), BF16), shape((blocks, 2, ROWS, ff), F32)],
         compiler_params=pltpu.CompilerParams(dimension_semantics=("arbitrary",), vmem_limit_bytes=64_000_000),
         cost_estimate=pl.CostEstimate(flops=25_000_000_000, bytes_accessed=80_000_000, transcendentals=3_000_000),
         name="forward",
-    )(counts, place, plan_col, plan_col, x_col.reshape(-1, dim), w_gate, w_up, w_down)
+    )(counts, place, plan_col, x_col.reshape(-1, dim), w_gate, w_up, w_down)
     return result[:depth], result[depth], result[depth + 1]
 
 
-def expert_backward(depth, n_dev, counts, place, plan_col, dy_head, dy_tails, w_gate, w_up, w_down, x_saved, uv_saved, cap):
+def expert_backward(depth, counts, place, plan_col, dy_head, dy_tails, w_gate, w_up, w_down, x_saved, uv_saved, cap):
     n_tiles, n_exp, rows, blocks = layer_sizes(depth, plan_col.shape[2], w_gate, cap)
     head, dim = dy_head.shape[1:]
     tail = dy_tails[0].shape[0]
@@ -832,8 +872,7 @@
     middle = lambda i: jnp.clip(i - depth, 0, n_exp - 1)
     last = lambda i: jnp.maximum(i - depth - n_exp, 0)
 
-    def plan_at(part):
-        return lambda i, counts, place: (jnp.where(i < depth, i, last(i)), place[0] + part, 0)
+    plan_at = lambda i, counts, place: (jnp.where(i < depth, i, last(i)), place[0], 0)
 
     wide = pl.BlockSpec((1, dim, ff), lambda i, *_: (middle(i), 0, 0))
     tall = pl.BlockSpec((1, ff, dim), lambda i, *_: (middle(i), 0, 0))
@@ -846,7 +885,7 @@
             num_scalar_prefetch=2,
             grid=(2 * depth + n_exp,),
             in_specs=[
-                pl.BlockSpec((1, n_exp, toks), plan_at(0)), pl.BlockSpec((1, n_exp, toks), plan_at(n_dev // n_exp)),
+                pl.BlockSpec((1, 2 * n_exp, toks), plan_at),
                 pl.BlockSpec((head, dim), lambda i, *_: (first(i), 0)),
                 *[pl.BlockSpec((tail, dim), lambda i, *_: (0, 0))] * depth, wide, wide, tall, any_space, any_space,
             ],
@@ -865,7 +904,7 @@
         compiler_params=pltpu.CompilerParams(dimension_semantics=("arbitrary",), vmem_limit_bytes=66_000_000),
         cost_estimate=pl.CostEstimate(flops=50_000_000_000, bytes_accessed=150_000_000, transcendentals=3_000_000),
         name="backward",
-    )(counts, place, plan_col, plan_col, dy_head.reshape(-1, dim), *dy_tails, w_gate, w_up, w_down, x_saved, uv_saved)
+    )(counts, place, plan_col, dy_head.reshape(-1, dim), *dy_tails, w_gate, w_up, w_down, x_saved, uv_saved)
 
 
 def solution(mesh):
@@ -880,27 +919,24 @@
         cap = depth * (2 * tok_loc * top_k // (n_dev * w_gate.shape[0] - 2))
         n_exp = 8 * w_gate.shape[0]
         head = tok_loc // 2
-        x_col, dy_head, plan_col, wg_all, wu_all, wd_all = spread(
-            depth, n_dev, head, x_tok, dy_tok, route_idx.T, gates.T.astype(F32), w_gate, w_up, w_down
+        x_col, dy_head, dy_tail, plan_col, wg_all, wu_all, wd_all = spread(
+            depth, n_dev, head, x_tok, dy_tok, route_idx.T, gates.T, w_gate, w_up, w_down
         )
         turn = lambda a, d: lax.ppermute(a, 'z', [(i, (i + d) % depth) for i in range(depth)])
-        x_col, dy_tail = lax.optimization_barrier((x_col, dy_tok[head:]))
         dy_tails = [dy_tail] + [turn(dy_tail, d) for d in range(1, depth)]
         place = lax.axis_index('z')
         per = tok_loc // TILE
         counts = lax.dynamic_slice(plan_col[:, 2 * n_dev : 2 * n_dev + per, :n_dev], (0, 0, place * n_exp), (depth, per, n_exp))
         where = (counts.reshape(-1).astype(jnp.int32), place.reshape(1), plan_col)
-        y_parts, x_saved, uv_saved = expert_forward(depth, n_dev, *where, x_col, wg_all, wu_all, wd_all, cap)
+        y_parts, x_saved, uv_saved = expert_forward(depth, *where, x_col, wg_all, wu_all, wd_all, cap)
         y_sum = y_parts[0]
         turned = [turn(y_parts[d], d) for d in range(1, depth)]
         dx_part, grads = expert_backward(
-            depth, n_dev, *where, dy_head, dy_tails, wg_all, wu_all, wd_all, x_saved, uv_saved, cap
+            depth, *where, dy_head, dy_tails, wg_all, wu_all, wd_all, x_saved, uv_saved, cap
         )
-        dx, dw = collect(depth, dx_part.reshape(depth, tok_loc, -1), grads)
+        dx, *dw = collect(depth, dx_part.reshape(depth, tok_loc, -1), grads)
         y_sum, turned, dx, dw = lax.optimization_barrier((y_sum, turned, dx, dw))
         y = functools.reduce(jnp.add, turned, y_sum).astype(BF16)
-        dim, ff = w_gate.shape[1:]
-        g_down = jnp.concatenate([dw[2 * dim : 2 * dim + ff], dw[2 * dim + ff :]], axis=1)
-        return y, dx, dw[None, :dim], dw[None, dim : 2 * dim], g_down[None]
+        return y, dx, *[a[None] for a in dw]
 
     return jax.shard_map(local_step, mesh=grid, in_specs=(spec,) * 7, out_specs=(spec,) * 5, check_vma=False)

time: 510 us -> 465 us (0.912)
  Pallas kernels: 475 us -> 443 us
    pallas_call x1, Pallas kernels: 240 us -> 224 us  [collect(): pl.pallas_call(functools.partial(collect_kernel, depth), in_specs=[any_sp...]
    pallas_call x1, Pallas kernels: 51.7 us -> 42 us  [expert_forward(): pl.pallas_call(functools.partial(forward_kernel, depth, n_tiles, n_exp),...]
    pallas_call x1, Pallas kernels: 121 us -> 114 us  [spread(): pl.pallas_call(functools.partial(spread_kernel, depth, experts), in_specs...]
  transfers between devices with their start and end apart: 6 -> 6, of which waited for: 0 -> 0; matrix products, arithmetic and copies ran while one was open for 0% -> 0% of each run, Pallas kernels for 70% -> 71%
where the time goes in v5:
time: 465 us; the launch traced here: 463 us
  Pallas kernels  443 us (95%)
  local copies, waits for them, and re-layouts  7.29 us (2%)
  starting transfers between devices  7.1 us (2%)
  other arithmetic  4.76 us (1%)
    pallas_call x1, Pallas kernels, collect(): pl.pallas_call(functools.partial(collect_kernel, depth), in_specs=[any_sp...  224 us
    pallas_call x1, Pallas kernels, spread(): pl.pallas_call(functools.partial(spread_kernel, depth, experts), in_specs...  114 us
    pallas_call x1, Pallas kernels, expert_backward(): pl.pallas_call(functools.partial(backward_kernel, depth, n_tiles, n_exp),...  63.3 us
    pallas_call x1, Pallas kernels, expert_forward(): pl.pallas_call(functools.partial(forward_kernel, depth, n_tiles, n_exp),...  42 us
  transfers between devices with their start and end apart: 6, of which 0 were waited for; matrix products, arithmetic and copies ran while one was open for 0% of the time, Pallas kernels for 71%

profile of v5, /device:TPU:0, one launch (start us, length us, event | category | flops | bytes accessed | tf_op | source)
XLA Modules:
  0.0 462.7 jit_solution(15229801284924784782)
XLA Ops:
  0.6 113.6 %spread.1 = (bf16[4,512,1024]{2,1,0:T(8,128)(2,1)}, bf16[4,256,1024]{2,1,0:T(8,128)(2,1)}, bf16[256,1024]{1,0:T(8,128)(2,1)}, bf16[4,80,512]{2,1,0:T(8,128)(2,1)...) custom-call(bf16[512,1024]{1,0:T(8,128)(2,1)} %x_ref.1, ...), custom_call_target="tpu_custom_call" | custom-call | tf_op jit(solution)/shard_map/spread/pallas_call | solution.py:249
  114.2 2.5 collective-permute-start.5
  116.7 0.0 collective-permute-start.4
  116.7 0.6 collective-permute-start.3
  117.4 0.7 slice.3
  118.1 0.1 dynamic-slice_convert_fusion
  118.1 0.6 reshape.29.count_ref
  118.8 42.0 %forward.1 = (f32[512,1024]{1,0:T(8,128)}, f32[512,1024]{1,0:T(8,128)}, f32[512,1024]{1,0:T(8,128)}, f32[512,1024]{1,0:T(8,128)}, bf16[24,512,1024]{2,1,0:T(8,128)(2,1)}, /*index=5*/f32[24,2,512,512]{3,2,1,0:T(8,128)}) custom-call(s32[64]{0:T(128)} %reshape.29.count_ref, s32[1]{0:T(128)} %bitcast.2.z_ref, bf16[4,80,512]{2,1,0:T(8,128)(2,1)} %get-tuple-element.32.plan_ref, ...), custom_call_target="tpu_custom_call" | custom-call | flops 24999999488 | bytes 80000000 | tf_op jit(solution)/shard_map/forward/pallas_call | solution.py:840
  160.8 0.7 collective-permute-start
  161.5 2.3 collective-permute-start.1
  163.7 0.0 collective-permute-done.5.refs_3_
  163.7 0.0 copy-start.1
  163.7 1.0 collective-permute-start.2
  164.7 0.0 collective-permute-done.4.refs_2_
  164.7 0.0 collective-permute-done.3.refs_1_
  164.7 0.0 copy-done.1
  164.7 63.3 %backward.1 = (f32[2048,1024]{1,0:T(8,128)}, f32[8,3072,512]{2,1,0:T(8,128)}) custom-call(s32[64]{0:T(128)} %reshape.29.count_ref, s32[1]{0:T(128)} %bitcast.2.z_ref, bf16[4,80,512]{2,1,0:T(8,128)(2,1)} %get-tuple-element.32.plan_ref, bf16[1024,1024]{1,0:T(8,128)(2,1)} %bitcast.16, bf16[256,1024]{1,0:T(8,128)(2,1)} %get-tuple-element.42.refs_0_, ...), custom_call_target="tpu_custom_call" | custom-call | flops 49999998976 | bytes 150000000 | tf_op jit(solution)/shard_map/backward/pallas_call | solution.py:882
  228.1 224.0 %collect.1 = (bf16[512,1024]{1,0:T(8,128)(2,1)S(1)}, f32[1024,512]{1,0:T(8,128)S(1)}, f32[1024,512]{1,0:T(8,128)S(1)}, f32[512,1024]{1,0:T(8,128)S(1)}, f32[4,3072,512]{2,1,0:T(8,128)}) custom-call(f32[4,512,1024]{2,1,0:T(8,128)} %bitcast.12, f32[8,3072,512]{2,1,0:T(8,128)} %get-tuple-element.46.g_ref), custom_call_target="tpu_custom_call" | custom-call | tf_op jit(solution)/shard_map/collect/pallas_call | solution.py:514
  452.0 0.0 collective-permute-done
  452.1 0.0 collective-permute-done.1
  452.1 0.0 collective-permute-done.2
  452.1 1.0 copy.16
  453.1 1.3 copy.17
  454.4 1.3 copy.18
  455.7 0.0 copy-start
  455.7 1.3 copy.19
  457.0 1.0 copy-done
  458.0 4.7 %add_convert_fusion = bf16[512,1024]{1,0:T(8,128)(2,1)} fusion(f32[512,1024]{1,0:T(8,128)} %collective-permute-done.2, f32[512,1024]{1,0:T(8,128)} %collective-permute-done.1, f32[512,1024]{1,0:T(8,128)S(1)} %copy-done, f32[512,1024]{1,0:T(8,128)} %collective-permute-done), kind=kLoop, calls=%fused_computation | loop fusion | flops 2097152 | bytes 9437184 | tf_op jit(solution)/shard_map/convert_element_type | solution.py:939
Async XLA Ops:
  114.2 49.5 %collective-permute-start.5 = (bf16[256,1024]{1,0:T(8,128)(2,1)}, bf16[256,1024]{1,0:T(8,128)(2,1)S(1)}, u32[]{:S(2)}, u32[]{:S(2)}) collective-permute-start(bf16[256,1024]{1,0:T(8,128)(2,1)} %get-tuple-element.42.refs_0_), channel_id=1, source_target_pairs={{0,24},{8,0},{16,8},{24,16},{1,25},{9,1},{17,9},{25,17},{2,26},{10... | collective-permute-start | bytes 1572872 | tf_op jit(solution)/shard_map/ppermute | solution.py:925
  116.7 48.0 %collective-permute-start.4 = (bf16[256,1024]{1,0:T(8,128)(2,1)}, bf16[256,1024]{1,0:T(8,128)(2,1)}, u32[]{:S(2)}, u32[]{:S(2)}) collective-permute-start(bf16[256,1024]{1,0:T(8,128)(2,1)} %get-tuple-element.42.refs_0_), channel_id=1, source_target_pairs={{0,16},{8,24},{16,0},{24,8},{1,17},{9,25},{17,1},{25,9},{2,18},{10... | collective-permute-start | bytes 1572872 | tf_op jit(solution)/shard_map/ppermute | solution.py:925
  116.7 48.0 %collective-permute-start.3 = (bf16[256,1024]{1,0:T(8,128)(2,1)}, bf16[256,1024]{1,0:T(8,128)(2,1)}, u32[]{:S(2)}, u32[]{:S(2)}) collective-permute-start(bf16[256,1024]{1,0:T(8,128)(2,1)} %get-tuple-element.42.refs_0_), channel_id=1, source_target_pairs={{0,8},{8,16},{16,24},{24,0},{1,9},{9,17},{17,25},{25,1},{2,10},{10... | collective-permute-start | bytes 1572872 | tf_op jit(solution)/shard_map/ppermute | solution.py:925
  160.8 291.3 %collective-permute-start = (f32[512,1024]{1,0:T(8,128)}, f32[512,1024]{1,0:T(8,128)}, u32[]{:S(2)}, u32[]{:S(2)}) collective-permute-start(f32[512,1024]{1,0:T(8,128)} %get-tuple-element.38), channel_id=1, source_target_pairs={{0,8},{8,16},{16,24},{24,0},{1,9},{9,17},{17,25},{25,1},{2,10},{10... | collective-permute-start | bytes 6291464 | tf_op jit(solution)/shard_map/ppermute | solution.py:925
  161.5 290.6 %collective-permute-start.1 = (f32[512,1024]{1,0:T(8,128)}, f32[512,1024]{1,0:T(8,128)}, u32[]{:S(2)}, u32[]{:S(2)}) collective-permute-start(f32[512,1024]{1,0:T(8,128)} %get-tuple-element.39), channel_id=1, source_target_pairs={{0,16},{8,24},{16,0},{24,8},{1,17},{9,25},{17,1},{25,9},{2,18},{10... | collective-permute-start | bytes 6291464 | tf_op jit(solution)/shard_map/ppermute | solution.py:925
  163.7 1.0 copy-start.1
  163.7 288.3 %collective-permute-start.2 = (f32[512,1024]{1,0:T(8,128)}, f32[512,1024]{1,0:T(8,128)}, u32[]{:S(2)}, u32[]{:S(2)}) collective-permute-start(f32[512,1024]{1,0:T(8,128)} %get-tuple-element.40), channel_id=1, source_target_pairs={{0,24},{8,0},{16,8},{24,16},{1,25},{9,1},{17,9},{25,17},{2,26},{10... | collective-permute-start | bytes 6291464 | tf_op jit(solution)/shard_map/ppermute | solution.py:925
  455.7 2.3 copy-start

commit v6 on v5

--- a/solution.py
+++ b/solution.py
@@ -10,6 +10,7 @@
 F32 = jnp.float32
 BF16 = jnp.bfloat16
 TILE = 256
+HEAD = 8
 WIN = 128
 ALIGN = 16
 ROWS = 512
@@ -544,14 +545,16 @@
         off_ref[exp] = base
         blk_ref[exp] = block
         big, rest = blocks_of(run)
-        block += big + rest
-        base += jnp.maximum(big * ROWS + rest * (ROWS // 2), (run + ALIGN - 1) // ALIGN * ALIGN + WIN)
+        block += big
+        base += jnp.maximum(big * ROWS + rest, (run + ALIGN - 1) // ALIGN * ALIGN + WIN)
     blk_ref[n_exp] = block
 
 
 def blocks_of(count):
-    big = (count + ROWS // 2 - 1) // ROWS
-    return big, (count > big * ROWS).astype(jnp.int32)
+    over = count % ROWS
+    big = count // ROWS + jnp.where(over > ROWS // 2, 1, 0)
+    rest = jnp.where(over > ROWS // 4, ROWS // 2, jnp.where(over > 0, ROWS // 4, 0))
+    return big, jnp.where(over > ROWS // 2, 0, rest)
 
 
 def span(n_exp, cum_ref, tile, exp):
@@ -620,13 +623,15 @@
     *refs,
 ):
     y_refs, refs = refs[:depth], refs[depth:]
-    xs_ref, uv_ref, rows_ref, win_ref, x_out, uv_out, y_buf, cum_ref, off_ref, blk_ref, x_sem, uv_sem, y_sem = refs
+    xs_ref, uv_ref, xt_ref, uvt_ref, rows_ref, win_ref, x_out, uv_out, xt_out, uvt_out, y_buf = refs[:11]
+    cum_ref, off_ref, blk_ref, tail_ref, x_sem, uv_sem, t_sem, y_sem = refs[11:]
     step = pl.program_id(0)
     per = n_tiles // depth
 
     @pl.when(step == 0)
     def _():
         count_up(n_tiles, n_exp, count_ref, cum_ref, off_ref, blk_ref)
+        tail_ref[0] = 0
 
     @pl.when(step < depth)
     def _():
@@ -642,41 +647,60 @@
             pltpu.make_async_copy(uv_out.at[side], uv_ref.at[block], uv_sem.at[side]),
         )
 
+    def tail_saves(exp, size):
+        at = slice(0, size)
+        return (
+            pltpu.make_async_copy(xt_out.at[at], xt_ref.at[exp, at], t_sem.at[0]),
+            pltpu.make_async_copy(uvt_out.at[:, at], uvt_ref.at[exp, :, at], t_sem.at[1]),
+        )
+
+    def tail_saved():
+        for size in (ROWS // 2, ROWS // 4):
+            @pl.when(tail_ref[0] == size)
+            def _(size=size):
+                for copy in tail_saves(0, size):
+                    copy.wait()
+
     @pl.when((step >= depth) & (step < depth + n_exp))
     def _():
         exp = step - depth
         count = cum_ref[n_tiles * n_exp + exp]
         big, rest = blocks_of(count)
 
-        def run(b, size):
+        def run(start, x_blk, uv_blk):
+            size = x_blk.shape[0]
+            here = pl.ds(pl.multiple_of(off_ref[exp] + start, ALIGN), size)
+            live = lax.broadcasted_iota(jnp.int32, (size, 1), 0) < count - start
+            x_old = rows_ref[here, :]
+            x_blk[...] = jnp.where(live, x_old, jnp.zeros_like(x_old))
+            u = dot(x_blk[...], wg_ref[0])
+            v = dot(x_blk[...], wu_ref[0])
+            uv_blk[0] = u
+            uv_blk[1] = v
+            act = (u * jax.nn.sigmoid(u) * v).astype(BF16)
+            rows_ref[here, :] = dot(act, wd_ref[0]).astype(BF16)
+
+        @pl.loop(0, big)
+        def _(b):
             block = blk_ref[exp] + b
-            side = block % 2
 
             @pl.when(block >= 2)
             def _():
                 for copy in saves(block - 2):
                     copy.wait()
 
-            here = pl.ds(pl.multiple_of(off_ref[exp] + b * ROWS, ALIGN), size)
-            live = lax.broadcasted_iota(jnp.int32, (size, 1), 0) < count - b * ROWS
-            x_old = rows_ref[here, :]
-            x_out[side, :size] = jnp.where(live, x_old, jnp.zeros_like(x_old))
-            u = dot(x_out[side, :size], wg_ref[0])
-            v = dot(x_out[side, :size], wu_ref[0])
-            uv_out[side, 0, :size] = u
-            uv_out[side, 1, :size] = v
-            act = (u * jax.nn.sigmoid(u) * v).astype(BF16)
-            rows_ref[here, :] = dot(act, wd_ref[0]).astype(BF16)
+            run(b * ROWS, x_out.at[block % 2], uv_out.at[block % 2])
             for copy in saves(block):
                 copy.start()
 
-        @pl.loop(0, big)
-        def _(b):
-            run(b, ROWS)
-
-        @pl.when(rest > 0)
-        def _():
-            run(big, ROWS // 2)
+        for size in (ROWS // 2, ROWS // 4):
+            @pl.when(rest == size)
+            def _(size=size):
+                tail_saved()
+                run(big * ROWS, xt_out.at[slice(0, size)], uvt_out.at[:, slice(0, size)])
+                for copy in tail_saves(exp, size):
+                    copy.start()
+                tail_ref[0] = size
 
     @pl.when(step == depth + n_exp)
     def _():
@@ -687,6 +711,8 @@
                 for copy in saves(total - back):
                     copy.wait()
 
+        tail_saved()
+
     d = step - depth - n_exp
 
     def y_copy(d, k):
@@ -701,7 +727,7 @@
 
         plan_t = jnp.transpose(plan_ref[0].astype(F32))
         for i in range(per):
-            tile = ((z_ref[0] + d) % depth) * per + i
+            tile = (z_ref[0] ^ d) * per + i
             cols = slice(i * TILE, (i + 1) * TILE)
             scatter_tile(n_exp, cum_ref, off_ref, plan_t, True, tile, cols, rows_ref, win_ref, y_buf.at[d % 2])
         for k in range(depth):
@@ -719,8 +745,8 @@
     depth, n_tiles, n_exp, count_ref, z_ref, plan_ref, head_ref, *refs,
 ):
     tails, refs = refs[:depth], refs[depth:]
-    wg_ref, wu_ref, wd_ref, xs_ref, uv_ref, dx_ref, dw_ref = refs[:7]
-    rows_ref, win_ref, x_in, uv_in, tail_ref, cum_ref, off_ref, blk_ref, x_sem, uv_sem = refs[7:]
+    wg_ref, wu_ref, wd_ref, xs_ref, uv_ref, xt_ref, uvt_ref, dx_ref, dw_ref = refs[:9]
+    rows_ref, win_ref, x_in, uv_in, xt_in, uvt_in, tok_ref, cum_ref, off_ref, blk_ref, x_sem, uv_sem, t_sem = refs[9:]
     step = pl.program_id(0)
     per = n_tiles // depth
 
@@ -730,17 +756,17 @@
 
     @pl.when(step < depth)
     def _():
+        split = head_ref.shape[0]
+        tok_ref[:split, :] = head_ref[...]
         for d in range(depth):
-            @pl.when((z_ref[0] + depth - step) % depth == d)
-            def _():
-                tail_ref[...] = tails[d][...]
+            @pl.when((z_ref[0] ^ step) == d)
+            def _(d=d):
+                tok_ref[split:, :] = tails[d][...]
 
         plan = plan_ref[0].astype(F32)
-        split = head_ref.shape[0]
         for i in range(per):
             cols = slice(i * TILE, (i + 1) * TILE)
-            toks = head_ref.at[cols, :] if i * TILE < split else tail_ref.at[slice(i * TILE - split, (i + 1) * TILE - split), :]
-            gather_tile(n_exp, cum_ref, off_ref, plan, True, step * per + i, cols, toks, rows_ref)
+            gather_tile(n_exp, cum_ref, off_ref, plan, True, step * per + i, cols, tok_ref.at[cols, :], rows_ref)
 
     def loads(block):
         side = block % 2
@@ -754,38 +780,47 @@
         for copy in loads(0):
             copy.start()
 
+    def tail_loads(exp, size):
+        at = slice(0, size)
+        return (
+            pltpu.make_async_copy(xt_ref.at[exp, at], xt_in.at[at], t_sem.at[0]),
+            pltpu.make_async_copy(uvt_ref.at[exp, :, at], uvt_in.at[:, at], t_sem.at[1]),
+        )
+
     @pl.when((step >= depth) & (step < depth + n_exp))
     def _():
         exp = step - depth
         count = cum_ref[n_tiles * n_exp + exp]
         big, rest = blocks_of(count)
         dim, ff = wg_ref.shape[1:]
+        sizes = (ROWS // 2, ROWS // 4)
+        for size in sizes:
+            @pl.when(rest == size)
+            def _(size=size):
+                for copy in tail_loads(exp, size):
+                    copy.start()
 
         @pl.when(count == 0)
         def _():
-            dw_ref[...] = jnp.zeros_like(dw_ref)
-
-        def run(b, size):
-            block = blk_ref[exp] + b
-            side = block % 2
-
-            @pl.when(block + 1 < blk_ref[n_exp])
-            def _():
-                for copy in loads(block + 1):
-                    copy.start()
+            @pl.loop(0, 3 * dim // ff)
+            def _(i):
+                dw_ref[0, pl.ds(i * ff, ff), :] = jnp.zeros((ff, ff), F32)
+
+        def run(start, x_blk, uv_blk, copies):
+            size = x_blk.shape[0]
 
             def add(at, value):
-                dw_ref[0, at, :] = jnp.where(b == 0, 0.0, dw_ref[0, at, :]) + value
-
-            here = pl.ds(pl.multiple_of(off_ref[exp] + b * ROWS, ALIGN), size)
-            live = lax.broadcasted_iota(jnp.int32, (size, 1), 0) < count - b * ROWS
+                dw_ref[0, at, :] = jnp.where(start == 0, 0.0, dw_ref[0, at, :]) + value
+
+            here = pl.ds(pl.multiple_of(off_ref[exp] + start, ALIGN), size)
+            live = lax.broadcasted_iota(jnp.int32, (size, 1), 0) < count - start
             g_old = rows_ref[here, :]
             g_blk = jnp.where(live, g_old, jnp.zeros_like(g_old))
             da = dot(g_blk, wd_ref[0], ((1,), (1,)))
-            for copy in loads(block):
+            for copy in copies:
                 copy.wait()
-            u = uv_in[side, 0, :size]
-            v = uv_in[side, 1, :size]
+            u = uv_blk[0]
+            v = uv_blk[1]
             s = jax.nn.sigmoid(u)
             act = (u * s * v).astype(BF16)
             du = (da * v * s * (1.0 + u * (1.0 - s))).astype(BF16)
@@ -794,16 +829,24 @@
             add(slice(2 * dim + ff, 3 * dim), dot(act, g_blk[:, ff:], ((0,), (0,))))
             dxr = dot(du, wg_ref[0], ((1,), (1,))) + dot(dv, wu_ref[0], ((1,), (1,)))
             rows_ref[here, :] = dxr.astype(BF16)
-            add(slice(0, dim), dot(x_in[side, :size], du, ((0,), (0,))))
-            add(slice(dim, 2 * dim), dot(x_in[side, :size], dv, ((0,), (0,))))
+            add(slice(0, dim), dot(x_blk[...], du, ((0,), (0,))))
+            add(slice(dim, 2 * dim), dot(x_blk[...], dv, ((0,), (0,))))
 
         @pl.loop(0, big)
         def _(b):
-            run(b, ROWS)
-
-        @pl.when(rest > 0)
-        def _():
-            run(big, ROWS // 2)
+            block = blk_ref[exp] + b
+
+            @pl.when(block + 1 < blk_ref[n_exp])
+            def _():
+                for copy in loads(block + 1):
+                    copy.start()
+
+            run(b * ROWS, x_in.at[block % 2], uv_in.at[block % 2], loads(block))
+
+        for size in sizes:
+            @pl.when(rest == size)
+            def _(size=size):
+                run(big * ROWS, xt_in.at[slice(0, size)], uvt_in.at[:, slice(0, size)], tail_loads(exp, size))
 
     @pl.when(step >= depth + n_exp)
     def _():
@@ -818,8 +861,10 @@
     tokens = depth * toks
     n_exp = w_gate.shape[0]
     n_tiles = tokens // TILE
-    rows = n_exp * max(-(-cap // (ROWS // 2)) * (ROWS // 2), -(-cap // ALIGN) * ALIGN + WIN) + ROWS
-    return n_tiles, n_exp, rows, n_exp * -(-cap // ROWS)
+    full = lambda n: n // ROWS + (n % ROWS > ROWS // 2)
+    part = lambda n: 0 if n % ROWS == 0 or n % ROWS > ROWS // 2 else ROWS // 2 if n % ROWS > ROWS // 4 else ROWS // 4
+    most = max(max(full(n) * ROWS + part(n), -(-n // ALIGN) * ALIGN + WIN) for n in range(cap + 1))
+    return n_tiles, n_exp, n_exp * most + ROWS, n_exp * max(1, full(cap))
 
 
 def expert_forward(depth, counts, place, plan_col, x_col, w_gate, w_up, w_down, cap):
@@ -830,7 +875,7 @@
     middle = lambda i: jnp.clip(i - depth, 0, n_exp - 1)
     last = lambda i: jnp.maximum(i - depth - n_exp, 0)
 
-    plan_at = lambda i, counts, place: (jnp.where(i < depth, i, (place[0] + last(i)) % depth), place[0], 0)
+    plan_at = lambda i, counts, place: (jnp.where(i < depth, i, place[0] ^ last(i)), place[0], 0)
 
     wide = pl.BlockSpec((1, dim, ff), lambda i, *_: (middle(i), 0, 0))
     tall = pl.BlockSpec((1, ff, dim), lambda i, *_: (middle(i), 0, 0))
@@ -846,23 +891,27 @@
                 pl.BlockSpec((1, 2 * n_exp, toks), plan_at),
                 pl.BlockSpec((toks, dim), lambda i, *_: (first(i), 0)), wide, wide, tall,
             ],
-            out_specs=[any_space] * (depth + 2),
+            out_specs=[any_space] * (depth + 4),
             scratch_shapes=[
                 pltpu.VMEM((rows, dim), BF16), pltpu.VMEM((n_exp * WIN, dim), BF16),
-                pltpu.VMEM((2, ROWS, dim), BF16), pltpu.VMEM((2, 2, ROWS, ff), F32), pltpu.VMEM((2, toks, dim), F32),
+                pltpu.VMEM((2, ROWS, dim), BF16), pltpu.VMEM((2, 2, ROWS, ff), F32),
+                pltpu.VMEM((ROWS // 2, dim), BF16), pltpu.VMEM((2, ROWS // 2, ff), F32), pltpu.VMEM((2, toks, dim), F32),
                 pltpu.SMEM(((n_tiles + 1) * n_exp,), jnp.int32), pltpu.SMEM((n_exp,), jnp.int32),
-                pltpu.SMEM((n_exp + 1,), jnp.int32), dma((2,)), dma((2,)), dma((2,)),
+                pltpu.SMEM((n_exp + 1,), jnp.int32), pltpu.SMEM((1,), jnp.int32), dma((2,)), dma((2,)), dma((2,)), dma((2,)),
             ],
         ),
-        out_shape=[shape((toks, dim), F32)] * depth + [shape((blocks, ROWS, dim), BF16), shape((blocks, 2, ROWS, ff), F32)],
+        out_shape=[shape((toks, dim), F32)] * depth + [
+            shape((blocks, ROWS, dim), BF16), shape((blocks, 2, ROWS, ff), F32),
+            shape((n_exp, ROWS // 2, dim), BF16), shape((n_exp, 2, ROWS // 2, ff), F32),
+        ],
         compiler_params=pltpu.CompilerParams(dimension_semantics=("arbitrary",), vmem_limit_bytes=64_000_000),
         cost_estimate=pl.CostEstimate(flops=25_000_000_000, bytes_accessed=80_000_000, transcendentals=3_000_000),
         name="forward",
     )(counts, place, plan_col, x_col.reshape(-1, dim), w_gate, w_up, w_down)
-    return result[:depth], result[depth], result[depth + 1]
-
-
-def expert_backward(depth, counts, place, plan_col, dy_head, dy_tails, w_gate, w_up, w_down, x_saved, uv_saved, cap):
+    return result[:depth], result[depth:]
+
+
+def expert_backward(depth, counts, place, plan_col, dy_head, dy_tails, w_gate, w_up, w_down, saved, cap):
     n_tiles, n_exp, rows, blocks = layer_sizes(depth, plan_col.shape[2], w_gate, cap)
     head, dim = dy_head.shape[1:]
     tail = dy_tails[0].shape[0]
@@ -887,7 +936,7 @@
             in_specs=[
                 pl.BlockSpec((1, 2 * n_exp, toks), plan_at),
                 pl.BlockSpec((head, dim), lambda i, *_: (first(i), 0)),
-                *[pl.BlockSpec((tail, dim), lambda i, *_: (0, 0))] * depth, wide, wide, tall, any_space, any_space,
+                *[pl.BlockSpec((tail, dim), lambda i, *_: (0, 0))] * depth, wide, wide, tall, *[any_space] * 4,
             ],
             out_specs=[
                 pl.BlockSpec((toks, dim), lambda i, *_: (last(i), 0)),
@@ -895,16 +944,68 @@
             ],
             scratch_shapes=[
                 pltpu.VMEM((rows, dim), BF16), pltpu.VMEM((n_exp * WIN, dim), BF16),
-                pltpu.VMEM((2, ROWS, dim), BF16), pltpu.VMEM((2, 2, ROWS, ff), F32), pltpu.VMEM((tail, dim), BF16),
+                pltpu.VMEM((2, ROWS, dim), BF16), pltpu.VMEM((2, 2, ROWS, ff), F32),
+                pltpu.VMEM((ROWS // 2, dim), BF16), pltpu.VMEM((2, ROWS // 2, ff), F32), pltpu.VMEM((toks, dim), BF16),
                 pltpu.SMEM(((n_tiles + 1) * n_exp,), jnp.int32), pltpu.SMEM((n_exp,), jnp.int32),
-                pltpu.SMEM((n_exp + 1,), jnp.int32), dma((2,)), dma((2,)),
+                pltpu.SMEM((n_exp + 1,), jnp.int32), dma((2,)), dma((2,)), dma((2,)),
             ],
         ),
         out_shape=[shape((depth * toks, dim), F32), shape((n_exp, 3 * dim, ff), F32)],
         compiler_params=pltpu.CompilerParams(dimension_semantics=("arbitrary",), vmem_limit_bytes=66_000_000),
         cost_estimate=pl.CostEstimate(flops=50_000_000_000, bytes_accessed=150_000_000, transcendentals=3_000_000),
         name="backward",
-    )(counts, place, plan_col, dy_head.reshape(-1, dim), *dy_tails, w_gate, w_up, w_down, x_saved, uv_saved)
+    )(counts, place, plan_col, dy_head.reshape(-1, dim), *dy_tails, w_gate, w_up, w_down, *saved)
+
+
+def finish_kernel(part_refs, dx_ref, g_refs, y_out, dx_out, g_outs, bufs, out_buf, in_sem, out_sem, y_sem):
+    moves = [pltpu.make_async_copy(dx_ref, dx_out, out_sem.at[0])]
+    moves += [pltpu.make_async_copy(g.at[...], o.at[0], out_sem.at[1 + i]) for i, (g, o) in enumerate(zip(g_refs, g_outs))]
+    n = bufs.shape[0]
+    rows = bufs.shape[2]
+    loads = [
+        [pltpu.make_async_copy(p.at[pl.ds(k * rows, rows), :], bufs.at[k, i], in_sem.at[k, i]) for i, p in enumerate(part_refs)]
+        for k in range(n)
+    ]
+    for copies in loads:
+        for copy in copies:
+            copy.start()
+    for move in moves:
+        move.start()
+    stores = []
+    for k in range(n):
+        for copy in loads[k]:
+            copy.wait()
+        value = functools.reduce(jnp.add, [bufs[k, i] for i in range(len(part_refs))])
+        out_buf[k] = value.astype(BF16)
+        stores.append(pltpu.make_async_copy(out_buf.at[k], y_out.at[pl.ds(k * rows, rows), :], y_sem.at[k]))
+        stores[-1].start()
+    for copy in moves + stores:
+        copy.wait()
+
+
+def finish(parts, dx, grads):
+    toks, dim = dx.shape
+    n = 4
+    any_space = pl.BlockSpec(memory_space=pl.ANY)
+    shape = jax.ShapeDtypeStruct
+    dma = pltpu.SemaphoreType.DMA
+    k = len(parts)
+
+    def body(*refs):
+        finish_kernel(refs[:k], refs[k], refs[k + 1 : k + 4], refs[k + 4], refs[k + 5], refs[k + 6 : k + 9], *refs[k + 9 :])
+
+    return pl.pallas_call(
+        body,
+        in_specs=[any_space] * (k + 4),
+        out_specs=[any_space] * 5,
+        out_shape=[shape((toks, dim), BF16), shape((toks, dim), BF16)] + [shape((1, *g.shape), F32) for g in grads],
+        scratch_shapes=[
+            pltpu.VMEM((n, k, toks // n, dim), F32), pltpu.VMEM((n, toks // n, dim), BF16),
+            dma((n, k)), dma((4,)), dma((n,)),
+        ],
+        compiler_params=pltpu.CompilerParams(vmem_limit_bytes=24_000_000),
+        name="finish",
+    )(*parts, dx, *grads)
 
 
 def solution(mesh):
@@ -918,25 +1019,24 @@
         tok_loc, top_k = route_idx.shape
         cap = depth * (2 * tok_loc * top_k // (n_dev * w_gate.shape[0] - 2))
         n_exp = 8 * w_gate.shape[0]
-        head = tok_loc // 2
+        head = tok_loc // 16 * HEAD
         x_col, dy_head, dy_tail, plan_col, wg_all, wu_all, wd_all = spread(
             depth, n_dev, head, x_tok, dy_tok, route_idx.T, gates.T, w_gate, w_up, w_down
         )
-        turn = lambda a, d: lax.ppermute(a, 'z', [(i, (i + d) % depth) for i in range(depth)])
+        turn = lambda a, d: lax.ppermute(a, 'z', [(i, i ^ d) for i in range(depth)])
         dy_tails = [dy_tail] + [turn(dy_tail, d) for d in range(1, depth)]
         place = lax.axis_index('z')
         per = tok_loc // TILE
         counts = lax.dynamic_slice(plan_col[:, 2 * n_dev : 2 * n_dev + per, :n_dev], (0, 0, place * n_exp), (depth, per, n_exp))
         where = (counts.reshape(-1).astype(jnp.int32), place.reshape(1), plan_col)
-        y_parts, x_saved, uv_saved = expert_forward(depth, *where, x_col, wg_all, wu_all, wd_all, cap)
+        y_parts, saved = expert_forward(depth, *where, x_col, wg_all, wu_all, wd_all, cap)
+        y_parts, dy_tails = lax.optimization_barrier((y_parts, dy_tails))
         y_sum = y_parts[0]
         turned = [turn(y_parts[d], d) for d in range(1, depth)]
         dx_part, grads = expert_backward(
-            depth, *where, dy_head, dy_tails, wg_all, wu_all, wd_all, x_saved, uv_saved, cap
+            depth, *where, dy_head, dy_tails, wg_all, wu_all, wd_all, saved, cap
         )
         dx, *dw = collect(depth, dx_part.reshape(depth, tok_loc, -1), grads)
-        y_sum, turned, dx, dw = lax.optimization_barrier((y_sum, turned, dx, dw))
-        y = functools.reduce(jnp.add, turned, y_sum).astype(BF16)
-        return y, dx, *[a[None] for a in dw]
+        return tuple(finish([y_sum, *turned], dx, dw))
 
     return jax.shard_map(local_step, mesh=grid, in_specs=(spec,) * 7, out_specs=(spec,) * 5, check_vma=False)

time: 465 us -> 458 us (0.985)
  local copies, waits for them, and re-layouts: 7.29 us -> 1.38 us
  Pallas kernels: 443 us -> 438 us
  other arithmetic: 4.76 us -> 0.08 us
    pallas_call x0 -> x1, Pallas kernels: none -> 6.61 us  [finish(): pl.pallas_call(body, in_specs=[any_space] * (k + 4), out_specs=[any_space...]
    unnamed x8 -> x4, local copies, waits for them, and re-layouts: 5.96 us -> 0.01 us
    pallas_call x1, Pallas kernels: 63.3 us -> 58.3 us  [expert_backward(): pl.pallas_call(functools.partial(backward_kernel, depth, n_tiles, n_exp),...]
    convert_element_type x1 -> x0, other arithmetic: 4.68 us -> none  [local_step(): y = functools.reduce(jnp.add, turned, y_sum).astype(BF16)]
  transfers between devices with their start and end apart: 6 -> 6, of which waited for: 0 -> 0; matrix products, arithmetic and copies ran while one was open for 0% -> 0% of each run, Pallas kernels for 71% -> 70%
where the time goes in v6:
time: 458 us; the launch traced here: 452 us
  Pallas kernels  438 us (96%)
  starting transfers between devices  11.6 us (3%)
    pallas_call x1, Pallas kernels, collect(): pl.pallas_call(functools.partial(collect_kernel, depth), in_specs=[any_sp...  221 us
    pallas_call x1, Pallas kernels, spread(): pl.pallas_call(functools.partial(spread_kernel, depth, experts), in_specs...  114 us
    pallas_call x1, Pallas kernels, expert_backward(): pl.pallas_call(functools.partial(backward_kernel, depth, n_tiles, n_exp),...  58.3 us
    pallas_call x1, Pallas kernels, expert_forward(): pl.pallas_call(functools.partial(forward_kernel, depth, n_tiles, n_exp),...  37.8 us
    ppermute x6, starting transfers between devices, local_step(): turn = lambda a, d: lax.ppermute(a, 'z', [(i, i ^ d) for i in range(depth)])  11.6 us
  transfers between devices with their start and end apart: 6, of which 0 were waited for; matrix products, arithmetic and copies ran while one was open for 0% of the time, Pallas kernels for 70%

profile of v6, /device:TPU:0, one launch (start us, length us, event | category | flops | bytes accessed | tf_op | source)
XLA Modules:
  0.0 451.5 jit_solution(6178325122308883212)
XLA Ops:
  0.6 113.6 %spread.1 = (bf16[4,512,1024]{2,1,0:T(8,128)(2,1)}, bf16[4,256,1024]{2,1,0:T(8,128)(2,1)}, bf16[256,1024]{1,0:T(8,128)(2,1)}, bf16[4,80,512]{2,1,0:T(8,128)(2,1)...) custom-call(bf16[512,1024]{1,0:T(8,128)(2,1)} %x_ref.1, ...), custom_call_target="tpu_custom_call" | custom-call | tf_op jit(solution)/shard_map/spread/pallas_call | solution.py:250
  114.2 0.1 collective-permute-start
  114.3 3.0 collective-permute-start.1
  117.3 1.4 collective-permute-start.2
  118.7 0.7 slice.3
  119.4 0.1 dynamic-slice_convert_fusion
  119.4 0.7 reshape.29.count_ref
  120.1 37.8 %forward.1 = (f32[512,1024]{1,0:T(8,128)}, f32[512,1024]{1,0:T(8,128)}, f32[512,1024]{1,0:T(8,128)}, f32[512,1024]{1,0:T(8,128)}, bf16[16,512,1024]{2,1,0:T(8,12...) custom-call(s32[64]{0:T(128)} %reshape.29.count_ref, ...), custom_call_target="tpu_custom_call" | custom-call | flops 24999999488 | bytes 80000000 | tf_op jit(solution)/shard_map/forward/pallas_call | solution.py:885
  157.9 0.0 collective-permute-done.refs_1_
  157.9 0.0 copy-start.1
  157.9 0.0 collective-permute-done.1.refs_2_
  157.9 0.0 collective-permute-done.2.refs_3_
  157.9 4.6 %collective-permute-start.3 = (f32[512,1024]{1,0:T(8,128)}, f32[512,1024]{1,0:T(8,128)}, u32[]{:S(2)}, u32[]{:S(2)}) collective-permute-start(f32[512,1024]{1,0:T(8,128)} %get-tuple-element.45), channel_id=1, source_target_pairs={{0,8},{8,0},{16,24},{24,16},{1,9},{9,1},{17,25},{25,17},{2,10},{10... | collective-permute-start | bytes 6291464 | tf_op jit(solution)/shard_map/ppermute | solution.py:1026
  162.5 2.5 collective-permute-start.4
  165.0 0.0 collective-permute-start.5
  165.0 0.0 copy-done.1
  165.0 58.3 %backward.1 = (f32[2048,1024]{1,0:T(8,128)}, f32[8,3072,512]{2,1,0:T(8,128)}) custom-call(s32[64]{0:T(128)} %reshape.29.count_ref, s32[1]{0:T(128)} %bitcast.2.z_ref, bf16[4,80,512]{2,1,0:T(8,128)(2,1)} %get-tuple-element.34.plan_ref, bf16[1024,1024]{1,0:T(8,128)(2,1)} %bitcast.10, bf16[256,1024]{1,0:T(8,128)(2,1)} %get-tuple-element.49.refs_0_, ...), custom_call_target="tpu_custom_call" | custom-call | flops 49999998976 | bytes 150000000 | tf_op jit(solution)/shard_map/backward/pallas_call | solution.py:931
  223.3 0.0 copy-start
  223.4 221.3 %collect.1 = (bf16[512,1024]{1,0:T(8,128)(2,1)S(1)}, f32[1024,512]{1,0:T(8,128)S(1)}, f32[1024,512]{1,0:T(8,128)S(1)}, f32[512,1024]{1,0:T(8,128)S(1)}, f32[4,3072,512]{2,1,0:T(8,128)}) custom-call(f32[4,512,1024]{2,1,0:T(8,128)} %bitcast.6, f32[8,3072,512]{2,1,0:T(8,128)} %get-tuple-element.58.g_ref), custom_call_target="tpu_custom_call" | custom-call | tf_op jit(solution)/shard_map/collect/pallas_call | solution.py:515
  444.7 0.0 collective-permute-done.3.refs_1_
  444.7 0.0 collective-permute-done.4.refs_2_
  444.7 0.0 collective-permute-done.5.refs_3_
  444.7 0.0 copy-done
  444.7 6.6 %finish.1 = (bf16[512,1024]{1,0:T(8,128)(2,1)}, bf16[512,1024]{1,0:T(8,128)(2,1)}, f32[1,1024,512]{2,1,0:T(8,128)}, f32[1,1024,512]{2,1,0:T(8,128)}, f32[1,512,1024]{2,1,0:T(8,128)}) custom-call(f32[512,1024]{1,0:T(8,128)S(1)} %copy-done, f32[512,1024]{1,0:T(8,128)} %collective-permute-done.3.refs_1_, f32[512,1024]{1,0:T(8,128)} %collective-permute-done.4.refs_2_, ...), custom_call_target="tpu_custom_call" | custom-call | tf_op jit(solution)/shard_map/finish/pallas_call | solution.py:997
Async XLA Ops:
  114.2 43.7 %collective-permute-start = (bf16[256,1024]{1,0:T(8,128)(2,1)}, bf16[256,1024]{1,0:T(8,128)(2,1)S(1)}, u32[]{:S(2)}, u32[]{:S(2)}) collective-permute-start(bf16[256,1024]{1,0:T(8,128)(2,1)} %get-tuple-element.49.refs_0_), channel_id=1, source_target_pairs={{0,8},{8,0},{16,24},{24,16},{1,9},{9,1},{17,25},{25,17},{2,10},{10... | collective-permute-start | bytes 1572872 | tf_op jit(solution)/shard_map/ppermute | solution.py:1026
  114.3 43.6 %collective-permute-start.1 = (bf16[256,1024]{1,0:T(8,128)(2,1)}, bf16[256,1024]{1,0:T(8,128)(2,1)}, u32[]{:S(2)}, u32[]{:S(2)}) collective-permute-start(bf16[256,1024]{1,0:T(8,128)(2,1)} %get-tuple-element.49.refs_0_), channel_id=1, source_target_pairs={{0,16},{8,24},{16,0},{24,8},{1,17},{9,25},{17,1},{25,9},{2,18},{10... | collective-permute-start | bytes 1572872 | tf_op jit(solution)/shard_map/ppermute | solution.py:1026
  117.3 40.6 %collective-permute-start.2 = (bf16[256,1024]{1,0:T(8,128)(2,1)}, bf16[256,1024]{1,0:T(8,128)(2,1)}, u32[]{:S(2)}, u32[]{:S(2)}) collective-permute-start(bf16[256,1024]{1,0:T(8,128)(2,1)} %get-tuple-element.49.refs_0_), channel_id=1, source_target_pairs={{0,24},{8,16},{16,8},{24,0},{1,25},{9,17},{17,9},{25,1},{2,26},{10... | collective-permute-start | bytes 1572872 | tf_op jit(solution)/shard_map/ppermute | solution.py:1026
  157.9 7.1 %copy-start.1 = (bf16[256,1024]{1,0:T(8,128)(2,1)}, bf16[256,1024]{1,0:T(8,128)(2,1)S(1)}, u32[]{:S(2)}) copy-start(bf16[256,1024]{1,0:T(8,128)(2,1)S(1)} %collective-permute-done.refs_1_) | copy-start | bytes 1572868
  157.9 286.8 %collective-permute-start.3 = (f32[512,1024]{1,0:T(8,128)}, f32[512,1024]{1,0:T(8,128)}, u32[]{:S(2)}, u32[]{:S(2)}) collective-permute-start(f32[512,1024]{1,0:T(8,128)} %get-tuple-element.45), channel_id=1, source_target_pairs={{0,8},{8,0},{16,24},{24,16},{1,9},{9,1},{17,25},{25,17},{2,10},{10... | collective-permute-start | bytes 6291464 | tf_op jit(solution)/shard_map/ppermute | solution.py:1026
  162.5 282.2 %collective-permute-start.4 = (f32[512,1024]{1,0:T(8,128)}, f32[512,1024]{1,0:T(8,128)}, u32[]{:S(2)}, u32[]{:S(2)}) collective-permute-start(f32[512,1024]{1,0:T(8,128)} %get-tuple-element.46), channel_id=1, source_target_pairs={{0,16},{8,24},{16,0},{24,8},{1,17},{9,25},{17,1},{25,9},{2,18},{10... | collective-permute-start | bytes 6291464 | tf_op jit(solution)/shard_map/ppermute | solution.py:1026
  165.0 279.7 %collective-permute-start.5 = (f32[512,1024]{1,0:T(8,128)}, f32[512,1024]{1,0:T(8,128)}, u32[]{:S(2)}, u32[]{:S(2)}) collective-permute-start(f32[512,1024]{1,0:T(8,128)} %get-tuple-element.47), channel_id=1, source_target_pairs={{0,24},{8,16},{16,8},{24,0},{1,25},{9,17},{17,9},{25,1},{2,26},{10... | collective-permute-start | bytes 6291464 | tf_op jit(solution)/shard_map/ppermute | solution.py:1026
  223.3 221.4 %copy-start = (f32[512,1024]{1,0:T(8,128)S(1)}, f32[512,1024]{1,0:T(8,128)}, u32[]{:S(2)}) copy-start(f32[512,1024]{1,0:T(8,128)} %get-tuple-element.44.refs_0_) | copy-start | bytes 6291460

commit v7 on v6

--- a/solution.py
+++ b/solution.py
@@ -267,7 +267,7 @@
 
 CHUNK = 128
 BAND = 64
-TURNS = (4, 14, 20, 22)
+TURNS = (4, 15, 22, 24)
 FINISH = 3
 RING = 6
 
@@ -1027,7 +1027,7 @@
         dy_tails = [dy_tail] + [turn(dy_tail, d) for d in range(1, depth)]
         place = lax.axis_index('z')
         per = tok_loc // TILE
-        counts = lax.dynamic_slice(plan_col[:, 2 * n_dev : 2 * n_dev + per, :n_dev], (0, 0, place * n_exp), (depth, per, n_exp))
+        counts = lax.dynamic_slice(plan_col, (0, 2 * n_dev, place * n_exp), (depth, per, n_exp))
         where = (counts.reshape(-1).astype(jnp.int32), place.reshape(1), plan_col)
         y_parts, saved = expert_forward(depth, *where, x_col, wg_all, wu_all, wd_all, cap)
         y_parts, dy_tails = lax.optimization_barrier((y_parts, dy_tails))

time: 458 us -> 457 us (level)
    pallas_call x1, Pallas kernels: 221 us -> 215 us  [collect(): pl.pallas_call(functools.partial(collect_kernel, depth), in_specs=[any_sp...]
where the time goes in v7:
time: 457 us; the launch traced here: 449 us
  Pallas kernels  435 us (95%)
  starting transfers between devices  11.1 us (2%)
    pallas_call x1, Pallas kernels, collect(): pl.pallas_call(functools.partial(collect_kernel, depth), in_specs=[any_sp...  215 us
    pallas_call x1, Pallas kernels, spread(): pl.pallas_call(functools.partial(spread_kernel, depth, experts), in_specs...  114 us
    pallas_call x1, Pallas kernels, expert_backward(): pl.pallas_call(functools.partial(backward_kernel, depth, n_tiles, n_exp),...  61.1 us
    pallas_call x1, Pallas kernels, expert_forward(): pl.pallas_call(functools.partial(forward_kernel, depth, n_tiles, n_exp),...  38.6 us
    ppermute x6, starting transfers between devices, local_step(): turn = lambda a, d: lax.ppermute(a, 'z', [(i, i ^ d) for i in range(depth)])  11.1 us
  transfers between devices with their start and end apart: 6, of which 0 were waited for; matrix products, arithmetic and copies ran while one was open for 0% of the time, Pallas kernels for 70%

profile of v7, /device:TPU:0, one launch (start us, length us, event | category | flops | bytes accessed | tf_op | source)
XLA Modules:
  0.0 448.7 jit_solution(2064235778728239215)
XLA Ops:
  0.6 113.6 %spread.1 = (bf16[4,512,1024]{2,1,0:T(8,128)(2,1)}, bf16[4,256,1024]{2,1,0:T(8,128)(2,1)}, bf16[256,1024]{1,0:T(8,128)(2,1)}, bf16[4,80,512]{2,1,0:T(8,128)(2,1)...) custom-call(bf16[512,1024]{1,0:T(8,128)(2,1)} %x_ref.1, ...), custom_call_target="tpu_custom_call" | custom-call | tf_op jit(solution)/shard_map/spread/pallas_call | solution.py:250
  114.2 0.1 collective-permute-start
  114.3 3.0 collective-permute-start.1
  117.3 1.4 collective-permute-start.2
  118.7 0.8 dynamic-slice_convert_fusion
  119.4 0.7 reshape.29.count_ref
  120.1 38.6 %forward.1 = (f32[512,1024]{1,0:T(8,128)}, f32[512,1024]{1,0:T(8,128)}, f32[512,1024]{1,0:T(8,128)}, f32[512,1024]{1,0:T(8,128)}, bf16[16,512,1024]{2,1,0:T(8,12...) custom-call(s32[64]{0:T(128)} %reshape.29.count_ref, ...), custom_call_target="tpu_custom_call" | custom-call | flops 24999999488 | bytes 80000000 | tf_op jit(solution)/shard_map/forward/pallas_call | solution.py:885
  158.7 0.0 collective-permute-done.refs_1_
  158.8 0.0 copy-start.1
  158.8 0.0 collective-permute-done.1.refs_2_
  158.8 0.0 collective-permute-done.2.refs_3_
  158.8 3.7 collective-permute-start.3
  162.5 2.9 collective-permute-start.4
  165.5 0.0 collective-permute-start.5
  165.5 0.0 copy-done.1
  165.5 61.1 %backward.1 = (f32[2048,1024]{1,0:T(8,128)}, f32[8,3072,512]{2,1,0:T(8,128)}) custom-call(s32[64]{0:T(128)} %reshape.29.count_ref, s32[1]{0:T(128)} %bitcast.2.z_ref, bf16[4,80,512]{2,1,0:T(8,128)(2,1)} %get-tuple-element.34.plan_ref, bf16[1024,1024]{1,0:T(8,128)(2,1)} %bitcast.10, bf16[256,1024]{1,0:T(8,128)(2,1)} %get-tuple-element.49.refs_0_, ...), custom_call_target="tpu_custom_call" | custom-call | flops 49999998976 | bytes 150000000 | tf_op jit(solution)/shard_map/backward/pallas_call | solution.py:931
  226.6 0.0 copy-start
  226.6 215.3 %collect.1 = (bf16[512,1024]{1,0:T(8,128)(2,1)S(1)}, f32[1024,512]{1,0:T(8,128)S(1)}, f32[1024,512]{1,0:T(8,128)S(1)}, f32[512,1024]{1,0:T(8,128)S(1)}, f32[4,3072,512]{2,1,0:T(8,128)}) custom-call(f32[4,512,1024]{2,1,0:T(8,128)} %bitcast.6, f32[8,3072,512]{2,1,0:T(8,128)} %get-tuple-element.58.g_ref), custom_call_target="tpu_custom_call" | custom-call | tf_op jit(solution)/shard_map/collect/pallas_call | solution.py:515
  441.9 0.0 collective-permute-done.3.refs_1_
  441.9 0.0 collective-permute-done.4.refs_2_
  441.9 0.0 collective-permute-done.5.refs_3_
  441.9 0.0 copy-done
  441.9 6.6 %finish.1 = (bf16[512,1024]{1,0:T(8,128)(2,1)}, bf16[512,1024]{1,0:T(8,128)(2,1)}, f32[1,1024,512]{2,1,0:T(8,128)}, f32[1,1024,512]{2,1,0:T(8,128)}, f32[1,512,1024]{2,1,0:T(8,128)}) custom-call(f32[512,1024]{1,0:T(8,128)S(1)} %copy-done, f32[512,1024]{1,0:T(8,128)} %collective-permute-done.3.refs_1_, f32[512,1024]{1,0:T(8,128)} %collective-permute-done.4.refs_2_, ...), custom_call_target="tpu_custom_call" | custom-call | tf_op jit(solution)/shard_map/finish/pallas_call | solution.py:997
Async XLA Ops:
  114.2 44.5 %collective-permute-start = (bf16[256,1024]{1,0:T(8,128)(2,1)}, bf16[256,1024]{1,0:T(8,128)(2,1)S(1)}, u32[]{:S(2)}, u32[]{:S(2)}) collective-permute-start(bf16[256,1024]{1,0:T(8,128)(2,1)} %get-tuple-element.49.refs_0_), channel_id=1, source_target_pairs={{0,8},{8,0},{16,24},{24,16},{1,9},{9,1},{17,25},{25,17},{2,10},{10... | collective-permute-start | bytes 1572872 | tf_op jit(solution)/shard_map/ppermute | solution.py:1026
  114.3 44.5 %collective-permute-start.1 = (bf16[256,1024]{1,0:T(8,128)(2,1)}, bf16[256,1024]{1,0:T(8,128)(2,1)}, u32[]{:S(2)}, u32[]{:S(2)}) collective-permute-start(bf16[256,1024]{1,0:T(8,128)(2,1)} %get-tuple-element.49.refs_0_), channel_id=1, source_target_pairs={{0,16},{8,24},{16,0},{24,8},{1,17},{9,25},{17,1},{25,9},{2,18},{10... | collective-permute-start | bytes 1572872 | tf_op jit(solution)/shard_map/ppermute | solution.py:1026
  117.3 41.5 %collective-permute-start.2 = (bf16[256,1024]{1,0:T(8,128)(2,1)}, bf16[256,1024]{1,0:T(8,128)(2,1)}, u32[]{:S(2)}, u32[]{:S(2)}) collective-permute-start(bf16[256,1024]{1,0:T(8,128)(2,1)} %get-tuple-element.49.refs_0_), channel_id=1, source_target_pairs={{0,24},{8,16},{16,8},{24,0},{1,25},{9,17},{17,9},{25,1},{2,26},{10... | collective-permute-start | bytes 1572872 | tf_op jit(solution)/shard_map/ppermute | solution.py:1026
  158.8 6.7 %copy-start.1 = (bf16[256,1024]{1,0:T(8,128)(2,1)}, bf16[256,1024]{1,0:T(8,128)(2,1)S(1)}, u32[]{:S(2)}) copy-start(bf16[256,1024]{1,0:T(8,128)(2,1)S(1)} %collective-permute-done.refs_1_) | copy-start | bytes 1572868
  158.8 283.1 %collective-permute-start.3 = (f32[512,1024]{1,0:T(8,128)}, f32[512,1024]{1,0:T(8,128)}, u32[]{:S(2)}, u32[]{:S(2)}) collective-permute-start(f32[512,1024]{1,0:T(8,128)} %get-tuple-element.45), channel_id=1, source_target_pairs={{0,8},{8,0},{16,24},{24,16},{1,9},{9,1},{17,25},{25,17},{2,10},{10... | collective-permute-start | bytes 6291464 | tf_op jit(solution)/shard_map/ppermute | solution.py:1026
  162.5 279.4 %collective-permute-start.4 = (f32[512,1024]{1,0:T(8,128)}, f32[512,1024]{1,0:T(8,128)}, u32[]{:S(2)}, u32[]{:S(2)}) collective-permute-start(f32[512,1024]{1,0:T(8,128)} %get-tuple-element.46), channel_id=1, source_target_pairs={{0,16},{8,24},{16,0},{24,8},{1,17},{9,25},{17,1},{25,9},{2,18},{10... | collective-permute-start | bytes 6291464 | tf_op jit(solution)/shard_map/ppermute | solution.py:1026
  165.5 276.5 %collective-permute-start.5 = (f32[512,1024]{1,0:T(8,128)}, f32[512,1024]{1,0:T(8,128)}, u32[]{:S(2)}, u32[]{:S(2)}) collective-permute-start(f32[512,1024]{1,0:T(8,128)} %get-tuple-element.47), channel_id=1, source_target_pairs={{0,24},{8,16},{16,8},{24,0},{1,25},{9,17},{17,9},{25,1},{2,26},{10... | collective-permute-start | bytes 6291464 | tf_op jit(solution)/shard_map/ppermute | solution.py:1026
  226.6 215.4 %copy-start = (f32[512,1024]{1,0:T(8,128)S(1)}, f32[512,1024]{1,0:T(8,128)}, u32[]{:S(2)}) copy-start(f32[512,1024]{1,0:T(8,128)} %get-tuple-element.44.refs_0_) | copy-start | bytes 6291460
